TPU v7x, 8 devices: a whole 2x2x1 slice. The times are simulated.
8 devices in a mesh: rep: 2 (over y, z), dp: 4 (over x, core).
Axes of the slice: x: 2, y: 2, z: 1, core: 2. Of those that a mesh axis runs over, the one named last changes fastest.
Arguments:
- g_w_gate: bfloat16 [8, 2, 1024, 3072], P(('rep', 'dp')), parts along dimension 0
- g_w_up: bfloat16 [8, 2, 1024, 3072], P(('rep', 'dp')), parts along dimension 0
- g_w_down: bfloat16 [8, 2, 3072, 1024], P(('rep', 'dp')), parts along dimension 0
- w_gate: bfloat16 [2, 1024, 3072], replicated
- w_up: bfloat16 [2, 1024, 3072], replicated
- w_down: bfloat16 [2, 3072, 1024], replicated
- m_w_gate: float32 [2, 1024, 3072], P(None, 'dp')
- m_w_up: float32 [2, 1024, 3072], P(None, 'dp')
- m_w_down: float32 [2, 3072, 1024], P(None, 'dp')
- v_w_gate: float32 [2, 1024, 3072], P(None, 'dp')
- v_w_up: float32 [2, 1024, 3072], P(None, 'dp')
- v_w_down: float32 [2, 3072, 1024], P(None, 'dp')
Outputs:
- output 1: bfloat16 [4, 1024, 3072], P('rep'), parts along dimension 0
- output 2: bfloat16 [4, 1024, 3072], P('rep'), parts along dimension 0
- output 3: bfloat16 [4, 3072, 1024], P('rep'), parts along dimension 0
- output 4: float32 [4, 1024, 3072], P('rep', 'dp'), parts along dimension 0
- output 5: float32 [4, 1024, 3072], P('rep', 'dp'), parts along dimension 0
- output 6: float32 [4, 3072, 1024], P('rep', 'dp'), parts along dimension 0
- output 7: float32 [4, 1024, 3072], P('rep', 'dp'), parts along dimension 0
- output 8: float32 [4, 1024, 3072], P('rep', 'dp'), parts along dimension 0
- output 9: float32 [4, 3072, 1024], P('rep', 'dp'), parts along dimension 0
There are 2 independent parts. A program takes and returns all parts, laid end to end along the dimension named above; an argument that names none is the same for every part.
All inputs are finite; a program needn't handle non-finite values.
Results may differ from a plain program's by a relative error of at most 0.022.
Values are sent between devices in bfloat16 or wider.
A program may use at most 2 GiB of HBM per device.

v0:
```python
import jax
import jax.numpy as jnp
from jax import lax
from jax.sharding import PartitionSpec as P


def adamw(w, m, v, g):
    m = 0.9 * m + 0.1 * g
    v = 0.95 * v + 0.05 * g * g
    step = m * lax.rsqrt(v + 1e-8) + 0.1 * w
    return (w - 0.02 * step).astype(jnp.bfloat16), m, v


def solution(mesh):
    def step(*arrays):
        terms, weights, m, v = (arrays[i : i + 3] for i in (0, 3, 6, 9))
        gradients = [lax.psum_scatter(t[0], "dp", scatter_dimension=1, tiled=True).astype(jnp.float32) for t in terms]
        me = lax.axis_index("dp")
        own = [lax.dynamic_slice_in_dim(w, me * one.shape[1], one.shape[1], 1).astype(jnp.float32) for w, one in zip(weights, m, strict=True)]
        new = [adamw(w, m, v, g) for w, m, v, g in zip(own, m, v, gradients, strict=True)]
        whole = [lax.all_gather(one[0], "dp", axis=1, tiled=True) for one in new]
        return (*whole, *(one[1] for one in new), *(one[2] for one in new))

    all_of, cut = P(None, None, None), P(None, "dp", None)
    return jax.shard_map(
        step,
        mesh=mesh,
        in_specs=(P(("rep", "dp"), None, None, None),) * 3 + (all_of,) * 3 + (cut,) * 6,
        out_specs=(P("rep", None, None),) * 3 + (P("rep", "dp", None),) * 6,
        check_vma=False,
    )
```

profile of v0, /device:TPU:0, one launch (start us, length us, event | category | flops | bytes accessed | tf_op | source)
XLA Modules:
  0.0 577.5 jit_solution(16321195899225892048)
XLA Ops:
  7.2 0.0 reduce-scatter.8.cloned.1.call-start
  7.2 0.7 reduce-scatter.8.cloned.1.call-update
  7.9 0.0 reduce-scatter.6.cloned.1.call-start
  8.0 0.7 reduce-scatter.6.cloned.1.call-update
  8.7 0.0 reduce-scatter.4.cloned.1.call-start
  8.7 0.7 reduce-scatter.4.cloned.1.call-update
  9.4 0.0 all-gather.8.cloned.1.call-start
  9.4 98.0 %reduce-scatter.8.cloned.1.call-done = bf16[2,768,1024]{2,1,0:T(8,128)(2,1)} async-done(((bf16[2,3072,1024]{2,1,0:T(8,128)(2,1)}), bf16[2,768,1024]{2,1,0:T(8,128)(2,1)}) %reduce-scatter.8.cloned.1.call-update) | async-done | bytes 3145744 | tf_op jit(solution)/shard_map/reduce_scatter | solution.py:17
  107.4 15.6 %fusion.10 = (bf16[2,768,1024]{2,1,0:T(8,128)(2,1)}, f32[2,768,1024]{2,1,0:T(8,128)}, f32[2,768,1024]{2,1,0:T(8,128)}) fusion(bf16[2,3072,1024]{2,1,0:T(8,128)(2,1)} %param.17, s32[]{:T(128)S(6)} %select_n.8, bf16[2,768,1024]{2,1,0:T(8,128)(2,1)} %reduce-scatter.8.cloned.1.call-done, f32[2,768,1024]{2,1,0:T(8,128)} %param.23, f32[2,768,1024]{2,1,0:T(8,128)} %param.20), kind=kLoop, calls=%fused_computation.22 | loop fusion | flops 25165824 | bytes 34603012 | tf_op jit(solution)/shard_map/convert_element_type | solution.py:11
  123.1 0.0 all-gather.8.cloned.1.call-update
  123.1 0.0 all-gather.6.cloned.1.call-start
  123.1 80.9 %reduce-scatter.6.cloned.1.call-done = bf16[2,256,3072]{2,1,0:T(8,128)(2,1)} async-done(((bf16[2,1024,3072]{2,1,0:T(8,128)(2,1)}), bf16[2,256,3072]{2,1,0:T(8,128)(2,1)}) %reduce-scatter.6.cloned.1.call-update) | async-done | bytes 3145744 | tf_op jit(solution)/shard_map/reduce_scatter | solution.py:17
  204.1 15.6 %fusion.6 = (bf16[2,256,3072]{2,1,0:T(8,128)(2,1)}, f32[2,256,3072]{2,1,0:T(8,128)}, f32[2,256,3072]{2,1,0:T(8,128)}) fusion(bf16[2,1024,3072]{2,1,0:T(8,128)(2,1)} %param.16, s32[]{:T(128)S(6)} %select_n.7, bf16[2,256,3072]{2,1,0:T(8,128)(2,1)} %reduce-scatter.6.cloned.1.call-done, f32[2,256,3072]{2,1,0:T(8,128)} %param.22, f32[2,256,3072]{2,1,0:T(8,128)} %param.19), kind=kLoop, calls=%fused_computation.18 | loop fusion | flops 25165824 | bytes 34603012 | tf_op jit(solution)/shard_map/convert_element_type | solution.py:11
  219.7 0.0 all-gather.6.cloned.1.call-update
  219.7 0.0 all-gather.4.cloned.1.call-start
  219.8 81.0 %reduce-scatter.4.cloned.1.call-done = bf16[2,256,3072]{2,1,0:T(8,128)(2,1)} async-done(((bf16[2,1024,3072]{2,1,0:T(8,128)(2,1)}), bf16[2,256,3072]{2,1,0:T(8,128)(2,1)}) %reduce-scatter.4.cloned.1.call-update) | async-done | bytes 3145744 | tf_op jit(solution)/shard_map/reduce_scatter | solution.py:17
  300.7 14.9 %fusion.2 = (bf16[2,256,3072]{2,1,0:T(8,128)(2,1)}, f32[2,256,3072]{2,1,0:T(8,128)}, f32[2,256,3072]{2,1,0:T(8,128)}) fusion(bf16[2,1024,3072]{2,1,0:T(8,128)(2,1)} %param.15, s32[]{:T(128)S(6)} %select_n.7, bf16[2,256,3072]{2,1,0:T(8,128)(2,1)} %reduce-scatter.4.cloned.1.call-done, f32[2,256,3072]{2,1,0:T(8,128)} %param.21, f32[2,256,3072]{2,1,0:T(8,128)} %param.18), kind=kLoop, calls=%fused_computation.14 | loop fusion | flops 25165824 | bytes 34603012 | tf_op jit(solution)/shard_map/convert_element_type | solution.py:11
  315.7 0.0 all-gather.4.cloned.1.call-update
  315.7 66.4 %all-gather.8.cloned.1.call-done = bf16[2,3072,1024]{2,1,0:T(8,128)(2,1)} async-done(((bf16[2,768,1024]{2,1,0:T(8,128)(2,1)}), bf16[2,3072,1024]{2,1,0:T(8,128)(2,1)}) %all-gather.8.cloned.1.call-update) | async-done | bytes 12582928 | tf_op jit(solution)/shard_map/all_gather | solution.py:21
  382.1 81.3 %all-gather.6.cloned.1.call-done = bf16[2,1024,3072]{2,1,0:T(8,128)(2,1)} async-done(((bf16[2,256,3072]{2,1,0:T(8,128)(2,1)}), bf16[2,1024,3072]{2,1,0:T(8,128)(2,1)}) %all-gather.6.cloned.1.call-update) | async-done | bytes 12582928 | tf_op jit(solution)/shard_map/all_gather | solution.py:21
  463.4 81.3 %all-gather.4.cloned.1.call-done = bf16[2,1024,3072]{2,1,0:T(8,128)(2,1)} async-done(((bf16[2,256,3072]{2,1,0:T(8,128)(2,1)}), bf16[2,1024,3072]{2,1,0:T(8,128)(2,1)}) %all-gather.4.cloned.1.call-update) | async-done | bytes 12582928 | tf_op jit(solution)/shard_map/all_gather | solution.py:21
  544.6 0.0 copy-start
  544.6 0.0 slice-start
  544.6 0.0 slice-start.1
  544.6 12.4 %copy.24 = bf16[2,1024,3072]{2,1,0:T(8,128)(2,1)} copy(bf16[2,1024,3072]{2,1,0:T(8,128)(2,1)} %all-gather.4.cloned.1.call-done) | data formatting | bytes 25165824
  557.1 0.0 copy-done
  557.1 0.0 slice-start.2
  557.1 6.4 %copy.25 = bf16[2,1024,3072]{2,1,0:T(8,128)(2,1)} copy(bf16[2,1024,3072]{2,1,0:T(8,128)(2,1)S(1)} %copy-done) | data formatting | bytes 25165824
  563.4 0.0 slice-done
  563.4 1.1 slice-done.1
  564.5 1.3 slice-done.2
  565.8 4.8 copy.26
  (1 shorter events, 0.0 us)
Async XLA Ops:
  7.2 100.2 %reduce-scatter.8.cloned.1.call-start = ((), (), s32[]{:S(2)}) async-start(), calls=%async_computation.7 | async-start | bytes 15728640 | tf_op jit(solution)/shard_map/reduce_scatter | solution.py:17
  7.9 196.2 %reduce-scatter.6.cloned.1.call-start = ((), (), s32[]{:S(2)}) async-start(), calls=%async_computation.5 | async-start | bytes 15728640 | tf_op jit(solution)/shard_map/reduce_scatter | solution.py:17
  8.7 292.1 %reduce-scatter.4.cloned.1.call-start = ((), (), s32[]{:S(2)}) async-start(), calls=%async_computation.3 | async-start | bytes 15728640 | tf_op jit(solution)/shard_map/reduce_scatter | solution.py:17
  9.4 372.7 %all-gather.8.cloned.1.call-start = ((), (), s32[]{:S(2)}) async-start(), calls=%async_computation.8 | async-start | bytes 15728640 | tf_op jit(solution)/shard_map/all_gather | solution.py:21
  123.1 340.3 %all-gather.6.cloned.1.call-start = ((), (), s32[]{:S(2)}) async-start(), calls=%async_computation.6 | async-start | bytes 15728640 | tf_op jit(solution)/shard_map/all_gather | solution.py:21
  219.7 324.9 %all-gather.4.cloned.1.call-start = ((), (), s32[]{:S(2)}) async-start(), calls=%async_computation.4 | async-start | bytes 15728640 | tf_op jit(solution)/shard_map/all_gather | solution.py:21
  544.6 12.4 %copy-start = (bf16[2,1024,3072]{2,1,0:T(8,128)(2,1)S(1)}, bf16[2,1024,3072]{2,1,0:T(8,128)(2,1)}, u32[]{:S(2)}) copy-start(bf16[2,1024,3072]{2,1,0:T(8,128)(2,1)} %all-gather.6.cloned.1.call-done) | copy-start | bytes 37748740
  544.6 18.8 %slice-start = ((s8[12582912]{0:T(1024)(128)(4,1)}), s8[4194304]{0:T(1024)(128)(4,1)S(1)}, s32[]{:S(2)}) async-start(s8[12582912]{0:T(1024)(128)(4,1)} %bitcast.6), calls=%async_computation.9 | async-start | bytes 8388608
  544.6 19.9 %slice-start.1 = ((s8[12582912]{0:T(1024)(128)(4,1)}), s8[4194304]{0:T(1024)(128)(4,1)S(1)}, s32[]{:S(2)}) async-start(s8[12582912]{0:T(1024)(128)(4,1)} %bitcast.6), calls=%async_computation.10 | async-start | bytes 8388608
  557.1 8.8 %slice-start.2 = ((s8[12582912]{0:T(1024)(128)(4,1)}), s8[4194304]{0:T(1024)(128)(4,1)S(1)}, s32[]{:S(2)}) async-start(s8[12582912]{0:T(1024)(128)(4,1)} %bitcast.6), calls=%async_computation.11 | async-start | bytes 8388608
Sparse Core Ops, SparseCore 0:
  10.5 96.8 reduce-scatter.7
  110.0 94.0 reduce-scatter.5
  206.6 94.0 reduce-scatter.3
  302.7 79.3 all-gather.7
  384.0 79.2 all-gather.5
  465.3 79.2 all-gather.3
where the time goes:
time: 578 us; the launch traced here: 577 us
  waiting for transfers between devices  491 us (85%)
  other arithmetic  46.2 us (8%)
  local copies, waits for them, and re-layouts  26 us (4%)
  between operations  14.1 us (2%)
    reduce_scatter x3, waiting for transfers between devices, step(): lax.psum_scatter(t[0], 'dp', scatter_dimension=1, tiled=True)  260 us
    all_gather x3, waiting for transfers between devices, step(): whole = [lax.all_gather(one[0], 'dp', axis=1, tiled=True) for one in new]  229 us
    convert_element_type x3, other arithmetic, adamw(): return ((w - 0.02 * step).astype(jnp.bfloat16), m, v)  46.2 us
    unnamed x11, local copies, waits for them, and re-layouts  26 us
  transfers between devices with their start and end apart: 6, of which 6 were waited for; matrix products, arithmetic and copies ran while one was open for 8% of the time, Pallas kernels for 0%

commit v1 on v0

v1 whole, which is shorter than its diff:
```python
import functools

import jax
import jax.numpy as jnp
from jax import lax
from jax.experimental import pallas as pl
from jax.experimental.pallas import tpu as pltpu
from jax.sharding import PartitionSpec as P


ACROSS = [(0, 2), (2, 0), (1, 3), (3, 1)]
BESIDE = [(0, 1), (1, 0), (2, 3), (3, 2)]

CHUNKS = (
    (0, 0, 0, 64), (0, 0, 64, 192), (0, 1, 0, 256),
    (1, 0, 0, 256), (1, 1, 0, 256),
    (2, 0, 0, 768), (2, 1, 0, 576), (2, 1, 576, 192),
)


MESH = pl.DeviceIdType.MESH


def pair_body(chunk, nears, *refs):
    n = len(nears)
    terms, (both, *near_refs) = refs[:3], refs[3 : 4 + n]
    got, mine, total, got_send, got_recv, in_sem, out_sem, near_send, near_recv = refs[4 + n :]
    which, layer, first, rows = chunk
    me = lax.axis_index("dp")
    partner = {"dp": me ^ 1}
    barrier = pltpu.get_barrier_semaphore()
    pl.semaphore_signal(barrier, inc=1, device_id=partner, device_id_type=MESH)
    pl.semaphore_wait(barrier, 1)

    def block(which, layer, first, rows, owner):
        size = terms[which].shape[2] // 4
        return terms[which].at[0, layer, pl.ds(pl.multiple_of(owner * size + first, 16), rows)]

    tile = pair_tile(rows, terms[which].shape[3])
    count = rows // tile
    fars = [
        pltpu.make_async_remote_copy(
            block(which, layer, first + t * tile, tile, me ^ 3), got.at[pl.ds(t * tile, tile)],
            got_send.at[t], got_recv.at[t], device_id=partner, device_id_type=MESH)
        for t in range(count)
    ]
    owns = [
        pltpu.make_async_copy(block(which, layer, first + t * tile, tile, me ^ 2), mine.at[pl.ds(t * tile, tile)], in_sem.at[t])
        for t in range(count)
    ]
    beside = [
        pltpu.make_async_remote_copy(
            block(*CHUNKS[c], me ^ 1), near_refs[i], near_send.at[i], near_recv.at[i], device_id=partner, device_id_type=MESH)
        for i, c in enumerate(nears)
    ]
    outs = [pltpu.make_async_copy(total.at[pl.ds(t * tile, tile)], both.at[pl.ds(t * tile, tile)], out_sem.at[t]) for t in range(count)]
    for far, own in zip(fars, owns):
        far.start()
        own.start()
    for copy in beside:
        copy.start()
    for t in range(count):
        owns[t].wait()
        fars[t].wait_recv()
        here = pl.ds(t * tile, tile)
        total[here] = (got[here].astype(jnp.float32) + mine[here].astype(jnp.float32)).astype(jnp.bfloat16)
        outs[t].start()
    for t in range(count):
        fars[t].wait_send()
        outs[t].wait()
    for copy in beside:
        copy.wait()


def pair_tile(rows, cols):
    return min(rows, 64 * 3072 // cols)


def pair(terms, index, nears):
    chunk = CHUNKS[index]
    which, _, _, rows = chunk
    cols = terms[which].shape[3]
    count = rows // pair_tile(rows, cols)
    anywhere = pl.BlockSpec(memory_space=pl.ANY)
    shapes = [(rows, cols)] + [(CHUNKS[c][3], terms[CHUNKS[c][0]].shape[3]) for c in nears]
    return pl.pallas_call(
        functools.partial(pair_body, chunk, nears),
        in_specs=[anywhere] * 3,
        out_specs=[anywhere] * len(shapes),
        out_shape=[jax.ShapeDtypeStruct(shape, jnp.bfloat16) for shape in shapes],
        scratch_shapes=[pltpu.VMEM((rows, cols), jnp.bfloat16)] * 3
        + [pltpu.SemaphoreType.DMA((count,))] * 4
        + [pltpu.SemaphoreType.DMA((max(1, len(nears)),))] * 2,
        compiler_params=pltpu.CompilerParams(collective_id=index, has_side_effects=True),
        cost_estimate=pl.CostEstimate(flops=rows * cols, bytes_accessed=10 * rows * cols, transcendentals=0),
        name="pair",
    )(*terms)


def adamw_body(n_alias, me, own, near, far, w, m, v, *rest):
    send, out, m_out, v_out = rest[n_alias:]
    g = own[...].astype(jnp.float32) + near[...].astype(jnp.float32) + far[...].astype(jnp.float32)
    g = g.reshape(m.shape).astype(jnp.bfloat16).astype(jnp.float32)
    m_new = 0.9 * m[...] + 0.1 * g
    v_new = 0.95 * v[...] + 0.05 * g * g
    w_old = w[...].astype(jnp.float32)
    new = (w_old - 0.02 * (m_new * lax.rsqrt(v_new + 1e-8) + 0.1 * w_old)).astype(jnp.bfloat16)
    send[...] = new.reshape(send.shape)
    out[...] = new
    m_out[...] = m_new
    v_out[...] = v_new


def adamw(me, terms, near, far, w, m, v, layer, first, rows, before):
    block, cols = m.shape[1], m.shape[2]
    tile = min(rows, 64 * 3072 // cols)
    at, per = first // tile, block // tile
    mine = pl.BlockSpec((1, tile, cols), lambda i, me: (layer, at + i, 0))
    whole = pl.BlockSpec((1, tile, cols), lambda i, me: (layer, me[0] * per + at + i, 0))
    term = pl.BlockSpec((1, 1, tile, cols), lambda i, me: (0, layer, me[0] * per + at + i, 0))
    chunk = pl.BlockSpec((tile, cols), lambda i, me: (i, 0))
    anywhere = pl.BlockSpec(memory_space=pl.ANY)
    n_alias = len(before)
    size = rows * cols
    return pl.pallas_call(
        functools.partial(adamw_body, n_alias),
        grid_spec=pltpu.PrefetchScalarGridSpec(
            num_scalar_prefetch=1,
            grid=(rows // tile,),
            in_specs=[term, chunk, chunk, whole, mine, mine] + [anywhere] * n_alias,
            out_specs=[chunk, whole, mine, mine],
        ),
        out_shape=[
            jax.ShapeDtypeStruct((rows, cols), jnp.bfloat16),
            jax.ShapeDtypeStruct(w.shape, jnp.bfloat16),
            jax.ShapeDtypeStruct(m.shape, jnp.float32),
            jax.ShapeDtypeStruct(v.shape, jnp.float32),
        ],
        input_output_aliases={7 + i: 1 + i for i in range(n_alias)},
        cost_estimate=pl.CostEstimate(flops=14 * size, bytes_accessed=28 * size, transcendentals=size),
        name="adamw",
    )(me, terms, near, far, w, m, v, *before)


def place_body(layer, first, rows, block, me, beside, across, corner, before, out, held, in_sem, out_sem):
    blocks = (me[0] ^ 1, me[0] ^ 2, me[0] ^ 3)
    ins = [pltpu.make_async_copy(src, held.at[i], in_sem.at[i]) for i, src in enumerate((beside, across, corner))]
    outs = [
        pltpu.make_async_copy(held.at[i], out.at[layer, pl.ds(pl.multiple_of(b * block + first, 16), rows)], out_sem.at[i])
        for i, b in enumerate(blocks)
    ]
    for copy in ins:
        copy.start()
    for came, goes in zip(ins, outs):
        came.wait()
        goes.start()
    for copy in outs:
        copy.wait()


def place(me, pieces, out, layer, first, rows, block):
    cols = out.shape[2]
    anywhere = pl.BlockSpec(memory_space=pl.ANY)
    return pl.pallas_call(
        functools.partial(place_body, layer, first, rows, block),
        in_specs=[pl.BlockSpec(memory_space=pltpu.SMEM)] + [anywhere] * 4,
        out_specs=anywhere,
        out_shape=jax.ShapeDtypeStruct(out.shape, out.dtype),
        input_output_aliases={4: 0},
        scratch_shapes=[
            pltpu.VMEM((3, rows, cols), jnp.bfloat16),
            pltpu.SemaphoreType.DMA((3,)),
            pltpu.SemaphoreType.DMA((3,)),
        ],
        cost_estimate=pl.CostEstimate(flops=3 * rows * cols, bytes_accessed=12 * rows * cols, transcendentals=0),
        name="place",
    )(me, *pieces, out)


def solution(mesh):
    def inner(*arrays):
        terms, weights, m, v = (arrays[i : i + 3] for i in (0, 3, 6, 9))
        me = lax.axis_index("dp").astype(jnp.int32).reshape(1)

        def send(x, to):
            return lax.ppermute(x, "dp", to)

        arrived, near = [], []
        for c in range(len(CHUNKS)):
            both, *more = pair(terms, c, () if c == 0 else (0, 1) if c == 1 else (c,))
            near += more
            arrived.append(send(both, ACROSS))

        state = [() for _ in weights]
        across, beside, corner = [], [], []
        for c, (which, layer, first, rows) in enumerate(CHUNKS):
            one, *state[which] = adamw(
                me, terms[which], near[c], arrived[c], weights[which], m[which], v[which], layer, first, rows, tuple(state[which]))
            across.append(send(one, ACROSS))
            beside.append(send(one, BESIDE))
        for c, (which, layer, first, rows) in enumerate(CHUNKS):
            corner.append(send(across[c], BESIDE))
        for c, (which, layer, first, rows) in enumerate(CHUNKS):
            state[which][0] = place(me, (beside[c], across[c], corner[c]), state[which][0], layer, first, rows, m[which].shape[1])
        return tuple(state[which][i] for i in range(3) for which in range(3))

    all_of, cut_rows = P(None, None, None), P(None, "dp", None)
    return jax.shard_map(
        inner,
        mesh=mesh,
        in_specs=(P(("rep", "dp"), None, None, None),) * 3 + (all_of,) * 3 + (cut_rows,) * 6,
        out_specs=(P("rep", None, None),) * 3 + (P("rep", "dp", None),) * 6,
        check_vma=False,
    )
```

time: 578 us -> 445 us (0.77)
  waiting for transfers between devices: 491 us -> 288 us
  Pallas kernels: 0 us -> 128 us
  other arithmetic: 46.2 us -> 0 us
  starting transfers between devices: 0.24 us -> 23.3 us
  local copies, waits for them, and re-layouts: 26 us -> 4.65 us
  between operations: 14.1 us -> 0.96 us
    ppermute x0 -> x32, waiting for transfers between devices: none -> 288 us  [send(): return lax.ppermute(x, 'dp', to)]
    reduce_scatter x3 -> x0, waiting for transfers between devices: 260 us -> none  [step(): lax.psum_scatter(t[0], 'dp', scatter_dimension=1, tiled=True)]
    all_gather x3 -> x0, waiting for transfers between devices: 229 us -> none  [step(): whole = [lax.all_gather(one[0], 'dp', axis=1, tiled=True) for one in new]]
    pallas_call x0 -> x24, Pallas kernels: none -> 128 us  [the longest x8 60.8 us: adamw(): pl.pallas_call(functools.partial(adamw_body, n_alias), grid_spec=pltpu.Pr...]
    convert_element_type x3 -> x0, other arithmetic: 46.2 us -> none  [adamw(): return ((w - 0.02 * step).astype(jnp.bfloat16), m, v)]
    ppermute x0 -> x32, starting transfers between devices: none -> 23.3 us  [send(): return lax.ppermute(x, 'dp', to)]
    unnamed x11 -> x34, local copies, waits for them, and re-layouts: 26 us -> 4.65 us
  transfers between devices with their start and end apart: 6 -> 32, of which waited for: 6 -> 12; matrix products, arithmetic and copies ran while one was open for 8% -> 0% of each run, Pallas kernels for 0% -> 28%
where the time goes in v1:
time: 445 us; the launch traced here: 444 us
  waiting for transfers between devices  288 us (65%)
  Pallas kernels  128 us (29%)
  starting transfers between devices  23.3 us (5%)
  local copies, waits for them, and re-layouts  4.65 us (1%)
    ppermute x32, waiting for transfers between devices, send(): return lax.ppermute(x, 'dp', to)  288 us
    pallas_call x8, Pallas kernels, adamw(): pl.pallas_call(functools.partial(adamw_body, n_alias), grid_spec=pltpu.Pr...  60.8 us
    pallas_call x8, Pallas kernels, pair(): pl.pallas_call(functools.partial(pair_body, chunk, nears), in_specs=[anyw...  41.8 us
    pallas_call x8, Pallas kernels, place(): pl.pallas_call(functools.partial(place_body, layer, first, rows, block),...  24.9 us
    ppermute x32, starting transfers between devices, send(): return lax.ppermute(x, 'dp', to)  23.3 us
  transfers between devices with their start and end apart: 32, of which 12 were waited for; matrix products, arithmetic and copies ran while one was open for 0% of the time, Pallas kernels for 28%

profile of v1, /device:TPU:0, one launch (start us, length us, event | category | flops | bytes accessed | tf_op | source)
XLA Modules:
  0.0 444.2 jit_solution(1459468279066563190)
XLA Ops:
  0.6 3.2 pair.10
  3.8 3.0 collective-permute-start.2
  6.8 5.6 %pair.9 = (bf16[192,3072]{1,0:T(8,128)(2,1)}, bf16[64,3072]{1,0:T(8,128)(2,1)}, bf16[192,3072]{1,0:T(8,128)(2,1)}) custom-call(bf16[1,2,1024,3072]{3,2,1,0:T(8,128)(2,1)} %refs_0_.15, bf16[1,2,1024,3072]{3,2,1,0:T(8,128)(2,1)} %refs_1_.15, bf16[1,2,3072,1024]{3,2,1,0:T(8,128)(2,1)} %own.15), custom_call_target="tpu_custom_call" | custom-call | flops 589824 | bytes 5898240 | tf_op jit(solution)/shard_map/pair/pallas_call | solution.py:86
  12.4 0.0 collective-permute-start.1
  12.4 2.8 pair.13
  15.3 2.0 collective-permute-start.20
  17.3 0.7 copy-done.13
  18.1 3.8 adamw.8
  21.9 6.7 %pair.15 = (bf16[768,1024]{1,0:T(8,128)(2,1)}, bf16[768,1024]{1,0:T(8,128)(2,1)}) custom-call(bf16[1,2,1024,3072]{3,2,1,0:T(8,128)(2,1)} %refs_0_.15, bf16[1,2,1024,3072]{3,2,1,0:T(8,128)(2,1)} %refs_1_.15, bf16[1,2,3072,1024]{3,2,1,0:T(8,128)(2,1)} %own.15), custom_call_target="tpu_custom_call" | custom-call | flops 786432 | bytes 7864320 | tf_op jit(solution)/shard_map/pair/pallas_call | solution.py:86
  28.6 1.7 collective-permute-start.22
  30.3 0.3 collective-permute-start.10
  30.7 5.0 %pair.14 = (bf16[576,1024]{1,0:T(8,128)(2,1)}, bf16[576,1024]{1,0:T(8,128)(2,1)}) custom-call(bf16[1,2,1024,3072]{3,2,1,0:T(8,128)(2,1)} %refs_0_.15, bf16[1,2,1024,3072]{3,2,1,0:T(8,128)(2,1)} %refs_1_.15, bf16[1,2,3072,1024]{3,2,1,0:T(8,128)(2,1)} %own.15), custom_call_target="tpu_custom_call" | custom-call | flops 589824 | bytes 5898240 | tf_op jit(solution)/shard_map/pair/pallas_call | solution.py:86
  35.7 15.0 %collective-permute-done.20.far = bf16[192,1024]{1,0:T(8,128)(2,1)S(1)} collective-permute-done((bf16[192,1024]{1,0:T(8,128)(2,1)}, bf16[192,1024]{1,0:T(8,128)(2,1)S(1)}, u32[]{:S(2)}, u32[]{:S(2)}) %collective-permute-start.20) | collective-permute-done | bytes 393248 | tf_op jit(solution)/shard_map/ppermute | solution.py:186
  50.7 2.0 collective-permute-start.21
  52.7 6.2 %pair.8 = (bf16[256,3072]{1,0:T(8,128)(2,1)}, bf16[256,3072]{1,0:T(8,128)(2,1)}) custom-call(bf16[1,2,1024,3072]{3,2,1,0:T(8,128)(2,1)} %refs_0_.15, bf16[1,2,1024,3072]{3,2,1,0:T(8,128)(2,1)} %refs_1_.15, bf16[1,2,3072,1024]{3,2,1,0:T(8,128)(2,1)} %own.15), custom_call_target="tpu_custom_call" | custom-call | flops 786432 | bytes 7864320 | tf_op jit(solution)/shard_map/pair/pallas_call | solution.py:86
  58.9 0.0 collective-permute-start
  59.0 6.2 %pair.11 = (bf16[256,3072]{1,0:T(8,128)(2,1)}, bf16[256,3072]{1,0:T(8,128)(2,1)}) custom-call(bf16[1,2,1024,3072]{3,2,1,0:T(8,128)(2,1)} %refs_0_.15, bf16[1,2,1024,3072]{3,2,1,0:T(8,128)(2,1)} %refs_1_.15, bf16[1,2,3072,1024]{3,2,1,0:T(8,128)(2,1)} %own.15), custom_call_target="tpu_custom_call" | custom-call | flops 786432 | bytes 7864320 | tf_op jit(solution)/shard_map/pair/pallas_call | solution.py:86
  65.1 27.8 %collective-permute-done.10.across = bf16[64,3072]{1,0:T(8,128)(2,1)} collective-permute-done((bf16[64,3072]{1,0:T(8,128)(2,1)}, bf16[64,3072]{1,0:T(8,128)(2,1)}, u32[]{:S(2)}, u32[]{:S(2)}) %collective-permute-start.10) | collective-permute-done | bytes 393248 | tf_op jit(solution)/shard_map/ppermute | solution.py:186
  92.9 2.0 collective-permute-start.12
  95.0 6.2 %pair.12 = (bf16[256,3072]{1,0:T(8,128)(2,1)}, bf16[256,3072]{1,0:T(8,128)(2,1)}) custom-call(bf16[1,2,1024,3072]{3,2,1,0:T(8,128)(2,1)} %refs_0_.15, bf16[1,2,1024,3072]{3,2,1,0:T(8,128)(2,1)} %refs_1_.15, bf16[1,2,3072,1024]{3,2,1,0:T(8,128)(2,1)} %own.15), custom_call_target="tpu_custom_call" | custom-call | flops 786432 | bytes 7864320 | tf_op jit(solution)/shard_map/pair/pallas_call | solution.py:86
  101.1 1.0 copy-done.11
  102.2 16.1 %collective-permute-done.21.far = bf16[576,1024]{1,0:T(8,128)(2,1)} collective-permute-done((bf16[576,1024]{1,0:T(8,128)(2,1)}, bf16[576,1024]{1,0:T(8,128)(2,1)}, u32[]{:S(2)}, u32[]{:S(2)}) %collective-permute-start.21) | collective-permute-done | bytes 1179680 | tf_op jit(solution)/shard_map/ppermute | solution.py:186
  118.2 8.2 %adamw.9 = (bf16[192,3072]{1,0:T(8,128)(2,1)}, bf16[2,1024,3072]{2,1,0:T(8,128)(2,1)}, f32[2,256,3072]{2,1,0:T(8,128)}, f32[2,256,3072]{2,1,0:T(8,128)}) custom-call(s32[1]{0:T(128)} %bitcast.me, bf16[1,2,1024,3072]{3,2,1,0:T(8,128)(2,1)} %refs_0_.15, ...), custom_call_target="tpu_custom_call", output_to_operand_aliasing={{1}: (7, {}), {2}: (8, {}), {3}: (9, {})} | custom-call | flops 8257536 | bytes 16515072 | tf_op jit(solution)/shard_map/adamw/pallas_call | solution.py:125
  126.5 0.5 collective-permute-start.6
  127.0 0.6 copy-done.5
  127.6 9.2 %adamw.13 = (bf16[768,1024]{1,0:T(8,128)(2,1)}, bf16[2,3072,1024]{2,1,0:T(8,128)(2,1)}, f32[2,768,1024]{2,1,0:T(8,128)}, f32[2,768,1024]{2,1,0:T(8,128)}) custom-call(s32[1]{0:T(128)} %bitcast.me, bf16[1,2,3072,1024]{3,2,1,0:T(8,128)(2,1)} %own.15, bf16[768,1024]{1,0:T(8,128)(2,1)} %get-tuple-element.85.near, bf16[768,1024]{1,0:T(8,128)(2,1)} %copy-done.5, ...), custom_call_target="tpu_custom_call" | custom-call | flops 11010048 | bytes 22020096 | tf_op jit(solution)/shard_map/adamw/pallas_call | solution.py:125
  136.8 8.3 %adamw.14 = (bf16[576,1024]{1,0:T(8,128)(2,1)}, bf16[2,3072,1024]{2,1,0:T(8,128)(2,1)}, f32[2,768,1024]{2,1,0:T(8,128)}, f32[2,768,1024]{2,1,0:T(8,128)}) custom-call(s32[1]{0:T(128)} %bitcast.me, bf16[1,2,3072,1024]{3,2,1,0:T(8,128)(2,1)} %own.15, ...), custom_call_target="tpu_custom_call", output_to_operand_aliasing={{1}: (7, {}), {2}: (8, {}), {3}: (9, {})} | custom-call | flops 8257536 | bytes 16515072 | tf_op jit(solution)/shard_map/adamw/pallas_call | solution.py:125
  145.1 2.0 collective-permute-start.7
  147.1 4.8 %collective-permute-done.far = bf16[256,3072]{1,0:T(8,128)(2,1)} collective-permute-done((bf16[256,3072]{1,0:T(8,128)(2,1)}, bf16[256,3072]{1,0:T(8,128)(2,1)}, u32[]{:S(2)}, u32[]{:S(2)}) %collective-permute-start) | collective-permute-done | bytes 1572896 | tf_op jit(solution)/shard_map/ppermute | solution.py:186
  151.9 3.8 adamw.15
  155.7 29.9 %collective-permute-done.12.far = bf16[256,3072]{1,0:T(8,128)(2,1)} collective-permute-done((bf16[256,3072]{1,0:T(8,128)(2,1)}, bf16[256,3072]{1,0:T(8,128)(2,1)}, u32[]{:S(2)}, u32[]{:S(2)}) %collective-permute-start.12) | collective-permute-done | bytes 1572896 | tf_op jit(solution)/shard_map/ppermute | solution.py:186
  185.6 2.0 collective-permute-start.24
  187.6 9.2 %adamw.10 = (bf16[256,3072]{1,0:T(8,128)(2,1)}, bf16[2,1024,3072]{2,1,0:T(8,128)(2,1)}, f32[2,256,3072]{2,1,0:T(8,128)}, f32[2,256,3072]{2,1,0:T(8,128)}) custom-call(s32[1]{0:T(128)} %bitcast.me, bf16[1,2,1024,3072]{3,2,1,0:T(8,128)(2,1)} %refs_0_.15, ...), custom_call_target="tpu_custom_call", output_to_operand_aliasing={{1}: (7, {}), {2}: (8, {}), {3}: (9, {})} | custom-call | flops 11010048 | bytes 22020096 | tf_op jit(solution)/shard_map/adamw/pallas_call | solution.py:125
  196.8 22.4 %collective-permute-done.13.far = bf16[256,3072]{1,0:T(8,128)(2,1)S(1)} collective-permute-done((bf16[256,3072]{1,0:T(8,128)(2,1)}, bf16[256,3072]{1,0:T(8,128)(2,1)S(1)}, u32[]{:S(2)}, u32[]{:S(2)}) %collective-permute-start.13) | collective-permute-done | bytes 1572896 | tf_op jit(solution)/shard_map/ppermute | solution.py:186
  219.2 1.2 copy-done.2
  220.4 31.8 %collective-permute-done.24.across = bf16[192,1024]{1,0:T(8,128)(2,1)S(1)} collective-permute-done((bf16[192,1024]{1,0:T(8,128)(2,1)}, bf16[192,1024]{1,0:T(8,128)(2,1)S(1)}, u32[]{:S(2)}, u32[]{:S(2)}) %collective-permute-start.24) | collective-permute-done | bytes 393248 | tf_op jit(solution)/shard_map/ppermute | solution.py:186
  252.3 1.7 collective-permute-start.4
  254.0 0.3 collective-permute-start.27
  254.3 9.2 %adamw.11 = (bf16[256,3072]{1,0:T(8,128)(2,1)}, bf16[2,1024,3072]{2,1,0:T(8,128)(2,1)}, f32[2,256,3072]{2,1,0:T(8,128)}, f32[2,256,3072]{2,1,0:T(8,128)}) custom-call(s32[1]{0:T(128)} %bitcast.me, bf16[1,2,1024,3072]{3,2,1,0:T(8,128)(2,1)} %refs_1_.15, bf16[256,3072]{1,0:T(8,128)(2,1)} %get-tuple-element.73.near, bf16[256,3072]{1,0:T(8,128)(2,1)} %copy-done.2, ...), custom_call_target="tpu_custom_call" | custom-call | flops 11010048 | bytes 22020096 | tf_op jit(solution)/shard_map/adamw/pallas_call | solution.py:125
  263.4 9.2 %adamw.12 = (bf16[256,3072]{1,0:T(8,128)(2,1)}, bf16[2,1024,3072]{2,1,0:T(8,128)(2,1)}, f32[2,256,3072]{2,1,0:T(8,128)}, f32[2,256,3072]{2,1,0:T(8,128)}) custom-call(s32[1]{0:T(128)} %bitcast.me, bf16[1,2,1024,3072]{3,2,1,0:T(8,128)(2,1)} %refs_1_.15, ...), custom_call_target="tpu_custom_call", output_to_operand_aliasing={{1}: (7, {}), {2}: (8, {}), {3}: (9, {})} | custom-call | flops 11010048 | bytes 22020096 | tf_op jit(solution)/shard_map/adamw/pallas_call | solution.py:125
  272.6 1.8 collective-permute-start.15
  274.4 40.7 %collective-permute-done.27.across = bf16[576,1024]{1,0:T(8,128)(2,1)} collective-permute-done((bf16[576,1024]{1,0:T(8,128)(2,1)}, bf16[576,1024]{1,0:T(8,128)(2,1)}, u32[]{:S(2)}, u32[]{:S(2)}) %collective-permute-start.27) | collective-permute-done | bytes 1179680 | tf_op jit(solution)/shard_map/ppermute | solution.py:186
  315.1 1.7 collective-permute-start.18
  316.9 0.3 collective-permute-start.30
  317.2 31.7 %collective-permute-done.15.across = bf16[256,3072]{1,0:T(8,128)(2,1)} collective-permute-done((bf16[256,3072]{1,0:T(8,128)(2,1)}, bf16[256,3072]{1,0:T(8,128)(2,1)}, u32[]{:S(2)}, u32[]{:S(2)}) %collective-permute-start.15) | collective-permute-done | bytes 1572896 | tf_op jit(solution)/shard_map/ppermute | solution.py:186
  348.8 0.5 collective-permute-start.28
  349.3 33.2 %collective-permute-done.18.across = bf16[256,3072]{1,0:T(8,128)(2,1)} collective-permute-done((bf16[256,3072]{1,0:T(8,128)(2,1)}, bf16[256,3072]{1,0:T(8,128)(2,1)}, u32[]{:S(2)}, u32[]{:S(2)}) %collective-permute-start.18) | collective-permute-done | bytes 1572896 | tf_op jit(solution)/shard_map/ppermute | solution.py:186
  382.5 32.1 %collective-permute-done.30.across = bf16[768,1024]{1,0:T(8,128)(2,1)S(1)} collective-permute-done((bf16[768,1024]{1,0:T(8,128)(2,1)}, bf16[768,1024]{1,0:T(8,128)(2,1)S(1)}, u32[]{:S(2)}, u32[]{:S(2)}) %collective-permute-start.30) | collective-permute-done | bytes 1572896 | tf_op jit(solution)/shard_map/ppermute | solution.py:186
  414.6 0.5 collective-permute-start.19
  415.1 0.0 collective-permute-start.14
  415.2 0.5 collective-permute-start.16
  415.6 0.1 collective-permute-start.23
  415.7 0.1 copy-done.4
  415.8 2.3 collective-permute-done.31.corner
  418.0 0.1 collective-permute-start.25
  418.2 1.0 copy-done.8
  419.1 2.0 place.8.before
  421.2 3.1 place.9.before
  424.4 3.6 place.13.before
  428.0 3.1 place.14.before
  431.1 3.6 place.10
  434.8 3.6 place.11.before
  438.5 3.6 place.12
  442.1 2.1 place.15
  (58 shorter events, 0.1 us)
Async XLA Ops:
  3.8 13.5 %collective-permute-start.2 = (bf16[64,3072]{1,0:T(8,128)(2,1)}, bf16[64,3072]{1,0:T(8,128)(2,1)S(1)}, u32[]{:S(2)}, u32[]{:S(2)}) collective-permute-start(bf16[64,3072]{1,0:T(8,128)(2,1)} %pair.10), channel_id=1, source_target_pairs={{0,2},{2,0},{1,3},{3,1},{4,6},{6,4},{5,7},{7,5}} | collective-permute-start | bytes 1179656 | tf_op jit(solution)/shard_map/ppermute | solution.py:186
  12.4 88.7 %collective-permute-start.1 = (bf16[192,3072]{1,0:T(8,128)(2,1)}, bf16[192,3072]{1,0:T(8,128)(2,1)S(1)}, u32[]{:S(2)}, u32[]{:S(2)}) collective-permute-start(bf16[192,3072]{1,0:T(8,128)(2,1)} %get-tuple-element.59), channel_id=1, source_target_pairs={{0,2},{2,0},{1,3},{3,1},{4,6},{6,4},{5,7},{7,5}} | collective-permute-start | bytes 3538952 | tf_op jit(solution)/shard_map/ppermute | solution.py:186
  15.3 35.4 %collective-permute-start.20 = (bf16[192,1024]{1,0:T(8,128)(2,1)}, bf16[192,1024]{1,0:T(8,128)(2,1)S(1)}, u32[]{:S(2)}, u32[]{:S(2)}) collective-permute-start(bf16[192,1024]{1,0:T(8,128)(2,1)} %get-tuple-element.82), channel_id=1, source_target_pairs={{0,2},{2,0},{1,3},{3,1},{4,6},{6,4},{5,7},{7,5}} | collective-permute-start | bytes 1179656 | tf_op jit(solution)/shard_map/ppermute | solution.py:186
  17.3 0.7 copy-start.13
  21.9 37.0 %collective-permute-start.9 = (bf16[64,3072]{1,0:T(8,128)(2,1)}, bf16[64,3072]{1,0:T(8,128)(2,1)S(1)}, u32[]{:S(2)}, u32[]{:S(2)}) collective-permute-start(bf16[64,3072]{1,0:T(8,128)(2,1)} %get-tuple-element.69), channel_id=1, source_target_pairs={{0,1},{1,0},{2,3},{3,2},{4,5},{5,4},{6,7},{7,6}} | collective-permute-start | bytes 1179656 | tf_op jit(solution)/shard_map/ppermute | solution.py:186
  28.6 97.9 %collective-permute-start.22 = (bf16[768,1024]{1,0:T(8,128)(2,1)}, bf16[768,1024]{1,0:T(8,128)(2,1)S(1)}, u32[]{:S(2)}, u32[]{:S(2)}) collective-permute-start(bf16[768,1024]{1,0:T(8,128)(2,1)} %get-tuple-element.86), channel_id=1, source_target_pairs={{0,2},{2,0},{1,3},{3,1},{4,6},{6,4},{5,7},{7,5}} | collective-permute-start | bytes 4718600 | tf_op jit(solution)/shard_map/ppermute | solution.py:186
  30.3 62.6 %collective-permute-start.10 = (bf16[64,3072]{1,0:T(8,128)(2,1)}, bf16[64,3072]{1,0:T(8,128)(2,1)}, u32[]{:S(2)}, u32[]{:S(2)}) collective-permute-start(bf16[64,3072]{1,0:T(8,128)(2,1)} %get-tuple-element.69), channel_id=1, source_target_pairs={{0,2},{2,0},{1,3},{3,1},{4,6},{6,4},{5,7},{7,5}} | collective-permute-start | bytes 1179656 | tf_op jit(solution)/shard_map/ppermute | solution.py:186
  50.7 8.2 %copy-start.12 = (bf16[192,1024]{1,0:T(8,128)(2,1)}, bf16[192,1024]{1,0:T(8,128)(2,1)S(1)}, u32[]{:S(2)}) copy-start(bf16[192,1024]{1,0:T(8,128)(2,1)S(1)} %collective-permute-done.20.far) | copy-start | bytes 1179652
  50.7 67.5 %collective-permute-start.21 = (bf16[576,1024]{1,0:T(8,128)(2,1)}, bf16[576,1024]{1,0:T(8,128)(2,1)}, u32[]{:S(2)}, u32[]{:S(2)}) collective-permute-start(bf16[576,1024]{1,0:T(8,128)(2,1)} %get-tuple-element.84), channel_id=1, source_target_pairs={{0,2},{2,0},{1,3},{3,1},{4,6},{6,4},{5,7},{7,5}} | collective-permute-start | bytes 3538952 | tf_op jit(solution)/shard_map/ppermute | solution.py:186
  58.9 6.2 %copy-start.14 = (bf16[64,3072]{1,0:T(8,128)(2,1)}, bf16[64,3072]{1,0:T(8,128)(2,1)S(1)}, u32[]{:S(2)}) copy-start(bf16[64,3072]{1,0:T(8,128)(2,1)S(1)} %collective-permute-done.9.beside) | copy-start | bytes 1179652
  58.9 93.0 %collective-permute-start = (bf16[256,3072]{1,0:T(8,128)(2,1)}, bf16[256,3072]{1,0:T(8,128)(2,1)}, u32[]{:S(2)}, u32[]{:S(2)}) collective-permute-start(bf16[256,3072]{1,0:T(8,128)(2,1)} %get-tuple-element.57), channel_id=1, source_target_pairs={{0,2},{2,0},{1,3},{3,1},{4,6},{6,4},{5,7},{7,5}} | collective-permute-start | bytes 4718600 | tf_op jit(solution)/shard_map/ppermute | solution.py:186
  92.9 92.7 %collective-permute-start.12 = (bf16[256,3072]{1,0:T(8,128)(2,1)}, bf16[256,3072]{1,0:T(8,128)(2,1)}, u32[]{:S(2)}, u32[]{:S(2)}) collective-permute-start(bf16[256,3072]{1,0:T(8,128)(2,1)} %get-tuple-element.72), channel_id=1, source_target_pairs={{0,2},{2,0},{1,3},{3,1},{4,6},{6,4},{5,7},{7,5}} | collective-permute-start | bytes 4718600 | tf_op jit(solution)/shard_map/ppermute | solution.py:186
  101.1 1.0 copy-start.11
  102.1 117.1 %collective-permute-start.13 = (bf16[256,3072]{1,0:T(8,128)(2,1)}, bf16[256,3072]{1,0:T(8,128)(2,1)S(1)}, u32[]{:S(2)}, u32[]{:S(2)}) collective-permute-start(bf16[256,3072]{1,0:T(8,128)(2,1)} %get-tuple-element.74), channel_id=1, source_target_pairs={{0,2},{2,0},{1,3},{3,1},{4,6},{6,4},{5,7},{7,5}} | collective-permute-start | bytes 4718600 | tf_op jit(solution)/shard_map/ppermute | solution.py:186
  118.2 26.8 %collective-permute-start.11 = (bf16[64,3072]{1,0:T(8,128)(2,1)}, bf16[64,3072]{1,0:T(8,128)(2,1)S(1)}, u32[]{:S(2)}, u32[]{:S(2)}) collective-permute-start(bf16[64,3072]{1,0:T(8,128)(2,1)} %collective-permute-done.10.across), channel_id=1, source_target_pairs={{0,1},{1,0},{2,3},{3,2},{4,5},{5,4},{6,7},{7,6}} | collective-permute-start | bytes 1179656 | tf_op jit(solution)/shard_map/ppermute | solution.py:186
  126.5 1.1 copy-start.5
  126.5 127.5 %collective-permute-start.6 = (bf16[192,3072]{1,0:T(8,128)(2,1)}, bf16[192,3072]{1,0:T(8,128)(2,1)}, u32[]{:S(2)}, u32[]{:S(2)}) collective-permute-start(bf16[192,3072]{1,0:T(8,128)(2,1)} %get-tuple-element.68), channel_id=1, source_target_pairs={{0,1},{1,0},{2,3},{3,2},{4,5},{5,4},{6,7},{7,6}} | collective-permute-start | bytes 3538952 | tf_op jit(solution)/shard_map/ppermute | solution.py:186
  145.0 10.7 %copy-start.15 = (bf16[64,3072]{1,0:T(8,128)(2,1)}, bf16[64,3072]{1,0:T(8,128)(2,1)S(1)}, u32[]{:S(2)}) copy-start(bf16[64,3072]{1,0:T(8,128)(2,1)S(1)} %collective-permute-done.11.corner) | copy-start | bytes 1179652
  145.1 127.6 %collective-permute-start.7 = (bf16[192,3072]{1,0:T(8,128)(2,1)}, bf16[192,3072]{1,0:T(8,128)(2,1)}, u32[]{:S(2)}, u32[]{:S(2)}) collective-permute-start(bf16[192,3072]{1,0:T(8,128)(2,1)} %get-tuple-element.68), channel_id=1, source_target_pairs={{0,2},{2,0},{1,3},{3,1},{4,6},{6,4},{5,7},{7,5}} | collective-permute-start | bytes 3538952 | tf_op jit(solution)/shard_map/ppermute | solution.py:186
  151.9 122.5 %collective-permute-start.26 = (bf16[576,1024]{1,0:T(8,128)(2,1)}, bf16[576,1024]{1,0:T(8,128)(2,1)}, u32[]{:S(2)}, u32[]{:S(2)}) collective-permute-start(bf16[576,1024]{1,0:T(8,128)(2,1)} %get-tuple-element.94), channel_id=1, source_target_pairs={{0,1},{1,0},{2,3},{3,2},{4,5},{5,4},{6,7},{7,6}} | collective-permute-start | bytes 3538952 | tf_op jit(solution)/shard_map/ppermute | solution.py:186
  185.6 66.6 %collective-permute-start.24 = (bf16[192,1024]{1,0:T(8,128)(2,1)}, bf16[192,1024]{1,0:T(8,128)(2,1)S(1)}, u32[]{:S(2)}, u32[]{:S(2)}) collective-permute-start(bf16[192,1024]{1,0:T(8,128)(2,1)} %get-tuple-element.93), channel_id=1, source_target_pairs={{0,2},{2,0},{1,3},{3,1},{4,6},{6,4},{5,7},{7,5}} | collective-permute-start | bytes 1179656 | tf_op jit(solution)/shard_map/ppermute | solution.py:186
  219.2 1.2 copy-start.2
  220.4 96.5 %collective-permute-start.3 = (bf16[256,3072]{1,0:T(8,128)(2,1)}, bf16[256,3072]{1,0:T(8,128)(2,1)S(1)}, u32[]{:S(2)}, u32[]{:S(2)}) collective-permute-start(bf16[256,3072]{1,0:T(8,128)(2,1)} %get-tuple-element.67), channel_id=1, source_target_pairs={{0,1},{1,0},{2,3},{3,2},{4,5},{5,4},{6,7},{7,6}} | collective-permute-start | bytes 4718600 | tf_op jit(solution)/shard_map/ppermute | solution.py:186
  252.3 165.8 %copy-start.16 = (bf16[192,1024]{1,0:T(8,128)(2,1)}, bf16[192,1024]{1,0:T(8,128)(2,1)S(1)}, u32[]{:S(2)}) copy-start(bf16[192,1024]{1,0:T(8,128)(2,1)S(1)} %collective-permute-done.24.across) | copy-start | bytes 1179652
  252.3 64.9 %collective-permute-start.4 = (bf16[256,3072]{1,0:T(8,128)(2,1)}, bf16[256,3072]{1,0:T(8,128)(2,1)S(1)}, u32[]{:S(2)}, u32[]{:S(2)}) collective-permute-start(bf16[256,3072]{1,0:T(8,128)(2,1)} %get-tuple-element.67), channel_id=1, source_target_pairs={{0,2},{2,0},{1,3},{3,1},{4,6},{6,4},{5,7},{7,5}} | collective-permute-start | bytes 4718600 | tf_op jit(solution)/shard_map/ppermute | solution.py:186
  254.0 61.1 %collective-permute-start.27 = (bf16[576,1024]{1,0:T(8,128)(2,1)}, bf16[576,1024]{1,0:T(8,128)(2,1)}, u32[]{:S(2)}, u32[]{:S(2)}) collective-permute-start(bf16[576,1024]{1,0:T(8,128)(2,1)} %get-tuple-element.94), channel_id=1, source_target_pairs={{0,2},{2,0},{1,3},{3,1},{4,6},{6,4},{5,7},{7,5}} | collective-permute-start | bytes 3538952 | tf_op jit(solution)/shard_map/ppermute | solution.py:186
  272.6 76.2 %collective-permute-start.15 = (bf16[256,3072]{1,0:T(8,128)(2,1)}, bf16[256,3072]{1,0:T(8,128)(2,1)}, u32[]{:S(2)}, u32[]{:S(2)}) collective-permute-start(bf16[256,3072]{1,0:T(8,128)(2,1)} %get-tuple-element.78), channel_id=1, source_target_pairs={{0,2},{2,0},{1,3},{3,1},{4,6},{6,4},{5,7},{7,5}} | collective-permute-start | bytes 4718600 | tf_op jit(solution)/shard_map/ppermute | solution.py:186
  274.4 74.4 %collective-permute-start.17 = (bf16[256,3072]{1,0:T(8,128)(2,1)}, bf16[256,3072]{1,0:T(8,128)(2,1)S(1)}, u32[]{:S(2)}, u32[]{:S(2)}) collective-permute-start(bf16[256,3072]{1,0:T(8,128)(2,1)} %get-tuple-element.79), channel_id=1, source_target_pairs={{0,1},{1,0},{2,3},{3,2},{4,5},{5,4},{6,7},{7,6}} | collective-permute-start | bytes 4718600 | tf_op jit(solution)/shard_map/ppermute | solution.py:186
  315.1 67.4 %collective-permute-start.18 = (bf16[256,3072]{1,0:T(8,128)(2,1)}, bf16[256,3072]{1,0:T(8,128)(2,1)}, u32[]{:S(2)}, u32[]{:S(2)}) collective-permute-start(bf16[256,3072]{1,0:T(8,128)(2,1)} %get-tuple-element.79), channel_id=1, source_target_pairs={{0,2},{2,0},{1,3},{3,1},{4,6},{6,4},{5,7},{7,5}} | collective-permute-start | bytes 4718600 | tf_op jit(solution)/shard_map/ppermute | solution.py:186
  316.9 104.3 %copy-start = (bf16[256,3072]{1,0:T(8,128)(2,1)}, bf16[256,3072]{1,0:T(8,128)(2,1)S(1)}, u32[]{:S(2)}) copy-start(bf16[256,3072]{1,0:T(8,128)(2,1)S(1)} %collective-permute-done.3.beside) | copy-start | bytes 4718596
  316.9 97.7 %collective-permute-start.30 = (bf16[768,1024]{1,0:T(8,128)(2,1)}, bf16[768,1024]{1,0:T(8,128)(2,1)S(1)}, u32[]{:S(2)}, u32[]{:S(2)}) collective-permute-start(bf16[768,1024]{1,0:T(8,128)(2,1)} %get-tuple-element.95), channel_id=1, source_target_pairs={{0,2},{2,0},{1,3},{3,1},{4,6},{6,4},{5,7},{7,5}} | collective-permute-start | bytes 4718600 | tf_op jit(solution)/shard_map/ppermute | solution.py:186
  317.2 104.1 %copy-start.1 = (bf16[256,3072]{1,0:T(8,128)(2,1)}, bf16[256,3072]{1,0:T(8,128)(2,1)S(1)}, u32[]{:S(2)}) copy-start(bf16[256,3072]{1,0:T(8,128)(2,1)S(1)} %collective-permute-done.4.across) | copy-start | bytes 4718596
  317.2 97.4 %collective-permute-start.29 = (bf16[768,1024]{1,0:T(8,128)(2,1)}, bf16[768,1024]{1,0:T(8,128)(2,1)S(1)}, u32[]{:S(2)}, u32[]{:S(2)}) collective-permute-start(bf16[768,1024]{1,0:T(8,128)(2,1)} %get-tuple-element.95), channel_id=1, source_target_pairs={{0,1},{1,0},{2,3},{3,2},{4,5},{5,4},{6,7},{7,6}} | collective-permute-start | bytes 4718600 | tf_op jit(solution)/shard_map/ppermute | solution.py:186
  348.8 66.3 %collective-permute-start.8 = (bf16[192,3072]{1,0:T(8,128)(2,1)}, bf16[192,3072]{1,0:T(8,128)(2,1)S(1)}, u32[]{:S(2)}, u32[]{:S(2)}) collective-permute-start(bf16[192,3072]{1,0:T(8,128)(2,1)} %collective-permute-done.7.across), channel_id=1, source_target_pairs={{0,1},{1,0},{2,3},{3,2},{4,5},{5,4},{6,7},{7,6}} | collective-permute-start | bytes 3538952 | tf_op jit(solution)/shard_map/ppermute | solution.py:186
  348.8 66.8 %copy-start.3 = (bf16[256,3072]{1,0:T(8,128)(2,1)}, bf16[256,3072]{1,0:T(8,128)(2,1)S(1)}, u32[]{:S(2)}) copy-start(bf16[256,3072]{1,0:T(8,128)(2,1)S(1)} %collective-permute-done.17.beside) | copy-start | bytes 4718596
  348.8 66.3 %collective-permute-start.28 = (bf16[576,1024]{1,0:T(8,128)(2,1)}, bf16[576,1024]{1,0:T(8,128)(2,1)S(1)}, u32[]{:S(2)}, u32[]{:S(2)}) collective-permute-start(bf16[576,1024]{1,0:T(8,128)(2,1)} %collective-permute-done.27.across), channel_id=1, source_target_pairs={{0,1},{1,0},{2,3},{3,2},{4,5},{5,4},{6,7},{7,6}} | collective-permute-start | bytes 3538952 | tf_op jit(solution)/shard_map/ppermute | solution.py:186
  382.5 33.1 %collective-permute-start.5 = (bf16[256,3072]{1,0:T(8,128)(2,1)S(1)}, bf16[256,3072]{1,0:T(8,128)(2,1)S(1)}, u32[]{:S(2)}, u32[]{:S(2)}) collective-permute-start(bf16[256,3072]{1,0:T(8,128)(2,1)S(1)} %collective-permute-done.4.across), channel_id=1, source_target_pairs={{0,1},{1,0},{2,3},{3,2},{4,5},{5,4},{6,7},{7,6}} | collective-permute-start | bytes 4718600 | tf_op jit(solution)/shard_map/ppermute | solution.py:186
  414.6 1.2 copy-start.4
  414.6 3.4 collective-permute-start.31
  414.6 3.4 copy-start.6
  414.6 20.2 %collective-permute-start.19 = (bf16[256,3072]{1,0:T(8,128)(2,1)}, bf16[256,3072]{1,0:T(8,128)(2,1)}, u32[]{:S(2)}, u32[]{:S(2)}) collective-permute-start(bf16[256,3072]{1,0:T(8,128)(2,1)} %collective-permute-done.18.across), channel_id=1, source_target_pairs={{0,1},{1,0},{2,3},{3,2},{4,5},{5,4},{6,7},{7,6}} | collective-permute-start | bytes 4718600 | tf_op jit(solution)/shard_map/ppermute | solution.py:186
  415.1 3.0 copy-start.10
  415.1 23.3 %collective-permute-start.14 = (bf16[256,3072]{1,0:T(8,128)(2,1)}, bf16[256,3072]{1,0:T(8,128)(2,1)}, u32[]{:S(2)}, u32[]{:S(2)}) collective-permute-start(bf16[256,3072]{1,0:T(8,128)(2,1)} %get-tuple-element.78), channel_id=1, source_target_pairs={{0,1},{1,0},{2,3},{3,2},{4,5},{5,4},{6,7},{7,6}} | collective-permute-start | bytes 4718600 | tf_op jit(solution)/shard_map/ppermute | solution.py:186
  415.2 3.0 copy-start.9
  415.2 23.3 %collective-permute-start.16 = (bf16[256,3072]{1,0:T(8,128)(2,1)}, bf16[256,3072]{1,0:T(8,128)(2,1)}, u32[]{:S(2)}, u32[]{:S(2)}) collective-permute-start(bf16[256,3072]{1,0:T(8,128)(2,1)} %collective-permute-done.15.across), channel_id=1, source_target_pairs={{0,1},{1,0},{2,3},{3,2},{4,5},{5,4},{6,7},{7,6}} | collective-permute-start | bytes 4718600 | tf_op jit(solution)/shard_map/ppermute | solution.py:186
  415.6 2.5 copy-start.7
  415.6 26.5 %collective-permute-start.23 = (bf16[192,1024]{1,0:T(8,128)(2,1)}, bf16[192,1024]{1,0:T(8,128)(2,1)}, u32[]{:S(2)}, u32[]{:S(2)}) collective-permute-start(bf16[192,1024]{1,0:T(8,128)(2,1)} %get-tuple-element.93), channel_id=1, source_target_pairs={{0,1},{1,0},{2,3},{3,2},{4,5},{5,4},{6,7},{7,6}} | collective-permute-start | bytes 1179656 | tf_op jit(solution)/shard_map/ppermute | solution.py:186
  418.0 1.1 copy-start.8
  418.0 24.1 %collective-permute-start.25 = (bf16[192,1024]{1,0:T(8,128)(2,1)S(1)}, bf16[192,1024]{1,0:T(8,128)(2,1)}, u32[]{:S(2)}, u32[]{:S(2)}) collective-permute-start(bf16[192,1024]{1,0:T(8,128)(2,1)S(1)} %collective-permute-done.24.across), channel_id=1, source_target_pairs={{0,1},{1,0},{2,3},{3,2},{4,5},{5,4},{6,7},{7,6}} | collective-permute-start | bytes 1179656 | tf_op jit(solution)/shard_map/ppermute | solution.py:186

commit v2 on v1

--- a/solution.py
+++ b/solution.py
@@ -1,4 +1,5 @@
 import functools
+import math
 
 import jax
 import jax.numpy as jnp
@@ -12,12 +13,10 @@
 BESIDE = [(0, 1), (1, 0), (2, 3), (3, 2)]
 
 CHUNKS = (
-    (0, 0, 0, 64), (0, 0, 64, 192), (0, 1, 0, 256),
+    (0, 0, 0, 32), (0, 0, 32, 96), (0, 0, 128, 128), (0, 1, 0, 256),
     (1, 0, 0, 256), (1, 1, 0, 256),
-    (2, 0, 0, 768), (2, 1, 0, 576), (2, 1, 576, 192),
+    (2, 0, 0, 768), (2, 1, 0, 384), (2, 1, 384, 192), (2, 1, 576, 96), (2, 1, 672, 96),
 )
-
-
 MESH = pl.DeviceIdType.MESH
 
 
@@ -30,7 +29,6 @@
     partner = {"dp": me ^ 1}
     barrier = pltpu.get_barrier_semaphore()
     pl.semaphore_signal(barrier, inc=1, device_id=partner, device_id_type=MESH)
-    pl.semaphore_wait(barrier, 1)
 
     def block(which, layer, first, rows, owner):
         size = terms[which].shape[2] // 4
@@ -38,22 +36,23 @@
 
     tile = pair_tile(rows, terms[which].shape[3])
     count = rows // tile
+    owns = [
+        pltpu.make_async_copy(block(which, layer, first + t * tile, tile, me ^ 2), mine.at[pl.ds(t * tile, tile)], in_sem.at[t])
+        for t in range(count)
+    ]
     fars = [
         pltpu.make_async_remote_copy(
             block(which, layer, first + t * tile, tile, me ^ 3), got.at[pl.ds(t * tile, tile)],
             got_send.at[t], got_recv.at[t], device_id=partner, device_id_type=MESH)
         for t in range(count)
     ]
-    owns = [
-        pltpu.make_async_copy(block(which, layer, first + t * tile, tile, me ^ 2), mine.at[pl.ds(t * tile, tile)], in_sem.at[t])
-        for t in range(count)
-    ]
     beside = [
         pltpu.make_async_remote_copy(
             block(*CHUNKS[c], me ^ 1), near_refs[i], near_send.at[i], near_recv.at[i], device_id=partner, device_id_type=MESH)
         for i, c in enumerate(nears)
     ]
     outs = [pltpu.make_async_copy(total.at[pl.ds(t * tile, tile)], both.at[pl.ds(t * tile, tile)], out_sem.at[t]) for t in range(count)]
+    pl.semaphore_wait(barrier, 1)
     for far, own in zip(fars, owns):
         far.start()
         own.start()
@@ -72,8 +71,45 @@
         copy.wait()
 
 
+def first_pair_body(chunk, terms, both, got, mine, send_sem, recv_sem, in_sem):
+    _, layer, first, rows = chunk
+    me = lax.axis_index("dp")
+    partner = {"dp": me ^ 1}
+    barrier = pltpu.get_barrier_semaphore()
+    pl.semaphore_signal(barrier, inc=1, device_id=partner, device_id_type=MESH)
+
+    def block(owner):
+        size = terms.shape[2] // 4
+        return terms.at[0, layer, pl.ds(pl.multiple_of(owner * size + first, 16), rows)]
+
+    own = pltpu.make_async_copy(block(me ^ 2), mine, in_sem)
+    far = pltpu.make_async_remote_copy(block(me ^ 3), got, send_sem, recv_sem, device_id=partner, device_id_type=MESH)
+    own.start()
+    pl.semaphore_wait(barrier, 1)
+    far.start()
+    own.wait()
+    far.wait_recv()
+    both[...] = (got[...].astype(jnp.float32) + mine[...].astype(jnp.float32)).astype(jnp.bfloat16)
+    far.wait_send()
+
+
+def first_pair(terms):
+    which, _, _, rows = CHUNKS[0]
+    cols = terms[which].shape[3]
+    return pl.pallas_call(
+        functools.partial(first_pair_body, CHUNKS[0]),
+        in_specs=[pl.BlockSpec(memory_space=pltpu.HBM)],
+        out_specs=pl.BlockSpec(memory_space=pltpu.VMEM),
+        out_shape=jax.ShapeDtypeStruct((rows, cols), jnp.bfloat16),
+        scratch_shapes=[pltpu.VMEM((rows, cols), jnp.bfloat16)] * 2 + [pltpu.SemaphoreType.DMA] * 3,
+        compiler_params=pltpu.CompilerParams(collective_id=0, has_side_effects=True, vmem_limit_bytes=52 * 2**20),
+        cost_estimate=pl.CostEstimate(flops=rows * cols, bytes_accessed=8 * rows * cols, transcendentals=0),
+        name="first_pair",
+    )(terms[which])
+
+
 def pair_tile(rows, cols):
-    return min(rows, 64 * 3072 // cols)
+    return math.gcd(rows, 64 * 3072 // cols)
 
 
 def pair(terms, index, nears):
@@ -113,7 +149,7 @@
 
 def adamw(me, terms, near, far, w, m, v, layer, first, rows, before):
     block, cols = m.shape[1], m.shape[2]
-    tile = min(rows, 64 * 3072 // cols)
+    tile = math.gcd(rows, first, block, 64 * 3072 // cols)
     at, per = first // tile, block // tile
     mine = pl.BlockSpec((1, tile, cols), lambda i, me: (layer, at + i, 0))
     whole = pl.BlockSpec((1, tile, cols), lambda i, me: (layer, me[0] * per + at + i, 0))
@@ -142,19 +178,14 @@
     )(me, terms, near, far, w, m, v, *before)
 
 
-def place_body(layer, first, rows, block, me, beside, across, corner, before, out, held, in_sem, out_sem):
-    blocks = (me[0] ^ 1, me[0] ^ 2, me[0] ^ 3)
-    ins = [pltpu.make_async_copy(src, held.at[i], in_sem.at[i]) for i, src in enumerate((beside, across, corner))]
-    outs = [
-        pltpu.make_async_copy(held.at[i], out.at[layer, pl.ds(pl.multiple_of(b * block + first, 16), rows)], out_sem.at[i])
-        for i, b in enumerate(blocks)
-    ]
-    for copy in ins:
+def place_body(layer, first, rows, block, me, beside, across, corner, before, out, sem):
+    copies = [
+        pltpu.make_async_copy(src, out.at[layer, pl.ds(pl.multiple_of((me[0] ^ other) * block + first, 16), rows)], sem.at[i])
+        for i, (src, other) in enumerate(((beside, 1), (across, 2), (corner, 3)))
+    ]
+    for copy in copies:
         copy.start()
-    for came, goes in zip(ins, outs):
-        came.wait()
-        goes.start()
-    for copy in outs:
+    for copy in copies:
         copy.wait()
 
 
@@ -163,15 +194,12 @@
     anywhere = pl.BlockSpec(memory_space=pl.ANY)
     return pl.pallas_call(
         functools.partial(place_body, layer, first, rows, block),
-        in_specs=[pl.BlockSpec(memory_space=pltpu.SMEM)] + [anywhere] * 4,
+        in_specs=[pl.BlockSpec(memory_space=pltpu.SMEM)] + [pl.BlockSpec(memory_space=pltpu.VMEM)] * 3 + [anywhere],
         out_specs=anywhere,
         out_shape=jax.ShapeDtypeStruct(out.shape, out.dtype),
         input_output_aliases={4: 0},
-        scratch_shapes=[
-            pltpu.VMEM((3, rows, cols), jnp.bfloat16),
-            pltpu.SemaphoreType.DMA((3,)),
-            pltpu.SemaphoreType.DMA((3,)),
-        ],
+        scratch_shapes=[pltpu.SemaphoreType.DMA((3,))],
+        compiler_params=pltpu.CompilerParams(vmem_limit_bytes=16 * 2**20),
         cost_estimate=pl.CostEstimate(flops=3 * rows * cols, bytes_accessed=12 * rows * cols, transcendentals=0),
         name="place",
     )(me, *pieces, out)
@@ -187,7 +215,7 @@
 
         arrived, near = [], []
         for c in range(len(CHUNKS)):
-            both, *more = pair(terms, c, () if c == 0 else (0, 1) if c == 1 else (c,))
+            both, *more = pair(terms, c, (0, 1) if c == 1 else (c,)) if c else (first_pair(terms),)
             near += more
             arrived.append(send(both, ACROSS))
 

time: 445 us -> 455 us (1.022)
    pallas_call x8 -> x11, Pallas kernels: 24.9 us -> 21.3 us  [place(): pl.pallas_call(functools.partial(place_body, layer, first, rows, block),...]
    pallas_call x8 -> x11, Pallas kernels: 60.8 us -> 64.2 us  [adamw(): pl.pallas_call(functools.partial(adamw_body, n_alias), grid_spec=pltpu.Pr...]
    ppermute x32 -> x44, starting transfers between devices: 23.3 us -> 25.4 us  [send(): return lax.ppermute(x, 'dp', to)]
    pallas_call x8 -> x10, Pallas kernels: 41.8 us -> 43.8 us  [pair(): pl.pallas_call(functools.partial(pair_body, chunk, nears), in_specs=[anyw...]
    ppermute x32 -> x44, waiting for transfers between devices: 288 us -> 288 us  [send(): return lax.ppermute(x, 'dp', to)]
  transfers between devices with their start and end apart: 32 -> 44, of which waited for: 12 -> 10; matrix products, arithmetic and copies ran while one was open for 0% -> 0% of each run, Pallas kernels for 28% -> 28%
where the time goes in v2:
time: 455 us; the launch traced here: 454 us
  waiting for transfers between devices  288 us (63%)
  Pallas kernels  131 us (29%)
  starting transfers between devices  25.4 us (6%)
  local copies, waits for them, and re-layouts  8.56 us (2%)
    ppermute x44, waiting for transfers between devices, send(): return lax.ppermute(x, 'dp', to)  288 us
    pallas_call x11, Pallas kernels, adamw(): pl.pallas_call(functools.partial(adamw_body, n_alias), grid_spec=pltpu.Pr...  64.2 us
    pallas_call x10, Pallas kernels, pair(): pl.pallas_call(functools.partial(pair_body, chunk, nears), in_specs=[anyw...  43.8 us
    ppermute x44, starting transfers between devices, send(): return lax.ppermute(x, 'dp', to)  25.4 us
    pallas_call x11, Pallas kernels, place(): pl.pallas_call(functools.partial(place_body, layer, first, rows, block),...  21.3 us
  transfers between devices with their start and end apart: 44, of which 10 were waited for; matrix products, arithmetic and copies ran while one was open for 0% of the time, Pallas kernels for 28%

profile of v2, /device:TPU:0, one launch (start us, length us, event | category | flops | bytes accessed | tf_op | source)
XLA Modules:
  0.0 454.5 jit_solution(8988812149538974809)
XLA Ops:
  0.6 2.2 first_pair.1
  2.8 2.9 collective-permute-start.3
  5.7 3.6 pair.12
  9.4 2.4 pair.15
  11.8 2.0 collective-permute-start.24
  13.8 2.4 pair.16
  16.4 0.7 copy-done.28
  17.0 2.8 adamw.11
  19.8 2.0 collective-permute-start.14
  21.8 2.8 pair.17
  24.6 5.4 %collective-permute-done.24.far = bf16[96,1024]{1,0:T(8,128)(2,1)S(1)} collective-permute-done((bf16[96,1024]{1,0:T(8,128)(2,1)}, bf16[96,1024]{1,0:T(8,128)(2,1)S(1)}, u32[]{:S(2)}, u32[]{:S(2)}) %collective-permute-start.24) | collective-permute-done | bytes 196640 | tf_op jit(solution)/shard_map/ppermute | solution.py:214
  30.0 3.8 pair.11
  33.9 6.2 %pair.10 = (bf16[256,3072]{1,0:T(8,128)(2,1)}, bf16[256,3072]{1,0:T(8,128)(2,1)}) custom-call(bf16[1,2,1024,3072]{3,2,1,0:T(8,128)(2,1)} %refs_0_.19, bf16[1,2,1024,3072]{3,2,1,0:T(8,128)(2,1)} %refs_1_.19, bf16[1,2,3072,1024]{3,2,1,0:T(8,128)(2,1)} %own.21), custom_call_target="tpu_custom_call" | custom-call | flops 786432 | bytes 7864320 | tf_op jit(solution)/shard_map/pair/pallas_call | solution.py:122
  40.1 2.0 collective-permute-start
  42.2 3.8 pair.18
  46.0 2.0 collective-permute-start.27
  48.1 6.3 %pair.19 = (bf16[768,1024]{1,0:T(8,128)(2,1)}, bf16[768,1024]{1,0:T(8,128)(2,1)}) custom-call(bf16[1,2,1024,3072]{3,2,1,0:T(8,128)(2,1)} %refs_0_.19, bf16[1,2,1024,3072]{3,2,1,0:T(8,128)(2,1)} %refs_1_.19, bf16[1,2,3072,1024]{3,2,1,0:T(8,128)(2,1)} %own.21), custom_call_target="tpu_custom_call" | custom-call | flops 786432 | bytes 7864320 | tf_op jit(solution)/shard_map/pair/pallas_call | solution.py:122
  54.4 5.6 %adamw.12 = (bf16[96,3072]{1,0:T(8,128)(2,1)}, bf16[2,1024,3072]{2,1,0:T(8,128)(2,1)}, f32[2,256,3072]{2,1,0:T(8,128)}, f32[2,256,3072]{2,1,0:T(8,128)}) custom-call(s32[1]{0:T(128)} %bitcast.me, bf16[1,2,1024,3072]{3,2,1,0:T(8,128)(2,1)} %refs_0_.19, ...), custom_call_target="tpu_custom_call", output_to_operand_aliasing={{1}: (7, {}), {2}: (8, {}), {3}: (9, {})} | custom-call | flops 4128768 | bytes 8257536 | tf_op jit(solution)/shard_map/adamw/pallas_call | solution.py:161
  60.8 6.2 %pair.13 = (bf16[256,3072]{1,0:T(8,128)(2,1)}, bf16[256,3072]{1,0:T(8,128)(2,1)}) custom-call(bf16[1,2,1024,3072]{3,2,1,0:T(8,128)(2,1)} %refs_0_.19, bf16[1,2,1024,3072]{3,2,1,0:T(8,128)(2,1)} %refs_1_.19, bf16[1,2,3072,1024]{3,2,1,0:T(8,128)(2,1)} %own.21), custom_call_target="tpu_custom_call" | custom-call | flops 786432 | bytes 7864320 | tf_op jit(solution)/shard_map/pair/pallas_call | solution.py:122
  67.0 30.5 %collective-permute-done.1.far = bf16[128,3072]{1,0:T(8,128)(2,1)} collective-permute-done((bf16[128,3072]{1,0:T(8,128)(2,1)}, bf16[128,3072]{1,0:T(8,128)(2,1)}, u32[]{:S(2)}, u32[]{:S(2)}) %collective-permute-start.1) | collective-permute-done | bytes 786464 | tf_op jit(solution)/shard_map/ppermute | solution.py:214
  97.5 6.2 %pair.14 = (bf16[256,3072]{1,0:T(8,128)(2,1)}, bf16[256,3072]{1,0:T(8,128)(2,1)}) custom-call(bf16[1,2,1024,3072]{3,2,1,0:T(8,128)(2,1)} %refs_0_.19, bf16[1,2,1024,3072]{3,2,1,0:T(8,128)(2,1)} %refs_1_.19, bf16[1,2,3072,1024]{3,2,1,0:T(8,128)(2,1)} %own.21), custom_call_target="tpu_custom_call" | custom-call | flops 786432 | bytes 7864320 | tf_op jit(solution)/shard_map/pair/pallas_call | solution.py:122
  103.7 10.6 %collective-permute-done.27.far = bf16[384,1024]{1,0:T(8,128)(2,1)S(1)} collective-permute-done((bf16[384,1024]{1,0:T(8,128)(2,1)}, bf16[384,1024]{1,0:T(8,128)(2,1)S(1)}, u32[]{:S(2)}, u32[]{:S(2)}) %collective-permute-start.27) | collective-permute-done | bytes 786464 | tf_op jit(solution)/shard_map/ppermute | solution.py:214
  114.3 2.0 collective-permute-start.11
  116.3 4.9 %adamw.13 = (bf16[128,3072]{1,0:T(8,128)(2,1)}, bf16[2,1024,3072]{2,1,0:T(8,128)(2,1)}, f32[2,256,3072]{2,1,0:T(8,128)}, f32[2,256,3072]{2,1,0:T(8,128)}) custom-call(s32[1]{0:T(128)} %bitcast.me, bf16[1,2,1024,3072]{3,2,1,0:T(8,128)(2,1)} %refs_0_.19, ...), custom_call_target="tpu_custom_call", output_to_operand_aliasing={{1}: (7, {}), {2}: (8, {}), {3}: (9, {})} | custom-call | flops 5505024 | bytes 11010048 | tf_op jit(solution)/shard_map/adamw/pallas_call | solution.py:161
  121.2 106.0 %collective-permute-done.11.across = bf16[96,3072]{1,0:T(8,128)(2,1)S(1)} collective-permute-done((bf16[96,3072]{1,0:T(8,128)(2,1)}, bf16[96,3072]{1,0:T(8,128)(2,1)S(1)}, u32[]{:S(2)}, u32[]{:S(2)}) %collective-permute-start.11) | collective-permute-done | bytes 589856 | tf_op jit(solution)/shard_map/ppermute | solution.py:214
  227.7 0.9 copy-done.22
  228.7 9.2 %adamw.17 = (bf16[768,1024]{1,0:T(8,128)(2,1)}, bf16[2,3072,1024]{2,1,0:T(8,128)(2,1)}, f32[2,768,1024]{2,1,0:T(8,128)}, f32[2,768,1024]{2,1,0:T(8,128)}) custom-call(s32[1]{0:T(128)} %bitcast.me, bf16[1,2,3072,1024]{3,2,1,0:T(8,128)(2,1)} %own.21, bf16[768,1024]{1,0:T(8,128)(2,1)} %get-tuple-element.113.near, bf16[768,1024]{1,0:T(8,128)(2,1)} %copy-done.22, ...), custom_call_target="tpu_custom_call" | custom-call | flops 11010048 | bytes 22020096 | tf_op jit(solution)/shard_map/adamw/pallas_call | solution.py:161
  237.9 4.9 %adamw.18 = (bf16[384,1024]{1,0:T(8,128)(2,1)}, bf16[2,3072,1024]{2,1,0:T(8,128)(2,1)}, f32[2,768,1024]{2,1,0:T(8,128)}, f32[2,768,1024]{2,1,0:T(8,128)}) custom-call(s32[1]{0:T(128)} %bitcast.me, bf16[1,2,3072,1024]{3,2,1,0:T(8,128)(2,1)} %own.21, ...), custom_call_target="tpu_custom_call", output_to_operand_aliasing={{1}: (7, {}), {2}: (8, {}), {3}: (9, {})} | custom-call | flops 5505024 | bytes 11010048 | tf_op jit(solution)/shard_map/adamw/pallas_call | solution.py:161
  242.8 3.8 adamw.19
  246.6 2.8 adamw.20
  249.3 2.8 adamw.21
  252.1 1.7 collective-permute-start.30
  254.7 9.2 %adamw.14 = (bf16[256,3072]{1,0:T(8,128)(2,1)}, bf16[2,1024,3072]{2,1,0:T(8,128)(2,1)}, f32[2,256,3072]{2,1,0:T(8,128)}, f32[2,256,3072]{2,1,0:T(8,128)}) custom-call(s32[1]{0:T(128)} %bitcast.me, bf16[1,2,1024,3072]{3,2,1,0:T(8,128)(2,1)} %refs_0_.19, ...), custom_call_target="tpu_custom_call", output_to_operand_aliasing={{1}: (7, {}), {2}: (8, {}), {3}: (9, {})} | custom-call | flops 11010048 | bytes 22020096 | tf_op jit(solution)/shard_map/adamw/pallas_call | solution.py:161
  263.9 0.8 copy-done.6
  264.8 1.7 collective-permute-start.36
  266.7 0.7 copy-done.18
  267.9 0.8 collective-permute-done.34.corner
  268.6 0.7 copy-done.20
  269.5 7.5 %collective-permute-done.36.across = bf16[192,1024]{1,0:T(8,128)(2,1)S(1)} collective-permute-done((bf16[192,1024]{1,0:T(8,128)(2,1)}, bf16[192,1024]{1,0:T(8,128)(2,1)S(1)}, u32[]{:S(2)}, u32[]{:S(2)}) %collective-permute-start.36) | collective-permute-done | bytes 393248 | tf_op jit(solution)/shard_map/ppermute | solution.py:214
  277.0 0.7 copy-done.8
  278.2 1.7 collective-permute-start.39
  279.9 9.2 %adamw.15 = (bf16[256,3072]{1,0:T(8,128)(2,1)}, bf16[2,1024,3072]{2,1,0:T(8,128)(2,1)}, f32[2,256,3072]{2,1,0:T(8,128)}, f32[2,256,3072]{2,1,0:T(8,128)}) custom-call(s32[1]{0:T(128)} %bitcast.me, bf16[1,2,1024,3072]{3,2,1,0:T(8,128)(2,1)} %refs_1_.19, bf16[256,3072]{1,0:T(8,128)(2,1)} %get-tuple-element.97.near, ...), custom_call_target="tpu_custom_call" | custom-call | flops 11010048 | bytes 22020096 | tf_op jit(solution)/shard_map/adamw/pallas_call | solution.py:161
  289.1 9.2 %adamw.16 = (bf16[256,3072]{1,0:T(8,128)(2,1)}, bf16[2,1024,3072]{2,1,0:T(8,128)(2,1)}, f32[2,256,3072]{2,1,0:T(8,128)}, f32[2,256,3072]{2,1,0:T(8,128)}) custom-call(s32[1]{0:T(128)} %bitcast.me, bf16[1,2,1024,3072]{3,2,1,0:T(8,128)(2,1)} %refs_1_.19, ...), custom_call_target="tpu_custom_call", output_to_operand_aliasing={{1}: (7, {}), {2}: (8, {}), {3}: (9, {})} | custom-call | flops 11010048 | bytes 22020096 | tf_op jit(solution)/shard_map/adamw/pallas_call | solution.py:161
  298.6 29.0 %collective-permute-done.39.across = bf16[384,1024]{1,0:T(8,128)(2,1)} collective-permute-done((bf16[384,1024]{1,0:T(8,128)(2,1)}, bf16[384,1024]{1,0:T(8,128)(2,1)}, u32[]{:S(2)}, u32[]{:S(2)}) %collective-permute-start.39) | collective-permute-done | bytes 786464 | tf_op jit(solution)/shard_map/ppermute | solution.py:214
  327.6 1.7 collective-permute-start.42
  329.7 31.6 %collective-permute-done.19.across = bf16[256,3072]{1,0:T(8,128)(2,1)S(1)} collective-permute-done((bf16[256,3072]{1,0:T(8,128)(2,1)}, bf16[256,3072]{1,0:T(8,128)(2,1)S(1)}, u32[]{:S(2)}, u32[]{:S(2)}) %collective-permute-start.19) | collective-permute-done | bytes 1572896 | tf_op jit(solution)/shard_map/ppermute | solution.py:214
  361.2 0.5 collective-permute-start.6
  361.8 33.2 %collective-permute-done.42.across = bf16[768,1024]{1,0:T(8,128)(2,1)S(1)} collective-permute-done((bf16[768,1024]{1,0:T(8,128)(2,1)}, bf16[768,1024]{1,0:T(8,128)(2,1)S(1)}, u32[]{:S(2)}, u32[]{:S(2)}) %collective-permute-start.42) | collective-permute-done | bytes 1572896 | tf_op jit(solution)/shard_map/ppermute | solution.py:214
  394.9 33.2 %collective-permute-done.22.across = bf16[256,3072]{1,0:T(8,128)(2,1)S(1)} collective-permute-done((bf16[256,3072]{1,0:T(8,128)(2,1)}, bf16[256,3072]{1,0:T(8,128)(2,1)S(1)}, u32[]{:S(2)}, u32[]{:S(2)}) %collective-permute-start.22) | collective-permute-done | bytes 1572896 | tf_op jit(solution)/shard_map/ppermute | solution.py:214
  428.2 0.5 collective-permute-start.18
  429.2 0.9 copy-done.11
  430.1 0.9 copy-done.13
  431.1 0.9 copy-done.15
  432.0 0.8 place.11.before
  433.6 1.2 place.12.before
  434.9 2.2 place.17.before
  437.1 2.8 place.18.before
  440.0 2.1 place.19.before
  442.1 2.8 place.13.before
  445.0 1.8 place.20.before
  446.8 2.2 place.14
  449.0 2.2 place.15.before
  451.2 2.2 place.16
  453.5 0.8 place.21
  (117 shorter events, 5.9 us)
Async XLA Ops:
  2.8 13.5 %collective-permute-start.3 = (bf16[32,3072]{1,0:T(8,128)(2,1)S(1)}, bf16[32,3072]{1,0:T(8,128)(2,1)S(1)}, u32[]{:S(2)}, u32[]{:S(2)}) collective-permute-start(bf16[32,3072]{1,0:T(8,128)(2,1)S(1)} %first_pair.1), channel_id=1, source_target_pairs={{0,2},{2,0},{1,3},{3,1},{4,6},{6,4},{5,7},{7,5}} | collective-permute-start | bytes 589832 | tf_op jit(solution)/shard_map/ppermute | solution.py:214
  9.3 38.7 %collective-permute-start.2 = (bf16[96,3072]{1,0:T(8,128)(2,1)}, bf16[96,3072]{1,0:T(8,128)(2,1)S(1)}, u32[]{:S(2)}, u32[]{:S(2)}) collective-permute-start(bf16[96,3072]{1,0:T(8,128)(2,1)} %get-tuple-element.79), channel_id=1, source_target_pairs={{0,2},{2,0},{1,3},{3,1},{4,6},{6,4},{5,7},{7,5}} | collective-permute-start | bytes 1769480 | tf_op jit(solution)/shard_map/ppermute | solution.py:214
  11.8 18.2 %collective-permute-start.24 = (bf16[96,1024]{1,0:T(8,128)(2,1)}, bf16[96,1024]{1,0:T(8,128)(2,1)S(1)}, u32[]{:S(2)}, u32[]{:S(2)}) collective-permute-start(bf16[96,1024]{1,0:T(8,128)(2,1)} %get-tuple-element.106), channel_id=1, source_target_pairs={{0,2},{2,0},{1,3},{3,1},{4,6},{6,4},{5,7},{7,5}} | collective-permute-start | bytes 589832 | tf_op jit(solution)/shard_map/ppermute | solution.py:214
  16.3 23.8 %collective-permute-start.25 = (bf16[96,1024]{1,0:T(8,128)(2,1)}, bf16[96,1024]{1,0:T(8,128)(2,1)S(1)}, u32[]{:S(2)}, u32[]{:S(2)}) collective-permute-start(bf16[96,1024]{1,0:T(8,128)(2,1)} %get-tuple-element.108), channel_id=1, source_target_pairs={{0,2},{2,0},{1,3},{3,1},{4,6},{6,4},{5,7},{7,5}} | collective-permute-start | bytes 589832 | tf_op jit(solution)/shard_map/ppermute | solution.py:214
  19.8 22.3 %collective-permute-start.13 = (bf16[32,3072]{1,0:T(8,128)(2,1)}, bf16[32,3072]{1,0:T(8,128)(2,1)S(1)}, u32[]{:S(2)}, u32[]{:S(2)}) collective-permute-start(bf16[32,3072]{1,0:T(8,128)(2,1)} %get-tuple-element.93), channel_id=1, source_target_pairs={{0,1},{1,0},{2,3},{3,2},{4,5},{5,4},{6,7},{7,6}} | collective-permute-start | bytes 589832 | tf_op jit(solution)/shard_map/ppermute | solution.py:214
  19.8 26.2 %collective-permute-start.14 = (bf16[32,3072]{1,0:T(8,128)(2,1)}, bf16[32,3072]{1,0:T(8,128)(2,1)S(1)}, u32[]{:S(2)}, u32[]{:S(2)}) collective-permute-start(bf16[32,3072]{1,0:T(8,128)(2,1)} %get-tuple-element.93), channel_id=1, source_target_pairs={{0,2},{2,0},{1,3},{3,1},{4,6},{6,4},{5,7},{7,5}} | collective-permute-start | bytes 589832 | tf_op jit(solution)/shard_map/ppermute | solution.py:214
  30.0 3.9 copy-start.26
  30.0 30.0 %collective-permute-start.26 = (bf16[192,1024]{1,0:T(8,128)(2,1)}, bf16[192,1024]{1,0:T(8,128)(2,1)S(1)}, u32[]{:S(2)}, u32[]{:S(2)}) collective-permute-start(bf16[192,1024]{1,0:T(8,128)(2,1)} %get-tuple-element.110), channel_id=1, source_target_pairs={{0,2},{2,0},{1,3},{3,1},{4,6},{6,4},{5,7},{7,5}} | collective-permute-start | bytes 1179656 | tf_op jit(solution)/shard_map/ppermute | solution.py:214
  40.1 5.9 %copy-start.27 = (bf16[96,1024]{1,0:T(8,128)(2,1)}, bf16[96,1024]{1,0:T(8,128)(2,1)S(1)}, u32[]{:S(2)}) copy-start(bf16[96,1024]{1,0:T(8,128)(2,1)S(1)} %collective-permute-done.25.far) | copy-start | bytes 589828
  40.1 187.1 %collective-permute-start = (bf16[256,3072]{1,0:T(8,128)(2,1)}, bf16[256,3072]{1,0:T(8,128)(2,1)}, u32[]{:S(2)}, u32[]{:S(2)}) collective-permute-start(bf16[256,3072]{1,0:T(8,128)(2,1)} %get-tuple-element.75), channel_id=1, source_target_pairs={{0,2},{2,0},{1,3},{3,1},{4,6},{6,4},{5,7},{7,5}} | collective-permute-start | bytes 4718600 | tf_op jit(solution)/shard_map/ppermute | solution.py:214
  42.1 3.9 copy-start.10
  42.1 55.4 %collective-permute-start.1 = (bf16[128,3072]{1,0:T(8,128)(2,1)}, bf16[128,3072]{1,0:T(8,128)(2,1)}, u32[]{:S(2)}, u32[]{:S(2)}) collective-permute-start(bf16[128,3072]{1,0:T(8,128)(2,1)} %get-tuple-element.77), channel_id=1, source_target_pairs={{0,2},{2,0},{1,3},{3,1},{4,6},{6,4},{5,7},{7,5}} | collective-permute-start | bytes 2359304 | tf_op jit(solution)/shard_map/ppermute | solution.py:214
  46.0 8.3 %copy-start.12 = (bf16[32,3072]{1,0:T(8,128)(2,1)}, bf16[32,3072]{1,0:T(8,128)(2,1)S(1)}, u32[]{:S(2)}) copy-start(bf16[32,3072]{1,0:T(8,128)(2,1)S(1)} %collective-permute-done.14.across) | copy-start | bytes 589828
  46.0 68.2 %collective-permute-start.27 = (bf16[384,1024]{1,0:T(8,128)(2,1)}, bf16[384,1024]{1,0:T(8,128)(2,1)S(1)}, u32[]{:S(2)}, u32[]{:S(2)}) collective-permute-start(bf16[384,1024]{1,0:T(8,128)(2,1)} %get-tuple-element.112), channel_id=1, source_target_pairs={{0,2},{2,0},{1,3},{3,1},{4,6},{6,4},{5,7},{7,5}} | collective-permute-start | bytes 2359304 | tf_op jit(solution)/shard_map/ppermute | solution.py:214
  48.0 6.3 %copy-start.24 = (bf16[96,3072]{1,0:T(8,128)(2,1)}, bf16[96,3072]{1,0:T(8,128)(2,1)S(1)}, u32[]{:S(2)}) copy-start(bf16[96,3072]{1,0:T(8,128)(2,1)S(1)} %collective-permute-done.2.far) | copy-start | bytes 1769476
  48.0 12.3 %collective-permute-start.15 = (bf16[32,3072]{1,0:T(8,128)(2,1)S(1)}, bf16[32,3072]{1,0:T(8,128)(2,1)S(1)}, u32[]{:S(2)}, u32[]{:S(2)}) collective-permute-start(bf16[32,3072]{1,0:T(8,128)(2,1)S(1)} %collective-permute-done.14.across), channel_id=1, source_target_pairs={{0,1},{1,0},{2,3},{3,2},{4,5},{5,4},{6,7},{7,6}} | collective-permute-start | bytes 589832 | tf_op jit(solution)/shard_map/ppermute | solution.py:214
  60.0 54.3 %collective-permute-start.10 = (bf16[96,3072]{1,0:T(8,128)(2,1)}, bf16[96,3072]{1,0:T(8,128)(2,1)S(1)}, u32[]{:S(2)}, u32[]{:S(2)}) collective-permute-start(bf16[96,3072]{1,0:T(8,128)(2,1)} %get-tuple-element.92), channel_id=1, source_target_pairs={{0,1},{1,0},{2,3},{3,2},{4,5},{5,4},{6,7},{7,6}} | collective-permute-start | bytes 1769480 | tf_op jit(solution)/shard_map/ppermute | solution.py:214
  60.7 6.3 %copy-start.14 = (bf16[32,3072]{1,0:T(8,128)(2,1)}, bf16[32,3072]{1,0:T(8,128)(2,1)S(1)}, u32[]{:S(2)}) copy-start(bf16[32,3072]{1,0:T(8,128)(2,1)S(1)} %collective-permute-done.15.corner) | copy-start | bytes 589828
  60.7 166.8 %collective-permute-start.28 = (bf16[768,1024]{1,0:T(8,128)(2,1)}, bf16[768,1024]{1,0:T(8,128)(2,1)S(1)}, u32[]{:S(2)}, u32[]{:S(2)}) collective-permute-start(bf16[768,1024]{1,0:T(8,128)(2,1)} %get-tuple-element.114), channel_id=1, source_target_pairs={{0,2},{2,0},{1,3},{3,1},{4,6},{6,4},{5,7},{7,5}} | collective-permute-start | bytes 4718600 | tf_op jit(solution)/shard_map/ppermute | solution.py:214
  97.5 156.7 %collective-permute-start.16 = (bf16[256,3072]{1,0:T(8,128)(2,1)}, bf16[256,3072]{1,0:T(8,128)(2,1)}, u32[]{:S(2)}, u32[]{:S(2)}) collective-permute-start(bf16[256,3072]{1,0:T(8,128)(2,1)} %get-tuple-element.96), channel_id=1, source_target_pairs={{0,2},{2,0},{1,3},{3,1},{4,6},{6,4},{5,7},{7,5}} | collective-permute-start | bytes 4718600 | tf_op jit(solution)/shard_map/ppermute | solution.py:214
  114.2 6.9 %copy-start.23 = (bf16[384,1024]{1,0:T(8,128)(2,1)}, bf16[384,1024]{1,0:T(8,128)(2,1)S(1)}, u32[]{:S(2)}) copy-start(bf16[384,1024]{1,0:T(8,128)(2,1)S(1)} %collective-permute-done.27.far) | copy-start | bytes 2359300
  114.3 139.9 %collective-permute-start.17 = (bf16[256,3072]{1,0:T(8,128)(2,1)}, bf16[256,3072]{1,0:T(8,128)(2,1)}, u32[]{:S(2)}, u32[]{:S(2)}) collective-permute-start(bf16[256,3072]{1,0:T(8,128)(2,1)} %get-tuple-element.98), channel_id=1, source_target_pairs={{0,2},{2,0},{1,3},{3,1},{4,6},{6,4},{5,7},{7,5}} | collective-permute-start | bytes 4718600 | tf_op jit(solution)/shard_map/ppermute | solution.py:214
  114.3 6.9 %copy-start.2 = (bf16[96,3072]{1,0:T(8,128)(2,1)}, bf16[96,3072]{1,0:T(8,128)(2,1)S(1)}, u32[]{:S(2)}) copy-start(bf16[96,3072]{1,0:T(8,128)(2,1)S(1)} %collective-permute-done.10.beside) | copy-start | bytes 1769476
  114.3 112.9 %collective-permute-start.11 = (bf16[96,3072]{1,0:T(8,128)(2,1)}, bf16[96,3072]{1,0:T(8,128)(2,1)S(1)}, u32[]{:S(2)}, u32[]{:S(2)}) collective-permute-start(bf16[96,3072]{1,0:T(8,128)(2,1)} %get-tuple-element.92), channel_id=1, source_target_pairs={{0,2},{2,0},{1,3},{3,1},{4,6},{6,4},{5,7},{7,5}} | collective-permute-start | bytes 1769480 | tf_op jit(solution)/shard_map/ppermute | solution.py:214
  227.2 10.7 %copy-start.4 = (bf16[96,3072]{1,0:T(8,128)(2,1)}, bf16[96,3072]{1,0:T(8,128)(2,1)S(1)}, u32[]{:S(2)}) copy-start(bf16[96,3072]{1,0:T(8,128)(2,1)S(1)} %collective-permute-done.11.across) | copy-start | bytes 1769476
  227.2 24.9 %collective-permute-start.7 = (bf16[128,3072]{1,0:T(8,128)(2,1)}, bf16[128,3072]{1,0:T(8,128)(2,1)S(1)}, u32[]{:S(2)}, u32[]{:S(2)}) collective-permute-start(bf16[128,3072]{1,0:T(8,128)(2,1)} %get-tuple-element.91), channel_id=1, source_target_pairs={{0,1},{1,0},{2,3},{3,2},{4,5},{5,4},{6,7},{7,6}} | collective-permute-start | bytes 2359304 | tf_op jit(solution)/shard_map/ppermute | solution.py:214
  227.2 26.7 %collective-permute-start.8 = (bf16[128,3072]{1,0:T(8,128)(2,1)}, bf16[128,3072]{1,0:T(8,128)(2,1)}, u32[]{:S(2)}, u32[]{:S(2)}) collective-permute-start(bf16[128,3072]{1,0:T(8,128)(2,1)} %get-tuple-element.91), channel_id=1, source_target_pairs={{0,2},{2,0},{1,3},{3,1},{4,6},{6,4},{5,7},{7,5}} | collective-permute-start | bytes 2359304 | tf_op jit(solution)/shard_map/ppermute | solution.py:214
  227.5 36.3 %collective-permute-start.12 = (bf16[96,3072]{1,0:T(8,128)(2,1)S(1)}, bf16[96,3072]{1,0:T(8,128)(2,1)S(1)}, u32[]{:S(2)}, u32[]{:S(2)}) collective-permute-start(bf16[96,3072]{1,0:T(8,128)(2,1)S(1)} %collective-permute-done.11.across), channel_id=1, source_target_pairs={{0,1},{1,0},{2,3},{3,2},{4,5},{5,4},{6,7},{7,6}} | collective-permute-start | bytes 1769480 | tf_op jit(solution)/shard_map/ppermute | solution.py:214
  249.3 4.5 copy-start.29
  252.1 11.7 %copy-start = (bf16[128,3072]{1,0:T(8,128)(2,1)}, bf16[128,3072]{1,0:T(8,128)(2,1)S(1)}, u32[]{:S(2)}) copy-start(bf16[128,3072]{1,0:T(8,128)(2,1)S(1)} %collective-permute-done.7.beside) | copy-start | bytes 2359300
  252.1 12.6 %collective-permute-start.30 = (bf16[96,1024]{1,0:T(8,128)(2,1)}, bf16[96,1024]{1,0:T(8,128)(2,1)S(1)}, u32[]{:S(2)}, u32[]{:S(2)}) collective-permute-start(bf16[96,1024]{1,0:T(8,128)(2,1)} %get-tuple-element.127), channel_id=1, source_target_pairs={{0,2},{2,0},{1,3},{3,1},{4,6},{6,4},{5,7},{7,5}} | collective-permute-start | bytes 589832 | tf_op jit(solution)/shard_map/ppermute | solution.py:214
  253.9 12.6 %collective-permute-start.33 = (bf16[96,1024]{1,0:T(8,128)(2,1)S(1)}, bf16[96,1024]{1,0:T(8,128)(2,1)}, u32[]{:S(2)}, u32[]{:S(2)}) collective-permute-start(bf16[96,1024]{1,0:T(8,128)(2,1)S(1)} %copy-done.29), channel_id=1, source_target_pairs={{0,2},{2,0},{1,3},{3,1},{4,6},{6,4},{5,7},{7,5}} | collective-permute-start | bytes 589832 | tf_op jit(solution)/shard_map/ppermute | solution.py:214
  254.2 12.5 %collective-permute-start.32 = (bf16[96,1024]{1,0:T(8,128)(2,1)S(1)}, bf16[96,1024]{1,0:T(8,128)(2,1)S(1)}, u32[]{:S(2)}, u32[]{:S(2)}) collective-permute-start(bf16[96,1024]{1,0:T(8,128)(2,1)S(1)} %copy-done.29), channel_id=1, source_target_pairs={{0,1},{1,0},{2,3},{3,2},{4,5},{5,4},{6,7},{7,6}} | collective-permute-start | bytes 589832 | tf_op jit(solution)/shard_map/ppermute | solution.py:214
  254.2 24.0 %collective-permute-start.9 = (bf16[128,3072]{1,0:T(8,128)(2,1)}, bf16[128,3072]{1,0:T(8,128)(2,1)}, u32[]{:S(2)}, u32[]{:S(2)}) collective-permute-start(bf16[128,3072]{1,0:T(8,128)(2,1)} %collective-permute-done.8.across), channel_id=1, source_target_pairs={{0,1},{1,0},{2,3},{3,2},{4,5},{5,4},{6,7},{7,6}} | collective-permute-start | bytes 2359304 | tf_op jit(solution)/shard_map/ppermute | solution.py:214
  264.7 64.6 %collective-permute-start.4 = (bf16[256,3072]{1,0:T(8,128)(2,1)}, bf16[256,3072]{1,0:T(8,128)(2,1)S(1)}, u32[]{:S(2)}, u32[]{:S(2)}) collective-permute-start(bf16[256,3072]{1,0:T(8,128)(2,1)} %get-tuple-element.90), channel_id=1, source_target_pairs={{0,1},{1,0},{2,3},{3,2},{4,5},{5,4},{6,7},{7,6}} | collective-permute-start | bytes 4718600 | tf_op jit(solution)/shard_map/ppermute | solution.py:214
  264.8 1.9 copy-start.16
  264.8 12.2 %collective-permute-start.36 = (bf16[192,1024]{1,0:T(8,128)(2,1)}, bf16[192,1024]{1,0:T(8,128)(2,1)S(1)}, u32[]{:S(2)}, u32[]{:S(2)}) collective-permute-start(bf16[192,1024]{1,0:T(8,128)(2,1)} %get-tuple-element.129), channel_id=1, source_target_pairs={{0,2},{2,0},{1,3},{3,1},{4,6},{6,4},{5,7},{7,5}} | collective-permute-start | bytes 1179656 | tf_op jit(solution)/shard_map/ppermute | solution.py:214
  266.5 2.1 collective-permute-start.34
  267.4 62.3 %collective-permute-start.5 = (bf16[256,3072]{1,0:T(8,128)(2,1)}, bf16[256,3072]{1,0:T(8,128)(2,1)S(1)}, u32[]{:S(2)}, u32[]{:S(2)}) collective-permute-start(bf16[256,3072]{1,0:T(8,128)(2,1)} %get-tuple-element.90), channel_id=1, source_target_pairs={{0,2},{2,0},{1,3},{3,1},{4,6},{6,4},{5,7},{7,5}} | collective-permute-start | bytes 4718600 | tf_op jit(solution)/shard_map/ppermute | solution.py:214
  269.3 7.7 %collective-permute-start.35 = (bf16[192,1024]{1,0:T(8,128)(2,1)}, bf16[192,1024]{1,0:T(8,128)(2,1)S(1)}, u32[]{:S(2)}, u32[]{:S(2)}) collective-permute-start(bf16[192,1024]{1,0:T(8,128)(2,1)} %get-tuple-element.129), channel_id=1, source_target_pairs={{0,1},{1,0},{2,3},{3,2},{4,5},{5,4},{6,7},{7,6}} | collective-permute-start | bytes 1179656 | tf_op jit(solution)/shard_map/ppermute | solution.py:214
  277.0 21.3 %collective-permute-start.37 = (bf16[192,1024]{1,0:T(8,128)(2,1)S(1)}, bf16[192,1024]{1,0:T(8,128)(2,1)}, u32[]{:S(2)}, u32[]{:S(2)}) collective-permute-start(bf16[192,1024]{1,0:T(8,128)(2,1)S(1)} %collective-permute-done.36.across), channel_id=1, source_target_pairs={{0,1},{1,0},{2,3},{3,2},{4,5},{5,4},{6,7},{7,6}} | collective-permute-start | bytes 1179656 | tf_op jit(solution)/shard_map/ppermute | solution.py:214
  277.7 20.9 %collective-permute-start.38 = (bf16[384,1024]{1,0:T(8,128)(2,1)}, bf16[384,1024]{1,0:T(8,128)(2,1)}, u32[]{:S(2)}, u32[]{:S(2)}) collective-permute-start(bf16[384,1024]{1,0:T(8,128)(2,1)} %get-tuple-element.130), channel_id=1, source_target_pairs={{0,1},{1,0},{2,3},{3,2},{4,5},{5,4},{6,7},{7,6}} | collective-permute-start | bytes 2359304 | tf_op jit(solution)/shard_map/ppermute | solution.py:214
  278.2 49.4 %collective-permute-start.39 = (bf16[384,1024]{1,0:T(8,128)(2,1)}, bf16[384,1024]{1,0:T(8,128)(2,1)}, u32[]{:S(2)}, u32[]{:S(2)}) collective-permute-start(bf16[384,1024]{1,0:T(8,128)(2,1)} %get-tuple-element.130), channel_id=1, source_target_pairs={{0,2},{2,0},{1,3},{3,1},{4,6},{6,4},{5,7},{7,5}} | collective-permute-start | bytes 2359304 | tf_op jit(solution)/shard_map/ppermute | solution.py:214
  298.3 62.9 %collective-permute-start.19 = (bf16[256,3072]{1,0:T(8,128)(2,1)}, bf16[256,3072]{1,0:T(8,128)(2,1)S(1)}, u32[]{:S(2)}, u32[]{:S(2)}) collective-permute-start(bf16[256,3072]{1,0:T(8,128)(2,1)} %get-tuple-element.102), channel_id=1, source_target_pairs={{0,2},{2,0},{1,3},{3,1},{4,6},{6,4},{5,7},{7,5}} | collective-permute-start | bytes 4718600 | tf_op jit(solution)/shard_map/ppermute | solution.py:214
  298.6 62.6 %collective-permute-start.21 = (bf16[256,3072]{1,0:T(8,128)(2,1)}, bf16[256,3072]{1,0:T(8,128)(2,1)S(1)}, u32[]{:S(2)}, u32[]{:S(2)}) collective-permute-start(bf16[256,3072]{1,0:T(8,128)(2,1)} %get-tuple-element.103), channel_id=1, source_target_pairs={{0,1},{1,0},{2,3},{3,2},{4,5},{5,4},{6,7},{7,6}} | collective-permute-start | bytes 4718600 | tf_op jit(solution)/shard_map/ppermute | solution.py:214
  327.6 67.3 %collective-permute-start.42 = (bf16[768,1024]{1,0:T(8,128)(2,1)}, bf16[768,1024]{1,0:T(8,128)(2,1)S(1)}, u32[]{:S(2)}, u32[]{:S(2)}) collective-permute-start(bf16[768,1024]{1,0:T(8,128)(2,1)} %get-tuple-element.131), channel_id=1, source_target_pairs={{0,2},{2,0},{1,3},{3,1},{4,6},{6,4},{5,7},{7,5}} | collective-permute-start | bytes 4718600 | tf_op jit(solution)/shard_map/ppermute | solution.py:214
  329.4 98.8 %collective-permute-start.22 = (bf16[256,3072]{1,0:T(8,128)(2,1)}, bf16[256,3072]{1,0:T(8,128)(2,1)S(1)}, u32[]{:S(2)}, u32[]{:S(2)}) collective-permute-start(bf16[256,3072]{1,0:T(8,128)(2,1)} %get-tuple-element.103), channel_id=1, source_target_pairs={{0,2},{2,0},{1,3},{3,1},{4,6},{6,4},{5,7},{7,5}} | collective-permute-start | bytes 4718600 | tf_op jit(solution)/shard_map/ppermute | solution.py:214
  329.7 99.0 %collective-permute-start.41 = (bf16[768,1024]{1,0:T(8,128)(2,1)}, bf16[768,1024]{1,0:T(8,128)(2,1)S(1)}, u32[]{:S(2)}, u32[]{:S(2)}) collective-permute-start(bf16[768,1024]{1,0:T(8,128)(2,1)} %get-tuple-element.131), channel_id=1, source_target_pairs={{0,1},{1,0},{2,3},{3,2},{4,5},{5,4},{6,7},{7,6}} | collective-permute-start | bytes 4718600 | tf_op jit(solution)/shard_map/ppermute | solution.py:214
  361.2 66.9 %collective-permute-start.40 = (bf16[384,1024]{1,0:T(8,128)(2,1)}, bf16[384,1024]{1,0:T(8,128)(2,1)S(1)}, u32[]{:S(2)}, u32[]{:S(2)}) collective-permute-start(bf16[384,1024]{1,0:T(8,128)(2,1)} %collective-permute-done.39.across), channel_id=1, source_target_pairs={{0,1},{1,0},{2,3},{3,2},{4,5},{5,4},{6,7},{7,6}} | collective-permute-start | bytes 2359304 | tf_op jit(solution)/shard_map/ppermute | solution.py:214
  361.2 67.5 %collective-permute-start.6 = (bf16[256,3072]{1,0:T(8,128)(2,1)S(1)}, bf16[256,3072]{1,0:T(8,128)(2,1)S(1)}, u32[]{:S(2)}, u32[]{:S(2)}) collective-permute-start(bf16[256,3072]{1,0:T(8,128)(2,1)S(1)} %collective-permute-done.5.across), channel_id=1, source_target_pairs={{0,1},{1,0},{2,3},{3,2},{4,5},{5,4},{6,7},{7,6}} | collective-permute-start | bytes 4718600 | tf_op jit(solution)/shard_map/ppermute | solution.py:214
  394.9 34.2 %collective-permute-start.43 = (bf16[768,1024]{1,0:T(8,128)(2,1)S(1)}, bf16[768,1024]{1,0:T(8,128)(2,1)S(1)}, u32[]{:S(2)}, u32[]{:S(2)}) collective-permute-start(bf16[768,1024]{1,0:T(8,128)(2,1)S(1)} %collective-permute-done.42.across), channel_id=1, source_target_pairs={{0,1},{1,0},{2,3},{3,2},{4,5},{5,4},{6,7},{7,6}} | collective-permute-start | bytes 4718600 | tf_op jit(solution)/shard_map/ppermute | solution.py:214
  428.2 20.8 %collective-permute-start.23 = (bf16[256,3072]{1,0:T(8,128)(2,1)S(1)}, bf16[256,3072]{1,0:T(8,128)(2,1)S(1)}, u32[]{:S(2)}, u32[]{:S(2)}) collective-permute-start(bf16[256,3072]{1,0:T(8,128)(2,1)S(1)} %collective-permute-done.22.across), channel_id=1, source_target_pairs={{0,1},{1,0},{2,3},{3,2},{4,5},{5,4},{6,7},{7,6}} | collective-permute-start | bytes 4718600 | tf_op jit(solution)/shard_map/ppermute | solution.py:214
  428.2 23.0 %collective-permute-start.18 = (bf16[256,3072]{1,0:T(8,128)(2,1)}, bf16[256,3072]{1,0:T(8,128)(2,1)S(1)}, u32[]{:S(2)}, u32[]{:S(2)}) collective-permute-start(bf16[256,3072]{1,0:T(8,128)(2,1)} %get-tuple-element.102), channel_id=1, source_target_pairs={{0,1},{1,0},{2,3},{3,2},{4,5},{5,4},{6,7},{7,6}} | collective-permute-start | bytes 4718600 | tf_op jit(solution)/shard_map/ppermute | solution.py:214
  428.7 22.5 %collective-permute-start.20 = (bf16[256,3072]{1,0:T(8,128)(2,1)S(1)}, bf16[256,3072]{1,0:T(8,128)(2,1)S(1)}, u32[]{:S(2)}, u32[]{:S(2)}) collective-permute-start(bf16[256,3072]{1,0:T(8,128)(2,1)S(1)} %collective-permute-done.19.across), channel_id=1, source_target_pairs={{0,1},{1,0},{2,3},{3,2},{4,5},{5,4},{6,7},{7,6}} | collective-permute-start | bytes 4718600 | tf_op jit(solution)/shard_map/ppermute | solution.py:214
  428.7 24.7 %collective-permute-start.29 = (bf16[96,1024]{1,0:T(8,128)(2,1)}, bf16[96,1024]{1,0:T(8,128)(2,1)S(1)}, u32[]{:S(2)}, u32[]{:S(2)}) collective-permute-start(bf16[96,1024]{1,0:T(8,128)(2,1)} %get-tuple-element.127), channel_id=1, source_target_pairs={{0,1},{1,0},{2,3},{3,2},{4,5},{5,4},{6,7},{7,6}} | collective-permute-start | bytes 589832 | tf_op jit(solution)/shard_map/ppermute | solution.py:214
  429.2 24.3 %collective-permute-start.31 = (bf16[96,1024]{1,0:T(8,128)(2,1)}, bf16[96,1024]{1,0:T(8,128)(2,1)S(1)}, u32[]{:S(2)}, u32[]{:S(2)}) collective-permute-start(bf16[96,1024]{1,0:T(8,128)(2,1)} %copy-done.16), channel_id=1, source_target_pairs={{0,1},{1,0},{2,3},{3,2},{4,5},{5,4},{6,7},{7,6}} | collective-permute-start | bytes 589832 | tf_op jit(solution)/shard_map/ppermute | solution.py:214
  432.0 1.3 copy-start.3
  432.0 1.5 copy-start.5
  432.0 1.6 copy-start.7
  437.1 2.9 copy-start.9
  440.0 2.1 copy-start.1
  442.1 2.9 copy-start.19
  442.1 2.9 copy-start.21
  451.2 2.3 copy-start.17
  (10 other events, 8.3 us)

commit v3 on v2

--- a/solution.py
+++ b/solution.py
@@ -13,10 +13,11 @@
 BESIDE = [(0, 1), (1, 0), (2, 3), (3, 2)]
 
 CHUNKS = (
-    (0, 0, 0, 32), (0, 0, 32, 96), (0, 0, 128, 128), (0, 1, 0, 256),
+    (0, 0, 0, 48), (0, 0, 48, 80), (0, 0, 128, 128), (0, 1, 0, 256),
     (1, 0, 0, 256), (1, 1, 0, 256),
-    (2, 0, 0, 768), (2, 1, 0, 384), (2, 1, 384, 192), (2, 1, 576, 96), (2, 1, 672, 96),
+    (2, 0, 0, 768), (2, 1, 0, 384), (2, 1, 384, 240), (2, 1, 624, 96), (2, 1, 720, 48),
 )
+LAST = len(CHUNKS) - 1
 MESH = pl.DeviceIdType.MESH
 
 
@@ -178,29 +179,33 @@
     )(me, terms, near, far, w, m, v, *before)
 
 
-def place_body(layer, first, rows, block, me, beside, across, corner, before, out, sem):
-    copies = [
-        pltpu.make_async_copy(src, out.at[layer, pl.ds(pl.multiple_of((me[0] ^ other) * block + first, 16), rows)], sem.at[i])
-        for i, (src, other) in enumerate(((beside, 1), (across, 2), (corner, 3)))
-    ]
+def place_body(chunks, block, me, *refs):
+    pieces, (_, out, sem) = refs[: 3 * len(chunks)], refs[3 * len(chunks) :]
+    copies = []
+    for i, src in enumerate(pieces):
+        _, layer, first, rows = chunks[i // 3]
+        owner = me[0] ^ (1 + i % 3)
+        copies.append(pltpu.make_async_copy(src, out.at[layer, pl.ds(pl.multiple_of(owner * block + first, 16), rows)], sem.at[i]))
     for copy in copies:
         copy.start()
     for copy in copies:
         copy.wait()
 
 
-def place(me, pieces, out, layer, first, rows, block):
+def place(me, chunks, pieces, out, block):
     cols = out.shape[2]
+    size = sum(chunk[3] for chunk in chunks) * cols
     anywhere = pl.BlockSpec(memory_space=pl.ANY)
-    return pl.pallas_call(
-        functools.partial(place_body, layer, first, rows, block),
-        in_specs=[pl.BlockSpec(memory_space=pltpu.SMEM)] + [pl.BlockSpec(memory_space=pltpu.VMEM)] * 3 + [anywhere],
+    n = 3 * len(chunks)
+    return pl.pallas_call(
+        functools.partial(place_body, chunks, block),
+        in_specs=[pl.BlockSpec(memory_space=pltpu.SMEM)] + [pl.BlockSpec(memory_space=pltpu.VMEM)] * n + [anywhere],
         out_specs=anywhere,
         out_shape=jax.ShapeDtypeStruct(out.shape, out.dtype),
-        input_output_aliases={4: 0},
-        scratch_shapes=[pltpu.SemaphoreType.DMA((3,))],
+        input_output_aliases={1 + n: 0},
+        scratch_shapes=[pltpu.SemaphoreType.DMA((n,))],
         compiler_params=pltpu.CompilerParams(vmem_limit_bytes=16 * 2**20),
-        cost_estimate=pl.CostEstimate(flops=3 * rows * cols, bytes_accessed=12 * rows * cols, transcendentals=0),
+        cost_estimate=pl.CostEstimate(flops=3 * size, bytes_accessed=12 * size, transcendentals=0),
         name="place",
     )(me, *pieces, out)
 
@@ -215,7 +220,7 @@
 
         arrived, near = [], []
         for c in range(len(CHUNKS)):
-            both, *more = pair(terms, c, (0, 1) if c == 1 else (c,)) if c else (first_pair(terms),)
+            both, *more = pair(terms, c, () if c == 1 else (0, 1, 2) if c == 2 else (c,)) if c else (first_pair(terms),)
             near += more
             arrived.append(send(both, ACROSS))
 
@@ -226,10 +231,13 @@
                 me, terms[which], near[c], arrived[c], weights[which], m[which], v[which], layer, first, rows, tuple(state[which]))
             across.append(send(one, ACROSS))
             beside.append(send(one, BESIDE))
-        for c, (which, layer, first, rows) in enumerate(CHUNKS):
+        for c in range(len(CHUNKS)):
             corner.append(send(across[c], BESIDE))
-        for c, (which, layer, first, rows) in enumerate(CHUNKS):
-            state[which][0] = place(me, (beside[c], across[c], corner[c]), state[which][0], layer, first, rows, m[which].shape[1])
+        for c in range(LAST):
+            which = CHUNKS[c][0]
+            together = (c,) if c < LAST - 1 else (c, LAST)
+            pieces = [got[i] for i in together for got in (beside, across, corner)]
+            state[which][0] = place(me, [CHUNKS[i] for i in together], pieces, state[which][0], m[which].shape[1])
         return tuple(state[which][i] for i in range(3) for which in range(3))
 
     all_of, cut_rows = P(None, None, None), P(None, "dp", None)

time: 455 us -> 452 us (level)
  waiting for transfers between devices: 288 us -> 281 us
    ppermute x44, waiting for transfers between devices: 288 us -> 281 us  [send(): return lax.ppermute(x, 'dp', to)]
    pallas_call x11 -> x10, Pallas kernels: 21.3 us -> 20.7 us  [place(): pl.pallas_call(functools.partial(place_body, chunks, block), in_specs=[pl...]
  transfers between devices with their start and end apart: 44 -> 44, of which waited for: 10 -> 11; matrix products, arithmetic and copies ran while one was open for 0% -> 0% of each run, Pallas kernels for 28% -> 29%
where the time goes in v3:
time: 452 us; the launch traced here: 451 us
  waiting for transfers between devices  281 us (62%)
  Pallas kernels  135 us (30%)
  starting transfers between devices  29.1 us (6%)
  local copies, waits for them, and re-layouts  5.41 us (1%)
    ppermute x44, waiting for transfers between devices, send(): return lax.ppermute(x, 'dp', to)  281 us
    pallas_call x11, Pallas kernels, adamw(): pl.pallas_call(functools.partial(adamw_body, n_alias), grid_spec=pltpu.Pr...  66.7 us
    pallas_call x10, Pallas kernels, pair(): pl.pallas_call(functools.partial(pair_body, chunk, nears), in_specs=[anyw...  44.9 us
    ppermute x44, starting transfers between devices, send(): return lax.ppermute(x, 'dp', to)  29.1 us
    pallas_call x10, Pallas kernels, place(): pl.pallas_call(functools.partial(place_body, chunks, block), in_specs=[pl...  20.7 us
  transfers between devices with their start and end apart: 44, of which 11 were waited for; matrix products, arithmetic and copies ran while one was open for 0% of the time, Pallas kernels for 29%

profile of v3, /device:TPU:0, one launch (start us, length us, event | category | flops | bytes accessed | tf_op | source)
XLA Modules:
  0.0 451.1 jit_solution(10768226302532437793)
XLA Ops:
  0.6 2.3 first_pair.1
  2.9 2.9 collective-permute-start.3
  5.9 2.9 pair.12
  8.9 2.2 pair.19
  11.1 2.0 collective-permute-start.31
  13.1 3.1 pair.16
  16.3 5.0 %pair.11 = (bf16[128,3072]{1,0:T(8,128)(2,1)}, bf16[48,3072]{1,0:T(8,128)(2,1)}, bf16[80,3072]{1,0:T(8,128)(2,1)}, bf16[128,3072]{1,0:T(8,128)(2,1)}) custom-call(bf16[1,2,1024,3072]{3,2,1,0:T(8,128)(2,1)} %refs_0_.19, bf16[1,2,1024,3072]{3,2,1,0:T(8,128)(2,1)} %refs_1_.19, bf16[1,2,3072,1024]{3,2,1,0:T(8,128)(2,1)} %own.21), custom_call_target="tpu_custom_call" | custom-call | flops 393216 | bytes 3932160 | tf_op jit(solution)/shard_map/pair/pallas_call | solution.py:123
  21.3 2.0 collective-permute-start.1
  23.3 3.8 pair.17
  27.2 1.2 collective-permute-start.26
  28.4 2.5 pair.15
  30.9 0.8 collective-permute-start.24
  31.7 6.2 %pair.18 = (bf16[768,1024]{1,0:T(8,128)(2,1)}, bf16[768,1024]{1,0:T(8,128)(2,1)}) custom-call(bf16[1,2,1024,3072]{3,2,1,0:T(8,128)(2,1)} %refs_0_.19, bf16[1,2,1024,3072]{3,2,1,0:T(8,128)(2,1)} %refs_1_.19, bf16[1,2,3072,1024]{3,2,1,0:T(8,128)(2,1)} %own.21), custom_call_target="tpu_custom_call" | custom-call | flops 786432 | bytes 7864320 | tf_op jit(solution)/shard_map/pair/pallas_call | solution.py:123
  37.9 4.0 adamw.11
  41.9 32.3 %collective-permute-done.24.far = bf16[96,1024]{1,0:T(8,128)(2,1)S(1)} collective-permute-done((bf16[96,1024]{1,0:T(8,128)(2,1)}, bf16[96,1024]{1,0:T(8,128)(2,1)S(1)}, u32[]{:S(2)}, u32[]{:S(2)}) %collective-permute-start.24) | collective-permute-done | bytes 196640 | tf_op jit(solution)/shard_map/ppermute | solution.py:219
  74.2 1.7 collective-permute-start.27
  76.0 0.8 copy-done.16
  77.0 5.7 %adamw.12 = (bf16[80,3072]{1,0:T(8,128)(2,1)}, bf16[2,1024,3072]{2,1,0:T(8,128)(2,1)}, f32[2,256,3072]{2,1,0:T(8,128)}, f32[2,256,3072]{2,1,0:T(8,128)}) custom-call(s32[1]{0:T(128)} %bitcast.me, bf16[1,2,1024,3072]{3,2,1,0:T(8,128)(2,1)} %refs_0_.19, ...), custom_call_target="tpu_custom_call", output_to_operand_aliasing={{1}: (7, {}), {2}: (8, {}), {3}: (9, {})} | custom-call | flops 3440640 | bytes 6881280 | tf_op jit(solution)/shard_map/adamw/pallas_call | solution.py:162
  82.7 0.7 copy-done.8
  83.5 6.9 %pair.10 = (bf16[256,3072]{1,0:T(8,128)(2,1)}, bf16[256,3072]{1,0:T(8,128)(2,1)}) custom-call(bf16[1,2,1024,3072]{3,2,1,0:T(8,128)(2,1)} %refs_0_.19, bf16[1,2,1024,3072]{3,2,1,0:T(8,128)(2,1)} %refs_1_.19, bf16[1,2,3072,1024]{3,2,1,0:T(8,128)(2,1)} %own.21), custom_call_target="tpu_custom_call" | custom-call | flops 786432 | bytes 7864320 | tf_op jit(solution)/shard_map/pair/pallas_call | solution.py:123
  90.3 26.2 %collective-permute-done.14.refs_1_ = bf16[48,3072]{1,0:T(8,128)(2,1)S(1)} collective-permute-done((bf16[48,3072]{1,0:T(8,128)(2,1)}, bf16[48,3072]{1,0:T(8,128)(2,1)S(1)}, u32[]{:S(2)}, u32[]{:S(2)}) %collective-permute-start.14) | collective-permute-done | bytes 294944 | tf_op jit(solution)/shard_map/ppermute | solution.py:219
  116.5 1.5 collective-permute-start
  118.0 0.6 collective-permute-start.11
  118.6 6.2 %pair.13 = (bf16[256,3072]{1,0:T(8,128)(2,1)}, bf16[256,3072]{1,0:T(8,128)(2,1)}) custom-call(bf16[1,2,1024,3072]{3,2,1,0:T(8,128)(2,1)} %refs_0_.19, bf16[1,2,1024,3072]{3,2,1,0:T(8,128)(2,1)} %refs_1_.19, bf16[1,2,3072,1024]{3,2,1,0:T(8,128)(2,1)} %own.21), custom_call_target="tpu_custom_call" | custom-call | flops 786432 | bytes 7864320 | tf_op jit(solution)/shard_map/pair/pallas_call | solution.py:123
  124.8 6.2 %pair.14 = (bf16[256,3072]{1,0:T(8,128)(2,1)}, bf16[256,3072]{1,0:T(8,128)(2,1)}) custom-call(bf16[1,2,1024,3072]{3,2,1,0:T(8,128)(2,1)} %refs_0_.19, bf16[1,2,1024,3072]{3,2,1,0:T(8,128)(2,1)} %refs_1_.19, bf16[1,2,3072,1024]{3,2,1,0:T(8,128)(2,1)} %own.21), custom_call_target="tpu_custom_call" | custom-call | flops 786432 | bytes 7864320 | tf_op jit(solution)/shard_map/pair/pallas_call | solution.py:123
  131.0 0.7 copy-done.12
  131.7 1.5 collective-permute-start.16
  133.7 30.9 %collective-permute-done.11.refs_1_ = bf16[80,3072]{1,0:T(8,128)(2,1)S(1)} collective-permute-done((bf16[80,3072]{1,0:T(8,128)(2,1)}, bf16[80,3072]{1,0:T(8,128)(2,1)S(1)}, u32[]{:S(2)}, u32[]{:S(2)}) %collective-permute-start.11) | collective-permute-done | bytes 491552 | tf_op jit(solution)/shard_map/ppermute | solution.py:219
  164.6 5.1 %adamw.13 = (bf16[128,3072]{1,0:T(8,128)(2,1)}, bf16[2,1024,3072]{2,1,0:T(8,128)(2,1)}, f32[2,256,3072]{2,1,0:T(8,128)}, f32[2,256,3072]{2,1,0:T(8,128)}) custom-call(s32[1]{0:T(128)} %bitcast.me, bf16[1,2,1024,3072]{3,2,1,0:T(8,128)(2,1)} %refs_0_.19, ...), custom_call_target="tpu_custom_call", output_to_operand_aliasing={{1}: (7, {}), {2}: (8, {}), {3}: (9, {})} | custom-call | flops 5505024 | bytes 11010048 | tf_op jit(solution)/shard_map/adamw/pallas_call | solution.py:162
  170.1 1.4 collective-permute-start.8
  171.6 9.2 %adamw.17 = (bf16[768,1024]{1,0:T(8,128)(2,1)}, bf16[2,3072,1024]{2,1,0:T(8,128)(2,1)}, f32[2,768,1024]{2,1,0:T(8,128)}, f32[2,768,1024]{2,1,0:T(8,128)}) custom-call(s32[1]{0:T(128)} %bitcast.me, bf16[1,2,3072,1024]{3,2,1,0:T(8,128)(2,1)} %own.21, bf16[768,1024]{1,0:T(8,128)(2,1)} %get-tuple-element.109.near, bf16[768,1024]{1,0:T(8,128)(2,1)} %copy-done.14, ...), custom_call_target="tpu_custom_call" | custom-call | flops 11010048 | bytes 22020096 | tf_op jit(solution)/shard_map/adamw/pallas_call | solution.py:162
  180.8 4.9 %adamw.18 = (bf16[384,1024]{1,0:T(8,128)(2,1)}, bf16[2,3072,1024]{2,1,0:T(8,128)(2,1)}, f32[2,768,1024]{2,1,0:T(8,128)}, f32[2,768,1024]{2,1,0:T(8,128)}) custom-call(s32[1]{0:T(128)} %bitcast.me, bf16[1,2,3072,1024]{3,2,1,0:T(8,128)(2,1)} %own.21, ...), custom_call_target="tpu_custom_call", output_to_operand_aliasing={{1}: (7, {}), {2}: (8, {}), {3}: (9, {})} | custom-call | flops 5505024 | bytes 11010048 | tf_op jit(solution)/shard_map/adamw/pallas_call | solution.py:162
  185.7 5.7 %adamw.19 = (bf16[240,1024]{1,0:T(8,128)(2,1)}, bf16[2,3072,1024]{2,1,0:T(8,128)(2,1)}, f32[2,768,1024]{2,1,0:T(8,128)}, f32[2,768,1024]{2,1,0:T(8,128)}) custom-call(s32[1]{0:T(128)} %bitcast.me, bf16[1,2,3072,1024]{3,2,1,0:T(8,128)(2,1)} %own.21, ...), custom_call_target="tpu_custom_call", output_to_operand_aliasing={{1}: (7, {}), {2}: (8, {}), {3}: (9, {})} | custom-call | flops 3440640 | bytes 6881280 | tf_op jit(solution)/shard_map/adamw/pallas_call | solution.py:162
  191.4 2.5 adamw.20
  193.9 2.2 adamw.21
  196.1 1.2 collective-permute-start.33
  197.3 9.2 %adamw.14 = (bf16[256,3072]{1,0:T(8,128)(2,1)}, bf16[2,1024,3072]{2,1,0:T(8,128)(2,1)}, f32[2,256,3072]{2,1,0:T(8,128)}, f32[2,256,3072]{2,1,0:T(8,128)}) custom-call(s32[1]{0:T(128)} %bitcast.me, bf16[1,2,1024,3072]{3,2,1,0:T(8,128)(2,1)} %refs_0_.19, ...), custom_call_target="tpu_custom_call", output_to_operand_aliasing={{1}: (7, {}), {2}: (8, {}), {3}: (9, {})} | custom-call | flops 11010048 | bytes 22020096 | tf_op jit(solution)/shard_map/adamw/pallas_call | solution.py:162
  206.5 42.4 %collective-permute-done.8.refs_1_ = bf16[128,3072]{1,0:T(8,128)(2,1)} collective-permute-done((bf16[128,3072]{1,0:T(8,128)(2,1)}, bf16[128,3072]{1,0:T(8,128)(2,1)}, u32[]{:S(2)}, u32[]{:S(2)}) %collective-permute-start.8) | collective-permute-done | bytes 786464 | tf_op jit(solution)/shard_map/ppermute | solution.py:219
  249.0 1.5 collective-permute-start.29
  250.4 0.6 collective-permute-start.5
  251.2 5.0 %collective-permute-done.29.refs_1_ = bf16[96,1024]{1,0:T(8,128)(2,1)} collective-permute-done((bf16[96,1024]{1,0:T(8,128)(2,1)S(1)}, bf16[96,1024]{1,0:T(8,128)(2,1)}, u32[]{:S(2)}, u32[]{:S(2)}) %collective-permute-start.29) | collective-permute-done | bytes 196640 | tf_op jit(solution)/shard_map/ppermute | solution.py:219
  256.2 2.1 collective-permute-start.36
  258.3 41.0 %collective-permute-done.36.refs_1_ = bf16[240,1024]{1,0:T(8,128)(2,1)} collective-permute-done((bf16[240,1024]{1,0:T(8,128)(2,1)}, bf16[240,1024]{1,0:T(8,128)(2,1)}, u32[]{:S(2)}, u32[]{:S(2)}) %collective-permute-start.36) | collective-permute-done | bytes 491552 | tf_op jit(solution)/shard_map/ppermute | solution.py:219
  299.2 1.5 collective-permute-start.39
  300.7 9.2 %adamw.15 = (bf16[256,3072]{1,0:T(8,128)(2,1)}, bf16[2,1024,3072]{2,1,0:T(8,128)(2,1)}, f32[2,256,3072]{2,1,0:T(8,128)}, f32[2,256,3072]{2,1,0:T(8,128)}) custom-call(s32[1]{0:T(128)} %bitcast.me, bf16[1,2,1024,3072]{3,2,1,0:T(8,128)(2,1)} %refs_1_.19, bf16[256,3072]{1,0:T(8,128)(2,1)} %get-tuple-element.95.near, ...), custom_call_target="tpu_custom_call" | custom-call | flops 11010048 | bytes 22020096 | tf_op jit(solution)/shard_map/adamw/pallas_call | solution.py:162
  309.9 9.2 %adamw.16 = (bf16[256,3072]{1,0:T(8,128)(2,1)}, bf16[2,1024,3072]{2,1,0:T(8,128)(2,1)}, f32[2,256,3072]{2,1,0:T(8,128)}, f32[2,256,3072]{2,1,0:T(8,128)}) custom-call(s32[1]{0:T(128)} %bitcast.me, bf16[1,2,1024,3072]{3,2,1,0:T(8,128)(2,1)} %refs_1_.19, ...), custom_call_target="tpu_custom_call", output_to_operand_aliasing={{1}: (7, {}), {2}: (8, {}), {3}: (9, {})} | custom-call | flops 11010048 | bytes 22020096 | tf_op jit(solution)/shard_map/adamw/pallas_call | solution.py:162
  320.2 3.2 collective-permute-done.37.refs_2_
  324.2 1.5 collective-permute-start.42
  325.6 31.5 %collective-permute-done.19.refs_1_ = bf16[256,3072]{1,0:T(8,128)(2,1)S(1)} collective-permute-done((bf16[256,3072]{1,0:T(8,128)(2,1)}, bf16[256,3072]{1,0:T(8,128)(2,1)S(1)}, u32[]{:S(2)}, u32[]{:S(2)}) %collective-permute-start.19) | collective-permute-done | bytes 1572896 | tf_op jit(solution)/shard_map/ppermute | solution.py:219
  357.6 33.2 %collective-permute-done.22.refs_1_ = bf16[256,3072]{1,0:T(8,128)(2,1)S(1)} collective-permute-done((bf16[256,3072]{1,0:T(8,128)(2,1)}, bf16[256,3072]{1,0:T(8,128)(2,1)S(1)}, u32[]{:S(2)}, u32[]{:S(2)}) %collective-permute-start.22) | collective-permute-done | bytes 1572896 | tf_op jit(solution)/shard_map/ppermute | solution.py:219
  390.8 32.8 %collective-permute-done.42.refs_1_ = bf16[768,1024]{1,0:T(8,128)(2,1)S(1)} collective-permute-done((bf16[768,1024]{1,0:T(8,128)(2,1)}, bf16[768,1024]{1,0:T(8,128)(2,1)S(1)}, u32[]{:S(2)}, u32[]{:S(2)}) %collective-permute-start.42) | collective-permute-done | bytes 1572896 | tf_op jit(solution)/shard_map/ppermute | solution.py:219
  424.7 2.3 collective-permute-done.43.refs_2_
  427.2 1.0 copy-done.11
  428.1 1.0 copy-done.13
  429.1 0.9 place.10.refs_3_
  430.7 1.1 place.11.refs_3_
  432.4 2.8 place.12.refs_3_
  435.2 2.2 place.16.refs_3_
  437.4 2.8 place.17.refs_3_
  440.2 2.3 place.18.refs_6_
  442.5 2.2 place.13
  444.8 2.2 place.14.refs_3_
  447.0 2.2 place.15
  449.2 1.9 place.19
  (98 shorter events, 6.5 us)
Async XLA Ops:
  2.9 27.9 %collective-permute-start.3 = (bf16[48,3072]{1,0:T(8,128)(2,1)S(1)}, bf16[48,3072]{1,0:T(8,128)(2,1)S(1)}, u32[]{:S(2)}, u32[]{:S(2)}) collective-permute-start(bf16[48,3072]{1,0:T(8,128)(2,1)S(1)} %first_pair.1), channel_id=1, source_target_pairs={{0,2},{2,0},{1,3},{3,1},{4,6},{6,4},{5,7},{7,5}} | collective-permute-start | bytes 884744 | tf_op jit(solution)/shard_map/ppermute | solution.py:219
  8.8 67.1 %collective-permute-start.2 = (bf16[80,3072]{1,0:T(8,128)(2,1)}, bf16[80,3072]{1,0:T(8,128)(2,1)S(1)}, u32[]{:S(2)}, u32[]{:S(2)}) collective-permute-start(bf16[80,3072]{1,0:T(8,128)(2,1)} %pair.12), channel_id=1, source_target_pairs={{0,2},{2,0},{1,3},{3,1},{4,6},{6,4},{5,7},{7,5}} | collective-permute-start | bytes 1474568 | tf_op jit(solution)/shard_map/ppermute | solution.py:219
  11.1 16.1 %collective-permute-start.31 = (bf16[48,1024]{1,0:T(8,128)(2,1)}, bf16[48,1024]{1,0:T(8,128)(2,1)S(1)}, u32[]{:S(2)}, u32[]{:S(2)}) collective-permute-start(bf16[48,1024]{1,0:T(8,128)(2,1)} %get-tuple-element.122), channel_id=1, source_target_pairs={{0,2},{2,0},{1,3},{3,1},{4,6},{6,4},{5,7},{7,5}} | collective-permute-start | bytes 294920 | tf_op jit(solution)/shard_map/ppermute | solution.py:219
  16.2 60.5 %collective-permute-start.25 = (bf16[240,1024]{1,0:T(8,128)(2,1)}, bf16[240,1024]{1,0:T(8,128)(2,1)S(1)}, u32[]{:S(2)}, u32[]{:S(2)}) collective-permute-start(bf16[240,1024]{1,0:T(8,128)(2,1)} %get-tuple-element.106), channel_id=1, source_target_pairs={{0,2},{2,0},{1,3},{3,1},{4,6},{6,4},{5,7},{7,5}} | collective-permute-start | bytes 1474568 | tf_op jit(solution)/shard_map/ppermute | solution.py:219
  21.3 95.3 %collective-permute-start.1 = (bf16[128,3072]{1,0:T(8,128)(2,1)}, bf16[128,3072]{1,0:T(8,128)(2,1)}, u32[]{:S(2)}, u32[]{:S(2)}) collective-permute-start(bf16[128,3072]{1,0:T(8,128)(2,1)} %get-tuple-element.76), channel_id=1, source_target_pairs={{0,2},{2,0},{1,3},{3,1},{4,6},{6,4},{5,7},{7,5}} | collective-permute-start | bytes 2359304 | tf_op jit(solution)/shard_map/ppermute | solution.py:219
  27.2 3.7 copy-start.19
  27.2 90.9 %collective-permute-start.26 = (bf16[384,1024]{1,0:T(8,128)(2,1)}, bf16[384,1024]{1,0:T(8,128)(2,1)}, u32[]{:S(2)}, u32[]{:S(2)}) collective-permute-start(bf16[384,1024]{1,0:T(8,128)(2,1)} %get-tuple-element.108), channel_id=1, source_target_pairs={{0,2},{2,0},{1,3},{3,1},{4,6},{6,4},{5,7},{7,5}} | collective-permute-start | bytes 2359304 | tf_op jit(solution)/shard_map/ppermute | solution.py:219
  30.9 7.0 %copy-start.17 = (bf16[48,3072]{1,0:T(8,128)(2,1)}, bf16[48,3072]{1,0:T(8,128)(2,1)S(1)}, u32[]{:S(2)}) copy-start(bf16[48,3072]{1,0:T(8,128)(2,1)S(1)} %collective-permute-done.3.far) | copy-start | bytes 884740
  30.9 43.3 %collective-permute-start.24 = (bf16[96,1024]{1,0:T(8,128)(2,1)}, bf16[96,1024]{1,0:T(8,128)(2,1)S(1)}, u32[]{:S(2)}, u32[]{:S(2)}) collective-permute-start(bf16[96,1024]{1,0:T(8,128)(2,1)} %get-tuple-element.104), channel_id=1, source_target_pairs={{0,2},{2,0},{1,3},{3,1},{4,6},{6,4},{5,7},{7,5}} | collective-permute-start | bytes 589832 | tf_op jit(solution)/shard_map/ppermute | solution.py:219
  74.2 8.5 %copy-start.18 = (bf16[96,1024]{1,0:T(8,128)(2,1)}, bf16[96,1024]{1,0:T(8,128)(2,1)S(1)}, u32[]{:S(2)}) copy-start(bf16[96,1024]{1,0:T(8,128)(2,1)S(1)} %collective-permute-done.24.far) | copy-start | bytes 589828
  74.2 95.9 %collective-permute-start.27 = (bf16[768,1024]{1,0:T(8,128)(2,1)}, bf16[768,1024]{1,0:T(8,128)(2,1)S(1)}, u32[]{:S(2)}, u32[]{:S(2)}) collective-permute-start(bf16[768,1024]{1,0:T(8,128)(2,1)} %get-tuple-element.110), channel_id=1, source_target_pairs={{0,2},{2,0},{1,3},{3,1},{4,6},{6,4},{5,7},{7,5}} | collective-permute-start | bytes 4718600 | tf_op jit(solution)/shard_map/ppermute | solution.py:219
  76.0 0.8 copy-start.16
  76.0 6.7 %collective-permute-start.13 = (bf16[48,3072]{1,0:T(8,128)(2,1)}, bf16[48,3072]{1,0:T(8,128)(2,1)S(1)}, u32[]{:S(2)}, u32[]{:S(2)}) collective-permute-start(bf16[48,3072]{1,0:T(8,128)(2,1)} %get-tuple-element.91), channel_id=1, source_target_pairs={{0,1},{1,0},{2,3},{3,2},{4,5},{5,4},{6,7},{7,6}} | collective-permute-start | bytes 884744 | tf_op jit(solution)/shard_map/ppermute | solution.py:219
  76.7 6.0 %copy-start.15 = (bf16[240,1024]{1,0:T(8,128)(2,1)}, bf16[240,1024]{1,0:T(8,128)(2,1)S(1)}, u32[]{:S(2)}) copy-start(bf16[240,1024]{1,0:T(8,128)(2,1)S(1)} %collective-permute-done.25.far) | copy-start | bytes 1474564
  76.7 39.8 %collective-permute-start.14 = (bf16[48,3072]{1,0:T(8,128)(2,1)}, bf16[48,3072]{1,0:T(8,128)(2,1)S(1)}, u32[]{:S(2)}, u32[]{:S(2)}) collective-permute-start(bf16[48,3072]{1,0:T(8,128)(2,1)} %get-tuple-element.91), channel_id=1, source_target_pairs={{0,2},{2,0},{1,3},{3,1},{4,6},{6,4},{5,7},{7,5}} | collective-permute-start | bytes 884744 | tf_op jit(solution)/shard_map/ppermute | solution.py:219
  82.7 0.7 copy-start.8
  83.5 49.7 %collective-permute-start.10 = (bf16[80,3072]{1,0:T(8,128)(2,1)}, bf16[80,3072]{1,0:T(8,128)(2,1)S(1)}, u32[]{:S(2)}, u32[]{:S(2)}) collective-permute-start(bf16[80,3072]{1,0:T(8,128)(2,1)} %get-tuple-element.90), channel_id=1, source_target_pairs={{0,1},{1,0},{2,3},{3,2},{4,5},{5,4},{6,7},{7,6}} | collective-permute-start | bytes 1474568 | tf_op jit(solution)/shard_map/ppermute | solution.py:219
  116.5 8.2 %copy-start.10 = (bf16[48,3072]{1,0:T(8,128)(2,1)}, bf16[48,3072]{1,0:T(8,128)(2,1)S(1)}, u32[]{:S(2)}) copy-start(bf16[48,3072]{1,0:T(8,128)(2,1)S(1)} %collective-permute-done.14.refs_1_) | copy-start | bytes 884740
  116.5 14.4 %collective-permute-start.15 = (bf16[48,3072]{1,0:T(8,128)(2,1)S(1)}, bf16[48,3072]{1,0:T(8,128)(2,1)S(1)}, u32[]{:S(2)}, u32[]{:S(2)}) collective-permute-start(bf16[48,3072]{1,0:T(8,128)(2,1)S(1)} %collective-permute-done.14.refs_1_), channel_id=1, source_target_pairs={{0,1},{1,0},{2,3},{3,2},{4,5},{5,4},{6,7},{7,6}} | collective-permute-start | bytes 884744 | tf_op jit(solution)/shard_map/ppermute | solution.py:219
  116.5 74.8 %collective-permute-start = (bf16[256,3072]{1,0:T(8,128)(2,1)}, bf16[256,3072]{1,0:T(8,128)(2,1)}, u32[]{:S(2)}, u32[]{:S(2)}) collective-permute-start(bf16[256,3072]{1,0:T(8,128)(2,1)} %get-tuple-element.74), channel_id=1, source_target_pairs={{0,2},{2,0},{1,3},{3,1},{4,6},{6,4},{5,7},{7,5}} | collective-permute-start | bytes 4718600 | tf_op jit(solution)/shard_map/ppermute | solution.py:219
  118.0 46.5 %collective-permute-start.11 = (bf16[80,3072]{1,0:T(8,128)(2,1)}, bf16[80,3072]{1,0:T(8,128)(2,1)S(1)}, u32[]{:S(2)}, u32[]{:S(2)}) collective-permute-start(bf16[80,3072]{1,0:T(8,128)(2,1)} %get-tuple-element.90), channel_id=1, source_target_pairs={{0,2},{2,0},{1,3},{3,1},{4,6},{6,4},{5,7},{7,5}} | collective-permute-start | bytes 1474568 | tf_op jit(solution)/shard_map/ppermute | solution.py:219
  131.7 118.7 %collective-permute-start.16 = (bf16[256,3072]{1,0:T(8,128)(2,1)}, bf16[256,3072]{1,0:T(8,128)(2,1)}, u32[]{:S(2)}, u32[]{:S(2)}) collective-permute-start(bf16[256,3072]{1,0:T(8,128)(2,1)} %get-tuple-element.94), channel_id=1, source_target_pairs={{0,2},{2,0},{1,3},{3,1},{4,6},{6,4},{5,7},{7,5}} | collective-permute-start | bytes 4718600 | tf_op jit(solution)/shard_map/ppermute | solution.py:219
  133.2 36.5 %copy-start.2 = (bf16[80,3072]{1,0:T(8,128)(2,1)}, bf16[80,3072]{1,0:T(8,128)(2,1)S(1)}, u32[]{:S(2)}) copy-start(bf16[80,3072]{1,0:T(8,128)(2,1)S(1)} %collective-permute-done.10.refs_0_) | copy-start | bytes 1474564
  133.2 117.3 %collective-permute-start.17 = (bf16[256,3072]{1,0:T(8,128)(2,1)}, bf16[256,3072]{1,0:T(8,128)(2,1)}, u32[]{:S(2)}, u32[]{:S(2)}) collective-permute-start(bf16[256,3072]{1,0:T(8,128)(2,1)} %get-tuple-element.96), channel_id=1, source_target_pairs={{0,2},{2,0},{1,3},{3,1},{4,6},{6,4},{5,7},{7,5}} | collective-permute-start | bytes 4718600 | tf_op jit(solution)/shard_map/ppermute | solution.py:219
  164.6 5.1 %copy-start.4 = (bf16[80,3072]{1,0:T(8,128)(2,1)}, bf16[80,3072]{1,0:T(8,128)(2,1)S(1)}, u32[]{:S(2)}) copy-start(bf16[80,3072]{1,0:T(8,128)(2,1)S(1)} %collective-permute-done.11.refs_1_) | copy-start | bytes 1474564
  164.6 5.1 %collective-permute-start.12 = (bf16[80,3072]{1,0:T(8,128)(2,1)S(1)}, bf16[80,3072]{1,0:T(8,128)(2,1)S(1)}, u32[]{:S(2)}, u32[]{:S(2)}) collective-permute-start(bf16[80,3072]{1,0:T(8,128)(2,1)S(1)} %collective-permute-done.11.refs_1_), channel_id=1, source_target_pairs={{0,1},{1,0},{2,3},{3,2},{4,5},{5,4},{6,7},{7,6}} | collective-permute-start | bytes 1474568 | tf_op jit(solution)/shard_map/ppermute | solution.py:219
  169.7 11.1 %copy-start.6 = (bf16[80,3072]{1,0:T(8,128)(2,1)}, bf16[80,3072]{1,0:T(8,128)(2,1)S(1)}, u32[]{:S(2)}) copy-start(bf16[80,3072]{1,0:T(8,128)(2,1)S(1)} %collective-permute-done.12.refs_2_) | copy-start | bytes 1474564
  169.7 26.4 %collective-permute-start.7 = (bf16[128,3072]{1,0:T(8,128)(2,1)}, bf16[128,3072]{1,0:T(8,128)(2,1)S(1)}, u32[]{:S(2)}, u32[]{:S(2)}) collective-permute-start(bf16[128,3072]{1,0:T(8,128)(2,1)} %get-tuple-element.89), channel_id=1, source_target_pairs={{0,1},{1,0},{2,3},{3,2},{4,5},{5,4},{6,7},{7,6}} | collective-permute-start | bytes 2359304 | tf_op jit(solution)/shard_map/ppermute | solution.py:219
  170.1 1.4 copy-start.14
  170.1 78.8 %collective-permute-start.8 = (bf16[128,3072]{1,0:T(8,128)(2,1)}, bf16[128,3072]{1,0:T(8,128)(2,1)}, u32[]{:S(2)}, u32[]{:S(2)}) collective-permute-start(bf16[128,3072]{1,0:T(8,128)(2,1)} %get-tuple-element.89), channel_id=1, source_target_pairs={{0,2},{2,0},{1,3},{3,1},{4,6},{6,4},{5,7},{7,5}} | collective-permute-start | bytes 2359304 | tf_op jit(solution)/shard_map/ppermute | solution.py:219
  191.4 66.9 %collective-permute-start.35 = (bf16[240,1024]{1,0:T(8,128)(2,1)}, bf16[240,1024]{1,0:T(8,128)(2,1)}, u32[]{:S(2)}, u32[]{:S(2)}) collective-permute-start(bf16[240,1024]{1,0:T(8,128)(2,1)} %get-tuple-element.127), channel_id=1, source_target_pairs={{0,1},{1,0},{2,3},{3,2},{4,5},{5,4},{6,7},{7,6}} | collective-permute-start | bytes 1474568 | tf_op jit(solution)/shard_map/ppermute | solution.py:219
  196.1 10.4 %copy-start = (bf16[128,3072]{1,0:T(8,128)(2,1)}, bf16[128,3072]{1,0:T(8,128)(2,1)S(1)}, u32[]{:S(2)}) copy-start(bf16[128,3072]{1,0:T(8,128)(2,1)S(1)} %collective-permute-done.7.refs_0_) | copy-start | bytes 2359300
  196.1 54.9 %collective-permute-start.33 = (bf16[48,1024]{1,0:T(8,128)(2,1)}, bf16[48,1024]{1,0:T(8,128)(2,1)S(1)}, u32[]{:S(2)}, u32[]{:S(2)}) collective-permute-start(bf16[48,1024]{1,0:T(8,128)(2,1)} %get-tuple-element.126), channel_id=1, source_target_pairs={{0,2},{2,0},{1,3},{3,1},{4,6},{6,4},{5,7},{7,5}} | collective-permute-start | bytes 294920 | tf_op jit(solution)/shard_map/ppermute | solution.py:219
  197.3 51.7 %copy-start.20 = (bf16[96,1024]{1,0:T(8,128)(2,1)S(1)}, bf16[96,1024]{1,0:T(8,128)(2,1)}, u32[]{:S(2)}) copy-start(bf16[96,1024]{1,0:T(8,128)(2,1)} %get-tuple-element.120) | copy-start | bytes 589828
  249.0 7.2 %collective-permute-start.29 = (bf16[96,1024]{1,0:T(8,128)(2,1)S(1)}, bf16[96,1024]{1,0:T(8,128)(2,1)}, u32[]{:S(2)}, u32[]{:S(2)}) collective-permute-start(bf16[96,1024]{1,0:T(8,128)(2,1)S(1)} %copy-done.20), channel_id=1, source_target_pairs={{0,2},{2,0},{1,3},{3,1},{4,6},{6,4},{5,7},{7,5}} | collective-permute-start | bytes 589832 | tf_op jit(solution)/shard_map/ppermute | solution.py:219
  250.4 73.2 %collective-permute-start.4 = (bf16[256,3072]{1,0:T(8,128)(2,1)}, bf16[256,3072]{1,0:T(8,128)(2,1)S(1)}, u32[]{:S(2)}, u32[]{:S(2)}) collective-permute-start(bf16[256,3072]{1,0:T(8,128)(2,1)} %get-tuple-element.88), channel_id=1, source_target_pairs={{0,1},{1,0},{2,3},{3,2},{4,5},{5,4},{6,7},{7,6}} | collective-permute-start | bytes 4718600 | tf_op jit(solution)/shard_map/ppermute | solution.py:219
  250.4 73.7 %collective-permute-start.5 = (bf16[256,3072]{1,0:T(8,128)(2,1)}, bf16[256,3072]{1,0:T(8,128)(2,1)S(1)}, u32[]{:S(2)}, u32[]{:S(2)}) collective-permute-start(bf16[256,3072]{1,0:T(8,128)(2,1)} %get-tuple-element.88), channel_id=1, source_target_pairs={{0,2},{2,0},{1,3},{3,1},{4,6},{6,4},{5,7},{7,5}} | collective-permute-start | bytes 4718600 | tf_op jit(solution)/shard_map/ppermute | solution.py:219
  251.0 68.1 %collective-permute-start.9 = (bf16[128,3072]{1,0:T(8,128)(2,1)}, bf16[128,3072]{1,0:T(8,128)(2,1)}, u32[]{:S(2)}, u32[]{:S(2)}) collective-permute-start(bf16[128,3072]{1,0:T(8,128)(2,1)} %collective-permute-done.8.refs_1_), channel_id=1, source_target_pairs={{0,1},{1,0},{2,3},{3,2},{4,5},{5,4},{6,7},{7,6}} | collective-permute-start | bytes 2359304 | tf_op jit(solution)/shard_map/ppermute | solution.py:219
  256.2 43.1 %collective-permute-start.36 = (bf16[240,1024]{1,0:T(8,128)(2,1)}, bf16[240,1024]{1,0:T(8,128)(2,1)}, u32[]{:S(2)}, u32[]{:S(2)}) collective-permute-start(bf16[240,1024]{1,0:T(8,128)(2,1)} %get-tuple-element.127), channel_id=1, source_target_pairs={{0,2},{2,0},{1,3},{3,1},{4,6},{6,4},{5,7},{7,5}} | collective-permute-start | bytes 1474568 | tf_op jit(solution)/shard_map/ppermute | solution.py:219
  258.3 60.8 %collective-permute-start.38 = (bf16[384,1024]{1,0:T(8,128)(2,1)}, bf16[384,1024]{1,0:T(8,128)(2,1)}, u32[]{:S(2)}, u32[]{:S(2)}) collective-permute-start(bf16[384,1024]{1,0:T(8,128)(2,1)} %get-tuple-element.128), channel_id=1, source_target_pairs={{0,1},{1,0},{2,3},{3,2},{4,5},{5,4},{6,7},{7,6}} | collective-permute-start | bytes 2359304 | tf_op jit(solution)/shard_map/ppermute | solution.py:219
  299.2 20.4 %collective-permute-start.39 = (bf16[384,1024]{1,0:T(8,128)(2,1)}, bf16[384,1024]{1,0:T(8,128)(2,1)}, u32[]{:S(2)}, u32[]{:S(2)}) collective-permute-start(bf16[384,1024]{1,0:T(8,128)(2,1)} %get-tuple-element.128), channel_id=1, source_target_pairs={{0,2},{2,0},{1,3},{3,1},{4,6},{6,4},{5,7},{7,5}} | collective-permute-start | bytes 2359304 | tf_op jit(solution)/shard_map/ppermute | solution.py:219
  309.9 117.3 %copy-start.9 = (bf16[48,3072]{1,0:T(8,128)(2,1)S(1)}, bf16[48,3072]{1,0:T(8,128)(2,1)}, u32[]{:S(2)}) copy-start(bf16[48,3072]{1,0:T(8,128)(2,1)} %copy-done.8) | copy-start | bytes 884740
  319.1 6.5 %collective-permute-start.18 = (bf16[256,3072]{1,0:T(8,128)(2,1)}, bf16[256,3072]{1,0:T(8,128)(2,1)S(1)}, u32[]{:S(2)}, u32[]{:S(2)}) collective-permute-start(bf16[256,3072]{1,0:T(8,128)(2,1)} %get-tuple-element.100), channel_id=1, source_target_pairs={{0,1},{1,0},{2,3},{3,2},{4,5},{5,4},{6,7},{7,6}} | collective-permute-start | bytes 4718600 | tf_op jit(solution)/shard_map/ppermute | solution.py:219
  319.1 4.3 collective-permute-start.37
  319.6 37.5 %collective-permute-start.19 = (bf16[256,3072]{1,0:T(8,128)(2,1)}, bf16[256,3072]{1,0:T(8,128)(2,1)S(1)}, u32[]{:S(2)}, u32[]{:S(2)}) collective-permute-start(bf16[256,3072]{1,0:T(8,128)(2,1)} %get-tuple-element.100), channel_id=1, source_target_pairs={{0,2},{2,0},{1,3},{3,1},{4,6},{6,4},{5,7},{7,5}} | collective-permute-start | bytes 4718600 | tf_op jit(solution)/shard_map/ppermute | solution.py:219
  323.5 33.7 %collective-permute-start.21 = (bf16[256,3072]{1,0:T(8,128)(2,1)}, bf16[256,3072]{1,0:T(8,128)(2,1)S(1)}, u32[]{:S(2)}, u32[]{:S(2)}) collective-permute-start(bf16[256,3072]{1,0:T(8,128)(2,1)} %get-tuple-element.101), channel_id=1, source_target_pairs={{0,1},{1,0},{2,3},{3,2},{4,5},{5,4},{6,7},{7,6}} | collective-permute-start | bytes 4718600 | tf_op jit(solution)/shard_map/ppermute | solution.py:219
  323.6 67.2 %collective-permute-start.22 = (bf16[256,3072]{1,0:T(8,128)(2,1)}, bf16[256,3072]{1,0:T(8,128)(2,1)S(1)}, u32[]{:S(2)}, u32[]{:S(2)}) collective-permute-start(bf16[256,3072]{1,0:T(8,128)(2,1)} %get-tuple-element.101), channel_id=1, source_target_pairs={{0,2},{2,0},{1,3},{3,1},{4,6},{6,4},{5,7},{7,5}} | collective-permute-start | bytes 4718600 | tf_op jit(solution)/shard_map/ppermute | solution.py:219
  324.2 99.4 %collective-permute-start.42 = (bf16[768,1024]{1,0:T(8,128)(2,1)}, bf16[768,1024]{1,0:T(8,128)(2,1)S(1)}, u32[]{:S(2)}, u32[]{:S(2)}) collective-permute-start(bf16[768,1024]{1,0:T(8,128)(2,1)} %get-tuple-element.129), channel_id=1, source_target_pairs={{0,2},{2,0},{1,3},{3,1},{4,6},{6,4},{5,7},{7,5}} | collective-permute-start | bytes 4718600 | tf_op jit(solution)/shard_map/ppermute | solution.py:219
  325.6 98.0 %collective-permute-start.40 = (bf16[384,1024]{1,0:T(8,128)(2,1)}, bf16[384,1024]{1,0:T(8,128)(2,1)S(1)}, u32[]{:S(2)}, u32[]{:S(2)}) collective-permute-start(bf16[384,1024]{1,0:T(8,128)(2,1)} %collective-permute-done.39.refs_1_), channel_id=1, source_target_pairs={{0,1},{1,0},{2,3},{3,2},{4,5},{5,4},{6,7},{7,6}} | collective-permute-start | bytes 2359304 | tf_op jit(solution)/shard_map/ppermute | solution.py:219
  357.1 67.0 %collective-permute-start.41 = (bf16[768,1024]{1,0:T(8,128)(2,1)}, bf16[768,1024]{1,0:T(8,128)(2,1)S(1)}, u32[]{:S(2)}, u32[]{:S(2)}) collective-permute-start(bf16[768,1024]{1,0:T(8,128)(2,1)} %get-tuple-element.129), channel_id=1, source_target_pairs={{0,1},{1,0},{2,3},{3,2},{4,5},{5,4},{6,7},{7,6}} | collective-permute-start | bytes 4718600 | tf_op jit(solution)/shard_map/ppermute | solution.py:219
  357.1 67.0 %collective-permute-start.6 = (bf16[256,3072]{1,0:T(8,128)(2,1)S(1)}, bf16[256,3072]{1,0:T(8,128)(2,1)S(1)}, u32[]{:S(2)}, u32[]{:S(2)}) collective-permute-start(bf16[256,3072]{1,0:T(8,128)(2,1)S(1)} %collective-permute-done.5.refs_1_), channel_id=1, source_target_pairs={{0,1},{1,0},{2,3},{3,2},{4,5},{5,4},{6,7},{7,6}} | collective-permute-start | bytes 4718600 | tf_op jit(solution)/shard_map/ppermute | solution.py:219
  390.8 33.8 %collective-permute-start.23 = (bf16[256,3072]{1,0:T(8,128)(2,1)S(1)}, bf16[256,3072]{1,0:T(8,128)(2,1)S(1)}, u32[]{:S(2)}, u32[]{:S(2)}) collective-permute-start(bf16[256,3072]{1,0:T(8,128)(2,1)S(1)} %collective-permute-done.22.refs_1_), channel_id=1, source_target_pairs={{0,1},{1,0},{2,3},{3,2},{4,5},{5,4},{6,7},{7,6}} | collective-permute-start | bytes 4718600 | tf_op jit(solution)/shard_map/ppermute | solution.py:219
  423.6 3.4 collective-permute-start.43
  423.6 23.4 %collective-permute-start.20 = (bf16[256,3072]{1,0:T(8,128)(2,1)S(1)}, bf16[256,3072]{1,0:T(8,128)(2,1)S(1)}, u32[]{:S(2)}, u32[]{:S(2)}) collective-permute-start(bf16[256,3072]{1,0:T(8,128)(2,1)S(1)} %collective-permute-done.19.refs_1_), channel_id=1, source_target_pairs={{0,1},{1,0},{2,3},{3,2},{4,5},{5,4},{6,7},{7,6}} | collective-permute-start | bytes 4718600 | tf_op jit(solution)/shard_map/ppermute | solution.py:219
  424.1 25.1 %collective-permute-start.28 = (bf16[96,1024]{1,0:T(8,128)(2,1)}, bf16[96,1024]{1,0:T(8,128)(2,1)S(1)}, u32[]{:S(2)}, u32[]{:S(2)}) collective-permute-start(bf16[96,1024]{1,0:T(8,128)(2,1)} %get-tuple-element.120), channel_id=1, source_target_pairs={{0,1},{1,0},{2,3},{3,2},{4,5},{5,4},{6,7},{7,6}} | collective-permute-start | bytes 589832 | tf_op jit(solution)/shard_map/ppermute | solution.py:219
  424.2 25.1 %collective-permute-start.30 = (bf16[96,1024]{1,0:T(8,128)(2,1)}, bf16[96,1024]{1,0:T(8,128)(2,1)S(1)}, u32[]{:S(2)}, u32[]{:S(2)}) collective-permute-start(bf16[96,1024]{1,0:T(8,128)(2,1)} %collective-permute-done.29.refs_1_), channel_id=1, source_target_pairs={{0,1},{1,0},{2,3},{3,2},{4,5},{5,4},{6,7},{7,6}} | collective-permute-start | bytes 589832 | tf_op jit(solution)/shard_map/ppermute | solution.py:219
  424.6 24.6 %collective-permute-start.32 = (bf16[48,1024]{1,0:T(8,128)(2,1)}, bf16[48,1024]{1,0:T(8,128)(2,1)S(1)}, u32[]{:S(2)}, u32[]{:S(2)}) collective-permute-start(bf16[48,1024]{1,0:T(8,128)(2,1)} %get-tuple-element.126), channel_id=1, source_target_pairs={{0,1},{1,0},{2,3},{3,2},{4,5},{5,4},{6,7},{7,6}} | collective-permute-start | bytes 294920 | tf_op jit(solution)/shard_map/ppermute | solution.py:219
  427.0 22.2 %collective-permute-start.34 = (bf16[48,1024]{1,0:T(8,128)(2,1)S(1)}, bf16[48,1024]{1,0:T(8,128)(2,1)S(1)}, u32[]{:S(2)}, u32[]{:S(2)}) collective-permute-start(bf16[48,1024]{1,0:T(8,128)(2,1)S(1)} %collective-permute-done.33.refs_4_), channel_id=1, source_target_pairs={{0,1},{1,0},{2,3},{3,2},{4,5},{5,4},{6,7},{7,6}} | collective-permute-start | bytes 294920 | tf_op jit(solution)/shard_map/ppermute | solution.py:219
  427.2 1.0 copy-start.11
  428.1 1.0 copy-start.13
  429.1 1.3 copy-start.3
  429.1 1.5 copy-start.5
  429.1 1.6 copy-start.7
  430.7 1.7 copy-start.1
  (1 other events, 0.7 us)

commit v4 on v3

--- a/solution.py
+++ b/solution.py
@@ -35,7 +35,7 @@
         size = terms[which].shape[2] // 4
         return terms[which].at[0, layer, pl.ds(pl.multiple_of(owner * size + first, 16), rows)]
 
-    tile = pair_tile(rows, terms[which].shape[3])
+    tile = rows
     count = rows // tile
     owns = [
         pltpu.make_async_copy(block(which, layer, first + t * tile, tile, me ^ 2), mine.at[pl.ds(t * tile, tile)], in_sem.at[t])
@@ -109,15 +109,11 @@
     )(terms[which])
 
 
-def pair_tile(rows, cols):
-    return math.gcd(rows, 64 * 3072 // cols)
-
-
 def pair(terms, index, nears):
     chunk = CHUNKS[index]
     which, _, _, rows = chunk
     cols = terms[which].shape[3]
-    count = rows // pair_tile(rows, cols)
+    count = rows // rows
     anywhere = pl.BlockSpec(memory_space=pl.ANY)
     shapes = [(rows, cols)] + [(CHUNKS[c][3], terms[CHUNKS[c][0]].shape[3]) for c in nears]
     return pl.pallas_call(
@@ -150,7 +146,7 @@
 
 def adamw(me, terms, near, far, w, m, v, layer, first, rows, before):
     block, cols = m.shape[1], m.shape[2]
-    tile = math.gcd(rows, first, block, 64 * 3072 // cols)
+    tile = math.gcd(rows, first, block, 128 * 3072 // cols)
     at, per = first // tile, block // tile
     mine = pl.BlockSpec((1, tile, cols), lambda i, me: (layer, at + i, 0))
     whole = pl.BlockSpec((1, tile, cols), lambda i, me: (layer, me[0] * per + at + i, 0))

time: 452 us -> 450 us (level)
  transfers between devices with their start and end apart: 44 -> 44, of which waited for: 11 -> 12; matrix products, arithmetic and copies ran while one was open for 0% -> 0% of each run, Pallas kernels for 29% -> 29%
where the time goes in v4:
time: 450 us; the launch traced here: 449 us
  waiting for transfers between devices  281 us (62%)
  Pallas kernels  133 us (30%)
  starting transfers between devices  29.4 us (7%)
  local copies, waits for them, and re-layouts  5.41 us (1%)
    ppermute x44, waiting for transfers between devices, send(): return lax.ppermute(x, 'dp', to)  281 us
    pallas_call x11, Pallas kernels, adamw(): pl.pallas_call(functools.partial(adamw_body, n_alias), grid_spec=pltpu.Pr...  65.1 us
    pallas_call x10, Pallas kernels, pair(): pl.pallas_call(functools.partial(pair_body, chunk, nears), in_specs=[anyw...  44.4 us
    ppermute x44, starting transfers between devices, send(): return lax.ppermute(x, 'dp', to)  29.4 us
    pallas_call x10, Pallas kernels, place(): pl.pallas_call(functools.partial(place_body, chunks, block), in_specs=[pl...  20.7 us
  transfers between devices with their start and end apart: 44, of which 12 were waited for; matrix products, arithmetic and copies ran while one was open for 0% of the time, Pallas kernels for 29%

profile of v4, /device:TPU:0, one launch (start us, length us, event | category | flops | bytes accessed | tf_op | source)
XLA Modules:
  0.0 449.1 jit_solution(406746255338218453)
XLA Ops:
  0.6 2.3 first_pair.1
  2.9 2.9 collective-permute-start.3
  5.9 3.0 pair.12
  9.0 2.2 pair.19
  11.2 2.0 collective-permute-start.31
  13.2 3.0 pair.16
  16.3 5.0 %pair.11 = (bf16[128,3072]{1,0:T(8,128)(2,1)}, bf16[48,3072]{1,0:T(8,128)(2,1)}, bf16[80,3072]{1,0:T(8,128)(2,1)}, bf16[128,3072]{1,0:T(8,128)(2,1)}) custom-call(bf16[1,2,1024,3072]{3,2,1,0:T(8,128)(2,1)} %refs_0_.19, bf16[1,2,1024,3072]{3,2,1,0:T(8,128)(2,1)} %refs_1_.19, bf16[1,2,3072,1024]{3,2,1,0:T(8,128)(2,1)} %own.21), custom_call_target="tpu_custom_call" | custom-call | flops 393216 | bytes 3932160 | tf_op jit(solution)/shard_map/pair/pallas_call | solution.py:119
  21.3 2.0 collective-permute-start.1
  23.3 3.8 pair.17
  27.1 1.3 collective-permute-start.26
  28.4 2.5 pair.15
  30.9 0.8 collective-permute-start.24
  31.7 6.1 %pair.18 = (bf16[768,1024]{1,0:T(8,128)(2,1)}, bf16[768,1024]{1,0:T(8,128)(2,1)}) custom-call(bf16[1,2,1024,3072]{3,2,1,0:T(8,128)(2,1)} %refs_0_.19, bf16[1,2,1024,3072]{3,2,1,0:T(8,128)(2,1)} %refs_1_.19, bf16[1,2,3072,1024]{3,2,1,0:T(8,128)(2,1)} %own.21), custom_call_target="tpu_custom_call" | custom-call | flops 786432 | bytes 7864320 | tf_op jit(solution)/shard_map/pair/pallas_call | solution.py:119
  37.8 4.0 adamw.11
  41.7 32.5 %collective-permute-done.24.far = bf16[96,1024]{1,0:T(8,128)(2,1)S(1)} collective-permute-done((bf16[96,1024]{1,0:T(8,128)(2,1)}, bf16[96,1024]{1,0:T(8,128)(2,1)S(1)}, u32[]{:S(2)}, u32[]{:S(2)}) %collective-permute-start.24) | collective-permute-done | bytes 196640 | tf_op jit(solution)/shard_map/ppermute | solution.py:215
  74.2 1.7 collective-permute-start.27
  76.0 0.8 copy-done.16
  77.0 5.7 %adamw.12 = (bf16[80,3072]{1,0:T(8,128)(2,1)}, bf16[2,1024,3072]{2,1,0:T(8,128)(2,1)}, f32[2,256,3072]{2,1,0:T(8,128)}, f32[2,256,3072]{2,1,0:T(8,128)}) custom-call(s32[1]{0:T(128)} %bitcast.me, bf16[1,2,1024,3072]{3,2,1,0:T(8,128)(2,1)} %refs_0_.19, ...), custom_call_target="tpu_custom_call", output_to_operand_aliasing={{1}: (7, {}), {2}: (8, {}), {3}: (9, {})} | custom-call | flops 3440640 | bytes 6881280 | tf_op jit(solution)/shard_map/adamw/pallas_call | solution.py:158
  82.7 0.7 copy-done.8
  83.5 6.8 %pair.10 = (bf16[256,3072]{1,0:T(8,128)(2,1)}, bf16[256,3072]{1,0:T(8,128)(2,1)}) custom-call(bf16[1,2,1024,3072]{3,2,1,0:T(8,128)(2,1)} %refs_0_.19, bf16[1,2,1024,3072]{3,2,1,0:T(8,128)(2,1)} %refs_1_.19, bf16[1,2,3072,1024]{3,2,1,0:T(8,128)(2,1)} %own.21), custom_call_target="tpu_custom_call" | custom-call | flops 786432 | bytes 7864320 | tf_op jit(solution)/shard_map/pair/pallas_call | solution.py:119
  90.2 26.3 %collective-permute-done.14.refs_1_ = bf16[48,3072]{1,0:T(8,128)(2,1)S(1)} collective-permute-done((bf16[48,3072]{1,0:T(8,128)(2,1)}, bf16[48,3072]{1,0:T(8,128)(2,1)S(1)}, u32[]{:S(2)}, u32[]{:S(2)}) %collective-permute-start.14) | collective-permute-done | bytes 294944 | tf_op jit(solution)/shard_map/ppermute | solution.py:215
  116.5 1.5 collective-permute-start
  118.6 6.1 %pair.13 = (bf16[256,3072]{1,0:T(8,128)(2,1)}, bf16[256,3072]{1,0:T(8,128)(2,1)}) custom-call(bf16[1,2,1024,3072]{3,2,1,0:T(8,128)(2,1)} %refs_0_.19, bf16[1,2,1024,3072]{3,2,1,0:T(8,128)(2,1)} %refs_1_.19, bf16[1,2,3072,1024]{3,2,1,0:T(8,128)(2,1)} %own.21), custom_call_target="tpu_custom_call" | custom-call | flops 786432 | bytes 7864320 | tf_op jit(solution)/shard_map/pair/pallas_call | solution.py:119
  124.7 6.1 %pair.14 = (bf16[256,3072]{1,0:T(8,128)(2,1)}, bf16[256,3072]{1,0:T(8,128)(2,1)}) custom-call(bf16[1,2,1024,3072]{3,2,1,0:T(8,128)(2,1)} %refs_0_.19, bf16[1,2,1024,3072]{3,2,1,0:T(8,128)(2,1)} %refs_1_.19, bf16[1,2,3072,1024]{3,2,1,0:T(8,128)(2,1)} %own.21), custom_call_target="tpu_custom_call" | custom-call | flops 786432 | bytes 7864320 | tf_op jit(solution)/shard_map/pair/pallas_call | solution.py:119
  130.8 0.7 copy-done.12
  131.5 1.5 collective-permute-start.16
  133.5 31.1 %collective-permute-done.11.refs_1_ = bf16[80,3072]{1,0:T(8,128)(2,1)S(1)} collective-permute-done((bf16[80,3072]{1,0:T(8,128)(2,1)}, bf16[80,3072]{1,0:T(8,128)(2,1)S(1)}, u32[]{:S(2)}, u32[]{:S(2)}) %collective-permute-start.11) | collective-permute-done | bytes 491552 | tf_op jit(solution)/shard_map/ppermute | solution.py:215
  164.6 6.3 %adamw.13 = (bf16[128,3072]{1,0:T(8,128)(2,1)}, bf16[2,1024,3072]{2,1,0:T(8,128)(2,1)}, f32[2,256,3072]{2,1,0:T(8,128)}, f32[2,256,3072]{2,1,0:T(8,128)}) custom-call(s32[1]{0:T(128)} %bitcast.me, bf16[1,2,1024,3072]{3,2,1,0:T(8,128)(2,1)} %refs_0_.19, ...), custom_call_target="tpu_custom_call", output_to_operand_aliasing={{1}: (7, {}), {2}: (8, {}), {3}: (9, {})} | custom-call | flops 5505024 | bytes 11010048 | tf_op jit(solution)/shard_map/adamw/pallas_call | solution.py:158
  171.3 1.4 collective-permute-start.8
  172.8 8.2 %adamw.17 = (bf16[768,1024]{1,0:T(8,128)(2,1)}, bf16[2,3072,1024]{2,1,0:T(8,128)(2,1)}, f32[2,768,1024]{2,1,0:T(8,128)}, f32[2,768,1024]{2,1,0:T(8,128)}) custom-call(s32[1]{0:T(128)} %bitcast.me, bf16[1,2,3072,1024]{3,2,1,0:T(8,128)(2,1)} %own.21, bf16[768,1024]{1,0:T(8,128)(2,1)} %get-tuple-element.109.near, bf16[768,1024]{1,0:T(8,128)(2,1)} %copy-done.14, ...), custom_call_target="tpu_custom_call" | custom-call | flops 11010048 | bytes 22020096 | tf_op jit(solution)/shard_map/adamw/pallas_call | solution.py:158
  180.9 6.1 %adamw.18 = (bf16[384,1024]{1,0:T(8,128)(2,1)}, bf16[2,3072,1024]{2,1,0:T(8,128)(2,1)}, f32[2,768,1024]{2,1,0:T(8,128)}, f32[2,768,1024]{2,1,0:T(8,128)}) custom-call(s32[1]{0:T(128)} %bitcast.me, bf16[1,2,3072,1024]{3,2,1,0:T(8,128)(2,1)} %own.21, ...), custom_call_target="tpu_custom_call", output_to_operand_aliasing={{1}: (7, {}), {2}: (8, {}), {3}: (9, {})} | custom-call | flops 5505024 | bytes 11010048 | tf_op jit(solution)/shard_map/adamw/pallas_call | solution.py:158
  187.1 5.7 %adamw.19 = (bf16[240,1024]{1,0:T(8,128)(2,1)}, bf16[2,3072,1024]{2,1,0:T(8,128)(2,1)}, f32[2,768,1024]{2,1,0:T(8,128)}, f32[2,768,1024]{2,1,0:T(8,128)}) custom-call(s32[1]{0:T(128)} %bitcast.me, bf16[1,2,3072,1024]{3,2,1,0:T(8,128)(2,1)} %own.21, ...), custom_call_target="tpu_custom_call", output_to_operand_aliasing={{1}: (7, {}), {2}: (8, {}), {3}: (9, {})} | custom-call | flops 3440640 | bytes 6881280 | tf_op jit(solution)/shard_map/adamw/pallas_call | solution.py:158
  192.8 2.5 adamw.20
  195.3 2.2 adamw.21
  197.4 1.3 collective-permute-start.33
  198.7 8.2 %adamw.14 = (bf16[256,3072]{1,0:T(8,128)(2,1)}, bf16[2,1024,3072]{2,1,0:T(8,128)(2,1)}, f32[2,256,3072]{2,1,0:T(8,128)}, f32[2,256,3072]{2,1,0:T(8,128)}) custom-call(s32[1]{0:T(128)} %bitcast.me, bf16[1,2,1024,3072]{3,2,1,0:T(8,128)(2,1)} %refs_0_.19, ...), custom_call_target="tpu_custom_call", output_to_operand_aliasing={{1}: (7, {}), {2}: (8, {}), {3}: (9, {})} | custom-call | flops 11010048 | bytes 22020096 | tf_op jit(solution)/shard_map/adamw/pallas_call | solution.py:158
  206.9 42.0 %collective-permute-done.8.refs_1_ = bf16[128,3072]{1,0:T(8,128)(2,1)} collective-permute-done((bf16[128,3072]{1,0:T(8,128)(2,1)}, bf16[128,3072]{1,0:T(8,128)(2,1)}, u32[]{:S(2)}, u32[]{:S(2)}) %collective-permute-start.8) | collective-permute-done | bytes 786464 | tf_op jit(solution)/shard_map/ppermute | solution.py:215
  249.0 1.5 collective-permute-start.29
  250.4 0.6 collective-permute-start.5
  251.2 5.0 %collective-permute-done.29.refs_1_ = bf16[96,1024]{1,0:T(8,128)(2,1)} collective-permute-done((bf16[96,1024]{1,0:T(8,128)(2,1)S(1)}, bf16[96,1024]{1,0:T(8,128)(2,1)}, u32[]{:S(2)}, u32[]{:S(2)}) %collective-permute-start.29) | collective-permute-done | bytes 196640 | tf_op jit(solution)/shard_map/ppermute | solution.py:215
  256.2 2.1 collective-permute-start.36
  258.3 41.0 %collective-permute-done.36.refs_1_ = bf16[240,1024]{1,0:T(8,128)(2,1)} collective-permute-done((bf16[240,1024]{1,0:T(8,128)(2,1)}, bf16[240,1024]{1,0:T(8,128)(2,1)}, u32[]{:S(2)}, u32[]{:S(2)}) %collective-permute-start.36) | collective-permute-done | bytes 491552 | tf_op jit(solution)/shard_map/ppermute | solution.py:215
  299.2 1.5 collective-permute-start.39
  300.7 8.1 %adamw.15 = (bf16[256,3072]{1,0:T(8,128)(2,1)}, bf16[2,1024,3072]{2,1,0:T(8,128)(2,1)}, f32[2,256,3072]{2,1,0:T(8,128)}, f32[2,256,3072]{2,1,0:T(8,128)}) custom-call(s32[1]{0:T(128)} %bitcast.me, bf16[1,2,1024,3072]{3,2,1,0:T(8,128)(2,1)} %refs_1_.19, bf16[256,3072]{1,0:T(8,128)(2,1)} %get-tuple-element.95.near, ...), custom_call_target="tpu_custom_call" | custom-call | flops 11010048 | bytes 22020096 | tf_op jit(solution)/shard_map/adamw/pallas_call | solution.py:158
  308.9 8.2 %adamw.16 = (bf16[256,3072]{1,0:T(8,128)(2,1)}, bf16[2,1024,3072]{2,1,0:T(8,128)(2,1)}, f32[2,256,3072]{2,1,0:T(8,128)}, f32[2,256,3072]{2,1,0:T(8,128)}) custom-call(s32[1]{0:T(128)} %bitcast.me, bf16[1,2,1024,3072]{3,2,1,0:T(8,128)(2,1)} %refs_1_.19, ...), custom_call_target="tpu_custom_call", output_to_operand_aliasing={{1}: (7, {}), {2}: (8, {}), {3}: (9, {})} | custom-call | flops 11010048 | bytes 22020096 | tf_op jit(solution)/shard_map/adamw/pallas_call | solution.py:158
  318.0 0.8 collective-permute-start.19
  318.8 2.7 collective-permute-done.37.refs_2_
  322.1 1.5 collective-permute-start.42
  323.6 31.8 %collective-permute-done.19.refs_1_ = bf16[256,3072]{1,0:T(8,128)(2,1)S(1)} collective-permute-done((bf16[256,3072]{1,0:T(8,128)(2,1)}, bf16[256,3072]{1,0:T(8,128)(2,1)S(1)}, u32[]{:S(2)}, u32[]{:S(2)}) %collective-permute-start.19) | collective-permute-done | bytes 1572896 | tf_op jit(solution)/shard_map/ppermute | solution.py:215
  355.9 33.2 %collective-permute-done.22.refs_1_ = bf16[256,3072]{1,0:T(8,128)(2,1)S(1)} collective-permute-done((bf16[256,3072]{1,0:T(8,128)(2,1)}, bf16[256,3072]{1,0:T(8,128)(2,1)S(1)}, u32[]{:S(2)}, u32[]{:S(2)}) %collective-permute-start.22) | collective-permute-done | bytes 1572896 | tf_op jit(solution)/shard_map/ppermute | solution.py:215
  389.1 32.4 %collective-permute-done.42.refs_1_ = bf16[768,1024]{1,0:T(8,128)(2,1)S(1)} collective-permute-done((bf16[768,1024]{1,0:T(8,128)(2,1)}, bf16[768,1024]{1,0:T(8,128)(2,1)S(1)}, u32[]{:S(2)}, u32[]{:S(2)}) %collective-permute-start.42) | collective-permute-done | bytes 1572896 | tf_op jit(solution)/shard_map/ppermute | solution.py:215
  422.6 2.3 collective-permute-done.43.refs_2_
  425.1 1.0 copy-done.11
  426.1 1.0 copy-done.13
  427.1 0.9 place.10.refs_3_
  428.7 1.1 place.11.refs_3_
  430.4 2.8 place.12.refs_3_
  433.2 2.2 place.16.refs_3_
  435.4 2.8 place.17.refs_3_
  438.2 2.3 place.18.refs_6_
  440.5 2.2 place.13
  442.7 2.2 place.14.refs_3_
  445.0 2.2 place.15
  447.2 1.9 place.19
  (98 shorter events, 6.8 us)
Async XLA Ops:
  2.9 27.9 %collective-permute-start.3 = (bf16[48,3072]{1,0:T(8,128)(2,1)S(1)}, bf16[48,3072]{1,0:T(8,128)(2,1)S(1)}, u32[]{:S(2)}, u32[]{:S(2)}) collective-permute-start(bf16[48,3072]{1,0:T(8,128)(2,1)S(1)} %first_pair.1), channel_id=1, source_target_pairs={{0,2},{2,0},{1,3},{3,1},{4,6},{6,4},{5,7},{7,5}} | collective-permute-start | bytes 884744 | tf_op jit(solution)/shard_map/ppermute | solution.py:215
  8.9 67.0 %collective-permute-start.2 = (bf16[80,3072]{1,0:T(8,128)(2,1)}, bf16[80,3072]{1,0:T(8,128)(2,1)S(1)}, u32[]{:S(2)}, u32[]{:S(2)}) collective-permute-start(bf16[80,3072]{1,0:T(8,128)(2,1)} %pair.12), channel_id=1, source_target_pairs={{0,2},{2,0},{1,3},{3,1},{4,6},{6,4},{5,7},{7,5}} | collective-permute-start | bytes 1474568 | tf_op jit(solution)/shard_map/ppermute | solution.py:215
  11.2 15.9 %collective-permute-start.31 = (bf16[48,1024]{1,0:T(8,128)(2,1)}, bf16[48,1024]{1,0:T(8,128)(2,1)S(1)}, u32[]{:S(2)}, u32[]{:S(2)}) collective-permute-start(bf16[48,1024]{1,0:T(8,128)(2,1)} %get-tuple-element.122), channel_id=1, source_target_pairs={{0,2},{2,0},{1,3},{3,1},{4,6},{6,4},{5,7},{7,5}} | collective-permute-start | bytes 294920 | tf_op jit(solution)/shard_map/ppermute | solution.py:215
  16.3 60.5 %collective-permute-start.25 = (bf16[240,1024]{1,0:T(8,128)(2,1)}, bf16[240,1024]{1,0:T(8,128)(2,1)S(1)}, u32[]{:S(2)}, u32[]{:S(2)}) collective-permute-start(bf16[240,1024]{1,0:T(8,128)(2,1)} %get-tuple-element.106), channel_id=1, source_target_pairs={{0,2},{2,0},{1,3},{3,1},{4,6},{6,4},{5,7},{7,5}} | collective-permute-start | bytes 1474568 | tf_op jit(solution)/shard_map/ppermute | solution.py:215
  21.3 95.3 %collective-permute-start.1 = (bf16[128,3072]{1,0:T(8,128)(2,1)}, bf16[128,3072]{1,0:T(8,128)(2,1)}, u32[]{:S(2)}, u32[]{:S(2)}) collective-permute-start(bf16[128,3072]{1,0:T(8,128)(2,1)} %get-tuple-element.76), channel_id=1, source_target_pairs={{0,2},{2,0},{1,3},{3,1},{4,6},{6,4},{5,7},{7,5}} | collective-permute-start | bytes 2359304 | tf_op jit(solution)/shard_map/ppermute | solution.py:215
  27.1 3.8 copy-start.19
  27.1 90.9 %collective-permute-start.26 = (bf16[384,1024]{1,0:T(8,128)(2,1)}, bf16[384,1024]{1,0:T(8,128)(2,1)}, u32[]{:S(2)}, u32[]{:S(2)}) collective-permute-start(bf16[384,1024]{1,0:T(8,128)(2,1)} %get-tuple-element.108), channel_id=1, source_target_pairs={{0,2},{2,0},{1,3},{3,1},{4,6},{6,4},{5,7},{7,5}} | collective-permute-start | bytes 2359304 | tf_op jit(solution)/shard_map/ppermute | solution.py:215
  30.9 6.9 %copy-start.17 = (bf16[48,3072]{1,0:T(8,128)(2,1)}, bf16[48,3072]{1,0:T(8,128)(2,1)S(1)}, u32[]{:S(2)}) copy-start(bf16[48,3072]{1,0:T(8,128)(2,1)S(1)} %collective-permute-done.3.far) | copy-start | bytes 884740
  30.9 43.3 %collective-permute-start.24 = (bf16[96,1024]{1,0:T(8,128)(2,1)}, bf16[96,1024]{1,0:T(8,128)(2,1)S(1)}, u32[]{:S(2)}, u32[]{:S(2)}) collective-permute-start(bf16[96,1024]{1,0:T(8,128)(2,1)} %get-tuple-element.104), channel_id=1, source_target_pairs={{0,2},{2,0},{1,3},{3,1},{4,6},{6,4},{5,7},{7,5}} | collective-permute-start | bytes 589832 | tf_op jit(solution)/shard_map/ppermute | solution.py:215
  74.2 8.5 %copy-start.18 = (bf16[96,1024]{1,0:T(8,128)(2,1)}, bf16[96,1024]{1,0:T(8,128)(2,1)S(1)}, u32[]{:S(2)}) copy-start(bf16[96,1024]{1,0:T(8,128)(2,1)S(1)} %collective-permute-done.24.far) | copy-start | bytes 589828
  74.2 97.1 %collective-permute-start.27 = (bf16[768,1024]{1,0:T(8,128)(2,1)}, bf16[768,1024]{1,0:T(8,128)(2,1)S(1)}, u32[]{:S(2)}, u32[]{:S(2)}) collective-permute-start(bf16[768,1024]{1,0:T(8,128)(2,1)} %get-tuple-element.110), channel_id=1, source_target_pairs={{0,2},{2,0},{1,3},{3,1},{4,6},{6,4},{5,7},{7,5}} | collective-permute-start | bytes 4718600 | tf_op jit(solution)/shard_map/ppermute | solution.py:215
  76.0 0.8 copy-start.16
  76.0 6.7 %collective-permute-start.13 = (bf16[48,3072]{1,0:T(8,128)(2,1)}, bf16[48,3072]{1,0:T(8,128)(2,1)S(1)}, u32[]{:S(2)}, u32[]{:S(2)}) collective-permute-start(bf16[48,3072]{1,0:T(8,128)(2,1)} %get-tuple-element.91), channel_id=1, source_target_pairs={{0,1},{1,0},{2,3},{3,2},{4,5},{5,4},{6,7},{7,6}} | collective-permute-start | bytes 884744 | tf_op jit(solution)/shard_map/ppermute | solution.py:215
  76.7 6.0 %copy-start.15 = (bf16[240,1024]{1,0:T(8,128)(2,1)}, bf16[240,1024]{1,0:T(8,128)(2,1)S(1)}, u32[]{:S(2)}) copy-start(bf16[240,1024]{1,0:T(8,128)(2,1)S(1)} %collective-permute-done.25.far) | copy-start | bytes 1474564
  76.7 39.8 %collective-permute-start.14 = (bf16[48,3072]{1,0:T(8,128)(2,1)}, bf16[48,3072]{1,0:T(8,128)(2,1)S(1)}, u32[]{:S(2)}, u32[]{:S(2)}) collective-permute-start(bf16[48,3072]{1,0:T(8,128)(2,1)} %get-tuple-element.91), channel_id=1, source_target_pairs={{0,2},{2,0},{1,3},{3,1},{4,6},{6,4},{5,7},{7,5}} | collective-permute-start | bytes 884744 | tf_op jit(solution)/shard_map/ppermute | solution.py:215
  82.7 0.7 copy-start.8
  83.5 49.5 %collective-permute-start.10 = (bf16[80,3072]{1,0:T(8,128)(2,1)}, bf16[80,3072]{1,0:T(8,128)(2,1)S(1)}, u32[]{:S(2)}, u32[]{:S(2)}) collective-permute-start(bf16[80,3072]{1,0:T(8,128)(2,1)} %get-tuple-element.90), channel_id=1, source_target_pairs={{0,1},{1,0},{2,3},{3,2},{4,5},{5,4},{6,7},{7,6}} | collective-permute-start | bytes 1474568 | tf_op jit(solution)/shard_map/ppermute | solution.py:215
  116.5 8.1 %copy-start.10 = (bf16[48,3072]{1,0:T(8,128)(2,1)}, bf16[48,3072]{1,0:T(8,128)(2,1)S(1)}, u32[]{:S(2)}) copy-start(bf16[48,3072]{1,0:T(8,128)(2,1)S(1)} %collective-permute-done.14.refs_1_) | copy-start | bytes 884740
  116.5 14.2 %collective-permute-start.15 = (bf16[48,3072]{1,0:T(8,128)(2,1)S(1)}, bf16[48,3072]{1,0:T(8,128)(2,1)S(1)}, u32[]{:S(2)}, u32[]{:S(2)}) collective-permute-start(bf16[48,3072]{1,0:T(8,128)(2,1)S(1)} %collective-permute-done.14.refs_1_), channel_id=1, source_target_pairs={{0,1},{1,0},{2,3},{3,2},{4,5},{5,4},{6,7},{7,6}} | collective-permute-start | bytes 884744 | tf_op jit(solution)/shard_map/ppermute | solution.py:215
  116.5 76.2 %collective-permute-start = (bf16[256,3072]{1,0:T(8,128)(2,1)}, bf16[256,3072]{1,0:T(8,128)(2,1)}, u32[]{:S(2)}, u32[]{:S(2)}) collective-permute-start(bf16[256,3072]{1,0:T(8,128)(2,1)} %get-tuple-element.74), channel_id=1, source_target_pairs={{0,2},{2,0},{1,3},{3,1},{4,6},{6,4},{5,7},{7,5}} | collective-permute-start | bytes 4718600 | tf_op jit(solution)/shard_map/ppermute | solution.py:215
  118.0 46.5 %collective-permute-start.11 = (bf16[80,3072]{1,0:T(8,128)(2,1)}, bf16[80,3072]{1,0:T(8,128)(2,1)S(1)}, u32[]{:S(2)}, u32[]{:S(2)}) collective-permute-start(bf16[80,3072]{1,0:T(8,128)(2,1)} %get-tuple-element.90), channel_id=1, source_target_pairs={{0,2},{2,0},{1,3},{3,1},{4,6},{6,4},{5,7},{7,5}} | collective-permute-start | bytes 1474568 | tf_op jit(solution)/shard_map/ppermute | solution.py:215
  131.5 118.9 %collective-permute-start.16 = (bf16[256,3072]{1,0:T(8,128)(2,1)}, bf16[256,3072]{1,0:T(8,128)(2,1)}, u32[]{:S(2)}, u32[]{:S(2)}) collective-permute-start(bf16[256,3072]{1,0:T(8,128)(2,1)} %get-tuple-element.94), channel_id=1, source_target_pairs={{0,2},{2,0},{1,3},{3,1},{4,6},{6,4},{5,7},{7,5}} | collective-permute-start | bytes 4718600 | tf_op jit(solution)/shard_map/ppermute | solution.py:215
  132.9 38.0 %copy-start.2 = (bf16[80,3072]{1,0:T(8,128)(2,1)}, bf16[80,3072]{1,0:T(8,128)(2,1)S(1)}, u32[]{:S(2)}) copy-start(bf16[80,3072]{1,0:T(8,128)(2,1)S(1)} %collective-permute-done.10.refs_0_) | copy-start | bytes 1474564
  132.9 117.5 %collective-permute-start.17 = (bf16[256,3072]{1,0:T(8,128)(2,1)}, bf16[256,3072]{1,0:T(8,128)(2,1)}, u32[]{:S(2)}, u32[]{:S(2)}) collective-permute-start(bf16[256,3072]{1,0:T(8,128)(2,1)} %get-tuple-element.96), channel_id=1, source_target_pairs={{0,2},{2,0},{1,3},{3,1},{4,6},{6,4},{5,7},{7,5}} | collective-permute-start | bytes 4718600 | tf_op jit(solution)/shard_map/ppermute | solution.py:215
  164.6 6.3 %copy-start.4 = (bf16[80,3072]{1,0:T(8,128)(2,1)}, bf16[80,3072]{1,0:T(8,128)(2,1)S(1)}, u32[]{:S(2)}) copy-start(bf16[80,3072]{1,0:T(8,128)(2,1)S(1)} %collective-permute-done.11.refs_1_) | copy-start | bytes 1474564
  164.6 6.3 %collective-permute-start.12 = (bf16[80,3072]{1,0:T(8,128)(2,1)S(1)}, bf16[80,3072]{1,0:T(8,128)(2,1)S(1)}, u32[]{:S(2)}, u32[]{:S(2)}) collective-permute-start(bf16[80,3072]{1,0:T(8,128)(2,1)S(1)} %collective-permute-done.11.refs_1_), channel_id=1, source_target_pairs={{0,1},{1,0},{2,3},{3,2},{4,5},{5,4},{6,7},{7,6}} | collective-permute-start | bytes 1474568 | tf_op jit(solution)/shard_map/ppermute | solution.py:215
  170.9 10.0 %copy-start.6 = (bf16[80,3072]{1,0:T(8,128)(2,1)}, bf16[80,3072]{1,0:T(8,128)(2,1)S(1)}, u32[]{:S(2)}) copy-start(bf16[80,3072]{1,0:T(8,128)(2,1)S(1)} %collective-permute-done.12.refs_2_) | copy-start | bytes 1474564
  170.9 26.5 %collective-permute-start.7 = (bf16[128,3072]{1,0:T(8,128)(2,1)}, bf16[128,3072]{1,0:T(8,128)(2,1)S(1)}, u32[]{:S(2)}, u32[]{:S(2)}) collective-permute-start(bf16[128,3072]{1,0:T(8,128)(2,1)} %get-tuple-element.89), channel_id=1, source_target_pairs={{0,1},{1,0},{2,3},{3,2},{4,5},{5,4},{6,7},{7,6}} | collective-permute-start | bytes 2359304 | tf_op jit(solution)/shard_map/ppermute | solution.py:215
  171.3 1.4 copy-start.14
  171.3 77.6 %collective-permute-start.8 = (bf16[128,3072]{1,0:T(8,128)(2,1)}, bf16[128,3072]{1,0:T(8,128)(2,1)}, u32[]{:S(2)}, u32[]{:S(2)}) collective-permute-start(bf16[128,3072]{1,0:T(8,128)(2,1)} %get-tuple-element.89), channel_id=1, source_target_pairs={{0,2},{2,0},{1,3},{3,1},{4,6},{6,4},{5,7},{7,5}} | collective-permute-start | bytes 2359304 | tf_op jit(solution)/shard_map/ppermute | solution.py:215
  192.8 65.5 %collective-permute-start.35 = (bf16[240,1024]{1,0:T(8,128)(2,1)}, bf16[240,1024]{1,0:T(8,128)(2,1)}, u32[]{:S(2)}, u32[]{:S(2)}) collective-permute-start(bf16[240,1024]{1,0:T(8,128)(2,1)} %get-tuple-element.127), channel_id=1, source_target_pairs={{0,1},{1,0},{2,3},{3,2},{4,5},{5,4},{6,7},{7,6}} | collective-permute-start | bytes 1474568 | tf_op jit(solution)/shard_map/ppermute | solution.py:215
  197.4 9.5 %copy-start = (bf16[128,3072]{1,0:T(8,128)(2,1)}, bf16[128,3072]{1,0:T(8,128)(2,1)S(1)}, u32[]{:S(2)}) copy-start(bf16[128,3072]{1,0:T(8,128)(2,1)S(1)} %collective-permute-done.7.refs_0_) | copy-start | bytes 2359300
  197.4 53.6 %collective-permute-start.33 = (bf16[48,1024]{1,0:T(8,128)(2,1)}, bf16[48,1024]{1,0:T(8,128)(2,1)S(1)}, u32[]{:S(2)}, u32[]{:S(2)}) collective-permute-start(bf16[48,1024]{1,0:T(8,128)(2,1)} %get-tuple-element.126), channel_id=1, source_target_pairs={{0,2},{2,0},{1,3},{3,1},{4,6},{6,4},{5,7},{7,5}} | collective-permute-start | bytes 294920 | tf_op jit(solution)/shard_map/ppermute | solution.py:215
  198.7 50.2 %copy-start.20 = (bf16[96,1024]{1,0:T(8,128)(2,1)S(1)}, bf16[96,1024]{1,0:T(8,128)(2,1)}, u32[]{:S(2)}) copy-start(bf16[96,1024]{1,0:T(8,128)(2,1)} %get-tuple-element.120) | copy-start | bytes 589828
  249.0 7.2 %collective-permute-start.29 = (bf16[96,1024]{1,0:T(8,128)(2,1)S(1)}, bf16[96,1024]{1,0:T(8,128)(2,1)}, u32[]{:S(2)}, u32[]{:S(2)}) collective-permute-start(bf16[96,1024]{1,0:T(8,128)(2,1)S(1)} %copy-done.20), channel_id=1, source_target_pairs={{0,2},{2,0},{1,3},{3,1},{4,6},{6,4},{5,7},{7,5}} | collective-permute-start | bytes 589832 | tf_op jit(solution)/shard_map/ppermute | solution.py:215
  250.4 71.2 %collective-permute-start.4 = (bf16[256,3072]{1,0:T(8,128)(2,1)}, bf16[256,3072]{1,0:T(8,128)(2,1)S(1)}, u32[]{:S(2)}, u32[]{:S(2)}) collective-permute-start(bf16[256,3072]{1,0:T(8,128)(2,1)} %get-tuple-element.88), channel_id=1, source_target_pairs={{0,1},{1,0},{2,3},{3,2},{4,5},{5,4},{6,7},{7,6}} | collective-permute-start | bytes 4718600 | tf_op jit(solution)/shard_map/ppermute | solution.py:215
  250.4 71.7 %collective-permute-start.5 = (bf16[256,3072]{1,0:T(8,128)(2,1)}, bf16[256,3072]{1,0:T(8,128)(2,1)S(1)}, u32[]{:S(2)}, u32[]{:S(2)}) collective-permute-start(bf16[256,3072]{1,0:T(8,128)(2,1)} %get-tuple-element.88), channel_id=1, source_target_pairs={{0,2},{2,0},{1,3},{3,1},{4,6},{6,4},{5,7},{7,5}} | collective-permute-start | bytes 4718600 | tf_op jit(solution)/shard_map/ppermute | solution.py:215
  251.0 66.1 %collective-permute-start.9 = (bf16[128,3072]{1,0:T(8,128)(2,1)}, bf16[128,3072]{1,0:T(8,128)(2,1)}, u32[]{:S(2)}, u32[]{:S(2)}) collective-permute-start(bf16[128,3072]{1,0:T(8,128)(2,1)} %collective-permute-done.8.refs_1_), channel_id=1, source_target_pairs={{0,1},{1,0},{2,3},{3,2},{4,5},{5,4},{6,7},{7,6}} | collective-permute-start | bytes 2359304 | tf_op jit(solution)/shard_map/ppermute | solution.py:215
  256.2 43.1 %collective-permute-start.36 = (bf16[240,1024]{1,0:T(8,128)(2,1)}, bf16[240,1024]{1,0:T(8,128)(2,1)}, u32[]{:S(2)}, u32[]{:S(2)}) collective-permute-start(bf16[240,1024]{1,0:T(8,128)(2,1)} %get-tuple-element.127), channel_id=1, source_target_pairs={{0,2},{2,0},{1,3},{3,1},{4,6},{6,4},{5,7},{7,5}} | collective-permute-start | bytes 1474568 | tf_op jit(solution)/shard_map/ppermute | solution.py:215
  258.3 58.8 %collective-permute-start.38 = (bf16[384,1024]{1,0:T(8,128)(2,1)}, bf16[384,1024]{1,0:T(8,128)(2,1)}, u32[]{:S(2)}, u32[]{:S(2)}) collective-permute-start(bf16[384,1024]{1,0:T(8,128)(2,1)} %get-tuple-element.128), channel_id=1, source_target_pairs={{0,1},{1,0},{2,3},{3,2},{4,5},{5,4},{6,7},{7,6}} | collective-permute-start | bytes 2359304 | tf_op jit(solution)/shard_map/ppermute | solution.py:215
  299.2 18.7 %collective-permute-start.39 = (bf16[384,1024]{1,0:T(8,128)(2,1)}, bf16[384,1024]{1,0:T(8,128)(2,1)}, u32[]{:S(2)}, u32[]{:S(2)}) collective-permute-start(bf16[384,1024]{1,0:T(8,128)(2,1)} %get-tuple-element.128), channel_id=1, source_target_pairs={{0,2},{2,0},{1,3},{3,1},{4,6},{6,4},{5,7},{7,5}} | collective-permute-start | bytes 2359304 | tf_op jit(solution)/shard_map/ppermute | solution.py:215
  308.9 116.3 %copy-start.9 = (bf16[48,3072]{1,0:T(8,128)(2,1)S(1)}, bf16[48,3072]{1,0:T(8,128)(2,1)}, u32[]{:S(2)}) copy-start(bf16[48,3072]{1,0:T(8,128)(2,1)} %copy-done.8) | copy-start | bytes 884740
  317.1 6.5 %collective-permute-start.18 = (bf16[256,3072]{1,0:T(8,128)(2,1)}, bf16[256,3072]{1,0:T(8,128)(2,1)S(1)}, u32[]{:S(2)}, u32[]{:S(2)}) collective-permute-start(bf16[256,3072]{1,0:T(8,128)(2,1)} %get-tuple-element.100), channel_id=1, source_target_pairs={{0,1},{1,0},{2,3},{3,2},{4,5},{5,4},{6,7},{7,6}} | collective-permute-start | bytes 4718600 | tf_op jit(solution)/shard_map/ppermute | solution.py:215
  317.1 4.3 collective-permute-start.37
  318.0 37.5 %collective-permute-start.19 = (bf16[256,3072]{1,0:T(8,128)(2,1)}, bf16[256,3072]{1,0:T(8,128)(2,1)S(1)}, u32[]{:S(2)}, u32[]{:S(2)}) collective-permute-start(bf16[256,3072]{1,0:T(8,128)(2,1)} %get-tuple-element.100), channel_id=1, source_target_pairs={{0,2},{2,0},{1,3},{3,1},{4,6},{6,4},{5,7},{7,5}} | collective-permute-start | bytes 4718600 | tf_op jit(solution)/shard_map/ppermute | solution.py:215
  321.4 34.0 %collective-permute-start.21 = (bf16[256,3072]{1,0:T(8,128)(2,1)}, bf16[256,3072]{1,0:T(8,128)(2,1)S(1)}, u32[]{:S(2)}, u32[]{:S(2)}) collective-permute-start(bf16[256,3072]{1,0:T(8,128)(2,1)} %get-tuple-element.101), channel_id=1, source_target_pairs={{0,1},{1,0},{2,3},{3,2},{4,5},{5,4},{6,7},{7,6}} | collective-permute-start | bytes 4718600 | tf_op jit(solution)/shard_map/ppermute | solution.py:215
  321.6 67.6 %collective-permute-start.22 = (bf16[256,3072]{1,0:T(8,128)(2,1)}, bf16[256,3072]{1,0:T(8,128)(2,1)S(1)}, u32[]{:S(2)}, u32[]{:S(2)}) collective-permute-start(bf16[256,3072]{1,0:T(8,128)(2,1)} %get-tuple-element.101), channel_id=1, source_target_pairs={{0,2},{2,0},{1,3},{3,1},{4,6},{6,4},{5,7},{7,5}} | collective-permute-start | bytes 4718600 | tf_op jit(solution)/shard_map/ppermute | solution.py:215
  322.1 99.4 %collective-permute-start.42 = (bf16[768,1024]{1,0:T(8,128)(2,1)}, bf16[768,1024]{1,0:T(8,128)(2,1)S(1)}, u32[]{:S(2)}, u32[]{:S(2)}) collective-permute-start(bf16[768,1024]{1,0:T(8,128)(2,1)} %get-tuple-element.129), channel_id=1, source_target_pairs={{0,2},{2,0},{1,3},{3,1},{4,6},{6,4},{5,7},{7,5}} | collective-permute-start | bytes 4718600 | tf_op jit(solution)/shard_map/ppermute | solution.py:215
  323.6 98.0 %collective-permute-start.40 = (bf16[384,1024]{1,0:T(8,128)(2,1)}, bf16[384,1024]{1,0:T(8,128)(2,1)S(1)}, u32[]{:S(2)}, u32[]{:S(2)}) collective-permute-start(bf16[384,1024]{1,0:T(8,128)(2,1)} %collective-permute-done.39.refs_1_), channel_id=1, source_target_pairs={{0,1},{1,0},{2,3},{3,2},{4,5},{5,4},{6,7},{7,6}} | collective-permute-start | bytes 2359304 | tf_op jit(solution)/shard_map/ppermute | solution.py:215
  355.4 66.7 %collective-permute-start.41 = (bf16[768,1024]{1,0:T(8,128)(2,1)}, bf16[768,1024]{1,0:T(8,128)(2,1)S(1)}, u32[]{:S(2)}, u32[]{:S(2)}) collective-permute-start(bf16[768,1024]{1,0:T(8,128)(2,1)} %get-tuple-element.129), channel_id=1, source_target_pairs={{0,1},{1,0},{2,3},{3,2},{4,5},{5,4},{6,7},{7,6}} | collective-permute-start | bytes 4718600 | tf_op jit(solution)/shard_map/ppermute | solution.py:215
  355.4 66.7 %collective-permute-start.6 = (bf16[256,3072]{1,0:T(8,128)(2,1)S(1)}, bf16[256,3072]{1,0:T(8,128)(2,1)S(1)}, u32[]{:S(2)}, u32[]{:S(2)}) collective-permute-start(bf16[256,3072]{1,0:T(8,128)(2,1)S(1)} %collective-permute-done.5.refs_1_), channel_id=1, source_target_pairs={{0,1},{1,0},{2,3},{3,2},{4,5},{5,4},{6,7},{7,6}} | collective-permute-start | bytes 4718600 | tf_op jit(solution)/shard_map/ppermute | solution.py:215
  389.1 33.5 %collective-permute-start.23 = (bf16[256,3072]{1,0:T(8,128)(2,1)S(1)}, bf16[256,3072]{1,0:T(8,128)(2,1)S(1)}, u32[]{:S(2)}, u32[]{:S(2)}) collective-permute-start(bf16[256,3072]{1,0:T(8,128)(2,1)S(1)} %collective-permute-done.22.refs_1_), channel_id=1, source_target_pairs={{0,1},{1,0},{2,3},{3,2},{4,5},{5,4},{6,7},{7,6}} | collective-permute-start | bytes 4718600 | tf_op jit(solution)/shard_map/ppermute | solution.py:215
  421.6 3.4 collective-permute-start.43
  421.6 23.4 %collective-permute-start.20 = (bf16[256,3072]{1,0:T(8,128)(2,1)S(1)}, bf16[256,3072]{1,0:T(8,128)(2,1)S(1)}, u32[]{:S(2)}, u32[]{:S(2)}) collective-permute-start(bf16[256,3072]{1,0:T(8,128)(2,1)S(1)} %collective-permute-done.19.refs_1_), channel_id=1, source_target_pairs={{0,1},{1,0},{2,3},{3,2},{4,5},{5,4},{6,7},{7,6}} | collective-permute-start | bytes 4718600 | tf_op jit(solution)/shard_map/ppermute | solution.py:215
  422.1 25.1 %collective-permute-start.28 = (bf16[96,1024]{1,0:T(8,128)(2,1)}, bf16[96,1024]{1,0:T(8,128)(2,1)S(1)}, u32[]{:S(2)}, u32[]{:S(2)}) collective-permute-start(bf16[96,1024]{1,0:T(8,128)(2,1)} %get-tuple-element.120), channel_id=1, source_target_pairs={{0,1},{1,0},{2,3},{3,2},{4,5},{5,4},{6,7},{7,6}} | collective-permute-start | bytes 589832 | tf_op jit(solution)/shard_map/ppermute | solution.py:215
  422.1 25.1 %collective-permute-start.30 = (bf16[96,1024]{1,0:T(8,128)(2,1)}, bf16[96,1024]{1,0:T(8,128)(2,1)S(1)}, u32[]{:S(2)}, u32[]{:S(2)}) collective-permute-start(bf16[96,1024]{1,0:T(8,128)(2,1)} %collective-permute-done.29.refs_1_), channel_id=1, source_target_pairs={{0,1},{1,0},{2,3},{3,2},{4,5},{5,4},{6,7},{7,6}} | collective-permute-start | bytes 589832 | tf_op jit(solution)/shard_map/ppermute | solution.py:215
  422.6 24.6 %collective-permute-start.32 = (bf16[48,1024]{1,0:T(8,128)(2,1)}, bf16[48,1024]{1,0:T(8,128)(2,1)S(1)}, u32[]{:S(2)}, u32[]{:S(2)}) collective-permute-start(bf16[48,1024]{1,0:T(8,128)(2,1)} %get-tuple-element.126), channel_id=1, source_target_pairs={{0,1},{1,0},{2,3},{3,2},{4,5},{5,4},{6,7},{7,6}} | collective-permute-start | bytes 294920 | tf_op jit(solution)/shard_map/ppermute | solution.py:215
  425.0 22.2 %collective-permute-start.34 = (bf16[48,1024]{1,0:T(8,128)(2,1)S(1)}, bf16[48,1024]{1,0:T(8,128)(2,1)S(1)}, u32[]{:S(2)}, u32[]{:S(2)}) collective-permute-start(bf16[48,1024]{1,0:T(8,128)(2,1)S(1)} %collective-permute-done.33.refs_4_), channel_id=1, source_target_pairs={{0,1},{1,0},{2,3},{3,2},{4,5},{5,4},{6,7},{7,6}} | collective-permute-start | bytes 294920 | tf_op jit(solution)/shard_map/ppermute | solution.py:215
  425.1 1.0 copy-start.11
  426.1 1.0 copy-start.13
  427.1 1.3 copy-start.3
  427.1 1.5 copy-start.5
  427.1 1.6 copy-start.7
  428.7 1.7 copy-start.1
  (1 other events, 0.7 us)

commit v5 on v3

--- a/solution.py
+++ b/solution.py
@@ -110,7 +110,7 @@
 
 
 def pair_tile(rows, cols):
-    return math.gcd(rows, 64 * 3072 // cols)
+    return math.gcd(rows, 32 * 3072 // cols)
 
 
 def pair(terms, index, nears):
@@ -150,7 +150,7 @@
 
 def adamw(me, terms, near, far, w, m, v, layer, first, rows, before):
     block, cols = m.shape[1], m.shape[2]
-    tile = math.gcd(rows, first, block, 64 * 3072 // cols)
+    tile = math.gcd(rows, first, block, 32 * 3072 // cols)
     at, per = first // tile, block // tile
     mine = pl.BlockSpec((1, tile, cols), lambda i, me: (layer, at + i, 0))
     whole = pl.BlockSpec((1, tile, cols), lambda i, me: (layer, me[0] * per + at + i, 0))
@@ -210,6 +210,42 @@
     )(me, *pieces, out)
 
 
+def carry_body(chunk, block, me, beside, across, corner, before, out, held, in_sem, out_sem):
+    _, layer, first, rows = chunk
+    ins = [pltpu.make_async_copy(src, held.at[i], in_sem.at[i]) for i, src in enumerate((beside, across, corner))]
+    outs = [
+        pltpu.make_async_copy(held.at[i], out.at[layer, pl.ds(pl.multiple_of((me[0] ^ (1 + i)) * block + first, 16), rows)], out_sem.at[i])
+        for i in range(3)
+    ]
+    for copy in ins:
+        copy.start()
+    for came, goes in zip(ins, outs):
+        came.wait()
+        goes.start()
+    for copy in outs:
+        copy.wait()
+
+
+def carry(me, chunk, pieces, out, block):
+    _, _, _, rows = chunk
+    cols = out.shape[2]
+    anywhere = pl.BlockSpec(memory_space=pl.ANY)
+    return pl.pallas_call(
+        functools.partial(carry_body, chunk, block),
+        in_specs=[pl.BlockSpec(memory_space=pltpu.SMEM)] + [anywhere] * 4,
+        out_specs=anywhere,
+        out_shape=jax.ShapeDtypeStruct(out.shape, out.dtype),
+        input_output_aliases={4: 0},
+        scratch_shapes=[
+            pltpu.VMEM((3, rows, cols), jnp.bfloat16),
+            pltpu.SemaphoreType.DMA((3,)),
+            pltpu.SemaphoreType.DMA((3,)),
+        ],
+        cost_estimate=pl.CostEstimate(flops=3 * rows * cols, bytes_accessed=12 * rows * cols, transcendentals=0),
+        name="carry",
+    )(me, *pieces, out)
+
+
 def solution(mesh):
     def inner(*arrays):
         terms, weights, m, v = (arrays[i : i + 3] for i in (0, 3, 6, 9))
@@ -237,7 +273,10 @@
             which = CHUNKS[c][0]
             together = (c,) if c < LAST - 1 else (c, LAST)
             pieces = [got[i] for i in together for got in (beside, across, corner)]
-            state[which][0] = place(me, [CHUNKS[i] for i in together], pieces, state[which][0], m[which].shape[1])
+            if c < LAST - 2:
+                state[which][0] = carry(me, CHUNKS[c], pieces, state[which][0], m[which].shape[1])
+            else:
+                state[which][0] = place(me, [CHUNKS[i] for i in together], pieces, state[which][0], m[which].shape[1])
         return tuple(state[which][i] for i in range(3) for which in range(3))
 
     all_of, cut_rows = P(None, None, None), P(None, "dp", None)

time: 452 us -> 461 us (1.020)
  Pallas kernels: 135 us -> 150 us
  waiting for transfers between devices: 281 us -> 276 us
    pallas_call x0 -> x8, Pallas kernels: none -> 23.9 us  [carry(): pl.pallas_call(functools.partial(carry_body, chunk, block), in_specs=[pl....]
    pallas_call x10 -> x2, Pallas kernels: 20.7 us -> 2.1 us  [place(): pl.pallas_call(functools.partial(place_body, chunks, block), in_specs=[pl...]
    pallas_call x11, Pallas kernels: 66.7 us -> 76.3 us  [adamw(): pl.pallas_call(functools.partial(adamw_body, n_alias), grid_spec=pltpu.Pr...]
    ppermute x44, waiting for transfers between devices: 281 us -> 276 us  [send(): return lax.ppermute(x, 'dp', to)]
  transfers between devices with their start and end apart: 44 -> 44, of which waited for: 11 -> 11; matrix products, arithmetic and copies ran while one was open for 0% -> 0% of each run, Pallas kernels for 29% -> 32%
where the time goes in v5:
time: 461 us; the launch traced here: 459 us
  waiting for transfers between devices  276 us (60%)
  Pallas kernels  150 us (33%)
  starting transfers between devices  29.1 us (6%)
    ppermute x44, waiting for transfers between devices, send(): return lax.ppermute(x, 'dp', to)  276 us
    pallas_call x11, Pallas kernels, adamw(): pl.pallas_call(functools.partial(adamw_body, n_alias), grid_spec=pltpu.Pr...  76.3 us
    pallas_call x10, Pallas kernels, pair(): pl.pallas_call(functools.partial(pair_body, chunk, nears), in_specs=[anyw...  45.6 us
    ppermute x44, starting transfers between devices, send(): return lax.ppermute(x, 'dp', to)  29.1 us
    pallas_call x8, Pallas kernels, carry(): pl.pallas_call(functools.partial(carry_body, chunk, block), in_specs=[pl....  23.9 us
  transfers between devices with their start and end apart: 44, of which 11 were waited for; matrix products, arithmetic and copies ran while one was open for 0% of the time, Pallas kernels for 32%

profile of v5, /device:TPU:0, one launch (start us, length us, event | category | flops | bytes accessed | tf_op | source)
XLA Modules:
  0.0 459.5 jit_solution(1987730922851575640)
XLA Ops:
  0.6 2.3 first_pair.1
  2.9 2.9 collective-permute-start.3
  5.9 2.9 pair.12
  8.9 2.2 pair.19
  11.1 2.0 collective-permute-start.31
  13.1 3.1 pair.16
  16.3 5.1 %pair.11 = (bf16[128,3072]{1,0:T(8,128)(2,1)}, bf16[48,3072]{1,0:T(8,128)(2,1)}, bf16[80,3072]{1,0:T(8,128)(2,1)}, bf16[128,3072]{1,0:T(8,128)(2,1)}) custom-call(bf16[1,2,1024,3072]{3,2,1,0:T(8,128)(2,1)} %refs_0_.19, bf16[1,2,1024,3072]{3,2,1,0:T(8,128)(2,1)} %refs_1_.19, bf16[1,2,3072,1024]{3,2,1,0:T(8,128)(2,1)} %own.21), custom_call_target="tpu_custom_call" | custom-call | flops 393216 | bytes 3932160 | tf_op jit(solution)/shard_map/pair/pallas_call | solution.py:123
  21.4 2.0 collective-permute-start.1
  23.4 3.9 pair.17
  27.3 1.1 collective-permute-start.26
  28.4 2.4 pair.15
  30.9 1.0 collective-permute-start.24
  31.9 6.3 %pair.18 = (bf16[768,1024]{1,0:T(8,128)(2,1)}, bf16[768,1024]{1,0:T(8,128)(2,1)}) custom-call(bf16[1,2,1024,3072]{3,2,1,0:T(8,128)(2,1)} %refs_0_.19, bf16[1,2,1024,3072]{3,2,1,0:T(8,128)(2,1)} %refs_1_.19, bf16[1,2,3072,1024]{3,2,1,0:T(8,128)(2,1)} %own.21), custom_call_target="tpu_custom_call" | custom-call | flops 786432 | bytes 7864320 | tf_op jit(solution)/shard_map/pair/pallas_call | solution.py:123
  38.2 4.0 adamw.11
  42.2 32.1 %collective-permute-done.24.far = bf16[96,1024]{1,0:T(8,128)(2,1)S(1)} collective-permute-done((bf16[96,1024]{1,0:T(8,128)(2,1)}, bf16[96,1024]{1,0:T(8,128)(2,1)S(1)}, u32[]{:S(2)}, u32[]{:S(2)}) %collective-permute-start.24) | collective-permute-done | bytes 196640 | tf_op jit(solution)/shard_map/ppermute | solution.py:255
  74.2 0.7 copy-done.17
  74.9 1.7 collective-permute-start.27
  77.4 5.7 %adamw.12 = (bf16[80,3072]{1,0:T(8,128)(2,1)}, bf16[2,1024,3072]{2,1,0:T(8,128)(2,1)}, f32[2,256,3072]{2,1,0:T(8,128)}, f32[2,256,3072]{2,1,0:T(8,128)}) custom-call(s32[1]{0:T(128)} %bitcast.me, bf16[1,2,1024,3072]{3,2,1,0:T(8,128)(2,1)} %refs_0_.19, ...), custom_call_target="tpu_custom_call", output_to_operand_aliasing={{1}: (7, {}), {2}: (8, {}), {3}: (9, {})} | custom-call | flops 3440640 | bytes 6881280 | tf_op jit(solution)/shard_map/adamw/pallas_call | solution.py:162
  83.1 7.0 %pair.10 = (bf16[256,3072]{1,0:T(8,128)(2,1)}, bf16[256,3072]{1,0:T(8,128)(2,1)}) custom-call(bf16[1,2,1024,3072]{3,2,1,0:T(8,128)(2,1)} %refs_0_.19, bf16[1,2,1024,3072]{3,2,1,0:T(8,128)(2,1)} %refs_1_.19, bf16[1,2,3072,1024]{3,2,1,0:T(8,128)(2,1)} %own.21), custom_call_target="tpu_custom_call" | custom-call | flops 786432 | bytes 7864320 | tf_op jit(solution)/shard_map/pair/pallas_call | solution.py:123
  90.1 27.2 %collective-permute-done.14.across = bf16[48,3072]{1,0:T(8,128)(2,1)} collective-permute-done((bf16[48,3072]{1,0:T(8,128)(2,1)}, bf16[48,3072]{1,0:T(8,128)(2,1)}, u32[]{:S(2)}, u32[]{:S(2)}) %collective-permute-start.14) | collective-permute-done | bytes 294944 | tf_op jit(solution)/shard_map/ppermute | solution.py:255
  117.3 0.9 copy-done.10
  118.2 1.5 collective-permute-start
  119.7 0.6 collective-permute-start.11
  120.2 6.3 %pair.13 = (bf16[256,3072]{1,0:T(8,128)(2,1)}, bf16[256,3072]{1,0:T(8,128)(2,1)}) custom-call(bf16[1,2,1024,3072]{3,2,1,0:T(8,128)(2,1)} %refs_0_.19, bf16[1,2,1024,3072]{3,2,1,0:T(8,128)(2,1)} %refs_1_.19, bf16[1,2,3072,1024]{3,2,1,0:T(8,128)(2,1)} %own.21), custom_call_target="tpu_custom_call" | custom-call | flops 786432 | bytes 7864320 | tf_op jit(solution)/shard_map/pair/pallas_call | solution.py:123
  126.5 6.3 %pair.14 = (bf16[256,3072]{1,0:T(8,128)(2,1)}, bf16[256,3072]{1,0:T(8,128)(2,1)}) custom-call(bf16[1,2,1024,3072]{3,2,1,0:T(8,128)(2,1)} %refs_0_.19, bf16[1,2,1024,3072]{3,2,1,0:T(8,128)(2,1)} %refs_1_.19, bf16[1,2,3072,1024]{3,2,1,0:T(8,128)(2,1)} %own.21), custom_call_target="tpu_custom_call" | custom-call | flops 786432 | bytes 7864320 | tf_op jit(solution)/shard_map/pair/pallas_call | solution.py:123
  132.9 1.5 collective-permute-start.16
  134.4 0.6 collective-permute-start.17
  134.9 31.4 %collective-permute-done.11.across = bf16[80,3072]{1,0:T(8,128)(2,1)} collective-permute-done((bf16[80,3072]{1,0:T(8,128)(2,1)}, bf16[80,3072]{1,0:T(8,128)(2,1)}, u32[]{:S(2)}, u32[]{:S(2)}) %collective-permute-start.11) | collective-permute-done | bytes 491552 | tf_op jit(solution)/shard_map/ppermute | solution.py:255
  166.3 5.9 %adamw.13 = (bf16[128,3072]{1,0:T(8,128)(2,1)}, bf16[2,1024,3072]{2,1,0:T(8,128)(2,1)}, f32[2,256,3072]{2,1,0:T(8,128)}, f32[2,256,3072]{2,1,0:T(8,128)}) custom-call(s32[1]{0:T(128)} %bitcast.me, bf16[1,2,1024,3072]{3,2,1,0:T(8,128)(2,1)} %refs_0_.19, ...), custom_call_target="tpu_custom_call", output_to_operand_aliasing={{1}: (7, {}), {2}: (8, {}), {3}: (9, {})} | custom-call | flops 5505024 | bytes 11010048 | tf_op jit(solution)/shard_map/adamw/pallas_call | solution.py:162
  172.7 1.5 collective-permute-start.8
  174.2 11.0 %adamw.17 = (bf16[768,1024]{1,0:T(8,128)(2,1)}, bf16[2,3072,1024]{2,1,0:T(8,128)(2,1)}, f32[2,768,1024]{2,1,0:T(8,128)}, f32[2,768,1024]{2,1,0:T(8,128)}) custom-call(s32[1]{0:T(128)} %bitcast.me, bf16[1,2,3072,1024]{3,2,1,0:T(8,128)(2,1)} %own.21, bf16[768,1024]{1,0:T(8,128)(2,1)} %get-tuple-element.109.near, bf16[768,1024]{1,0:T(8,128)(2,1)} %copy-done.2, ...), custom_call_target="tpu_custom_call" | custom-call | flops 11010048 | bytes 22020096 | tf_op jit(solution)/shard_map/adamw/pallas_call | solution.py:162
  185.2 5.9 %adamw.18 = (bf16[384,1024]{1,0:T(8,128)(2,1)}, bf16[2,3072,1024]{2,1,0:T(8,128)(2,1)}, f32[2,768,1024]{2,1,0:T(8,128)}, f32[2,768,1024]{2,1,0:T(8,128)}) custom-call(s32[1]{0:T(128)} %bitcast.me, bf16[1,2,3072,1024]{3,2,1,0:T(8,128)(2,1)} %own.21, ...), custom_call_target="tpu_custom_call", output_to_operand_aliasing={{1}: (7, {}), {2}: (8, {}), {3}: (9, {})} | custom-call | flops 5505024 | bytes 11010048 | tf_op jit(solution)/shard_map/adamw/pallas_call | solution.py:162
  191.1 5.7 %adamw.19 = (bf16[240,1024]{1,0:T(8,128)(2,1)}, bf16[2,3072,1024]{2,1,0:T(8,128)(2,1)}, f32[2,768,1024]{2,1,0:T(8,128)}, f32[2,768,1024]{2,1,0:T(8,128)}) custom-call(s32[1]{0:T(128)} %bitcast.me, bf16[1,2,3072,1024]{3,2,1,0:T(8,128)(2,1)} %own.21, ...), custom_call_target="tpu_custom_call", output_to_operand_aliasing={{1}: (7, {}), {2}: (8, {}), {3}: (9, {})} | custom-call | flops 3440640 | bytes 6881280 | tf_op jit(solution)/shard_map/adamw/pallas_call | solution.py:162
  196.9 2.9 adamw.20
  199.8 2.2 adamw.21
  202.0 1.1 collective-permute-start.33
  203.1 11.0 %adamw.14 = (bf16[256,3072]{1,0:T(8,128)(2,1)}, bf16[2,1024,3072]{2,1,0:T(8,128)(2,1)}, f32[2,256,3072]{2,1,0:T(8,128)}, f32[2,256,3072]{2,1,0:T(8,128)}) custom-call(s32[1]{0:T(128)} %bitcast.me, bf16[1,2,1024,3072]{3,2,1,0:T(8,128)(2,1)} %refs_0_.19, ...), custom_call_target="tpu_custom_call", output_to_operand_aliasing={{1}: (7, {}), {2}: (8, {}), {3}: (9, {})} | custom-call | flops 11010048 | bytes 22020096 | tf_op jit(solution)/shard_map/adamw/pallas_call | solution.py:162
  214.2 36.4 %collective-permute-done.8.across = bf16[128,3072]{1,0:T(8,128)(2,1)} collective-permute-done((bf16[128,3072]{1,0:T(8,128)(2,1)}, bf16[128,3072]{1,0:T(8,128)(2,1)}, u32[]{:S(2)}, u32[]{:S(2)}) %collective-permute-start.8) | collective-permute-done | bytes 786464 | tf_op jit(solution)/shard_map/ppermute | solution.py:255
  250.6 1.5 collective-permute-start.29
  252.1 0.6 collective-permute-start.5
  252.9 4.9 %collective-permute-done.29.refs_1_ = bf16[96,1024]{1,0:T(8,128)(2,1)S(1)} collective-permute-done((bf16[96,1024]{1,0:T(8,128)(2,1)S(1)}, bf16[96,1024]{1,0:T(8,128)(2,1)S(1)}, u32[]{:S(2)}, u32[]{:S(2)}) %collective-permute-start.29) | collective-permute-done | bytes 196640 | tf_op jit(solution)/shard_map/ppermute | solution.py:255
  257.8 2.0 collective-permute-start.36
  259.8 41.0 %collective-permute-done.36.refs_1_ = bf16[240,1024]{1,0:T(8,128)(2,1)S(1)} collective-permute-done((bf16[240,1024]{1,0:T(8,128)(2,1)S(1)}, bf16[240,1024]{1,0:T(8,128)(2,1)S(1)}, u32[]{:S(2)}, u32[]{:S(2)}) %collective-permute-start.36) | collective-permute-done | bytes 491552 | tf_op jit(solution)/shard_map/ppermute | solution.py:255
  300.8 1.5 collective-permute-start.39
  302.3 11.0 %adamw.15 = (bf16[256,3072]{1,0:T(8,128)(2,1)}, bf16[2,1024,3072]{2,1,0:T(8,128)(2,1)}, f32[2,256,3072]{2,1,0:T(8,128)}, f32[2,256,3072]{2,1,0:T(8,128)}) custom-call(s32[1]{0:T(128)} %bitcast.me, bf16[1,2,1024,3072]{3,2,1,0:T(8,128)(2,1)} %refs_1_.19, bf16[256,3072]{1,0:T(8,128)(2,1)} %get-tuple-element.95.near, ...), custom_call_target="tpu_custom_call" | custom-call | flops 11010048 | bytes 22020096 | tf_op jit(solution)/shard_map/adamw/pallas_call | solution.py:162
  313.3 11.0 %adamw.16 = (bf16[256,3072]{1,0:T(8,128)(2,1)}, bf16[2,1024,3072]{2,1,0:T(8,128)(2,1)}, f32[2,256,3072]{2,1,0:T(8,128)}, f32[2,256,3072]{2,1,0:T(8,128)}) custom-call(s32[1]{0:T(128)} %bitcast.me, bf16[1,2,1024,3072]{3,2,1,0:T(8,128)(2,1)} %refs_1_.19, ...), custom_call_target="tpu_custom_call", output_to_operand_aliasing={{1}: (7, {}), {2}: (8, {}), {3}: (9, {})} | custom-call | flops 11010048 | bytes 22020096 | tf_op jit(solution)/shard_map/adamw/pallas_call | solution.py:162
  324.9 0.6 collective-permute-start.19
  325.4 3.2 collective-permute-done.37.refs_2_
  329.4 1.5 collective-permute-start.42
  330.8 31.6 %collective-permute-done.19.across = bf16[256,3072]{1,0:T(8,128)(2,1)} collective-permute-done((bf16[256,3072]{1,0:T(8,128)(2,1)}, bf16[256,3072]{1,0:T(8,128)(2,1)}, u32[]{:S(2)}, u32[]{:S(2)}) %collective-permute-start.19) | collective-permute-done | bytes 1572896 | tf_op jit(solution)/shard_map/ppermute | solution.py:255
  363.0 33.1 %collective-permute-done.22.across = bf16[256,3072]{1,0:T(8,128)(2,1)S(1)} collective-permute-done((bf16[256,3072]{1,0:T(8,128)(2,1)}, bf16[256,3072]{1,0:T(8,128)(2,1)S(1)}, u32[]{:S(2)}, u32[]{:S(2)}) %collective-permute-start.22) | collective-permute-done | bytes 1572896 | tf_op jit(solution)/shard_map/ppermute | solution.py:255
  396.0 32.8 %collective-permute-done.42.across = bf16[768,1024]{1,0:T(8,128)(2,1)S(1)} collective-permute-done((bf16[768,1024]{1,0:T(8,128)(2,1)}, bf16[768,1024]{1,0:T(8,128)(2,1)S(1)}, u32[]{:S(2)}, u32[]{:S(2)}) %collective-permute-start.42) | collective-permute-done | bytes 1572896 | tf_op jit(solution)/shard_map/ppermute | solution.py:255
  429.9 2.3 collective-permute-done.43.corner
  432.4 1.0 copy-done.8
  433.4 1.9 carry.8.before
  435.3 2.2 carry.9.before
  437.5 2.6 carry.10.before
  440.1 3.6 carry.14.before
  443.8 2.6 carry.15.refs_3_
  446.4 1.1 place.2.refs_6_
  447.5 3.6 carry.11
  451.1 3.6 carry.12.before
  454.8 3.6 carry.13
  458.5 1.0 place.3
  (100 shorter events, 4.7 us)
Async XLA Ops:
  2.9 27.9 %collective-permute-start.3 = (bf16[48,3072]{1,0:T(8,128)(2,1)S(1)}, bf16[48,3072]{1,0:T(8,128)(2,1)S(1)}, u32[]{:S(2)}, u32[]{:S(2)}) collective-permute-start(bf16[48,3072]{1,0:T(8,128)(2,1)S(1)} %first_pair.1), channel_id=1, source_target_pairs={{0,2},{2,0},{1,3},{3,1},{4,6},{6,4},{5,7},{7,5}} | collective-permute-start | bytes 884744 | tf_op jit(solution)/shard_map/ppermute | solution.py:255
  8.8 67.8 %collective-permute-start.2 = (bf16[80,3072]{1,0:T(8,128)(2,1)}, bf16[80,3072]{1,0:T(8,128)(2,1)S(1)}, u32[]{:S(2)}, u32[]{:S(2)}) collective-permute-start(bf16[80,3072]{1,0:T(8,128)(2,1)} %pair.12), channel_id=1, source_target_pairs={{0,2},{2,0},{1,3},{3,1},{4,6},{6,4},{5,7},{7,5}} | collective-permute-start | bytes 1474568 | tf_op jit(solution)/shard_map/ppermute | solution.py:255
  11.1 16.2 %collective-permute-start.31 = (bf16[48,1024]{1,0:T(8,128)(2,1)}, bf16[48,1024]{1,0:T(8,128)(2,1)S(1)}, u32[]{:S(2)}, u32[]{:S(2)}) collective-permute-start(bf16[48,1024]{1,0:T(8,128)(2,1)} %get-tuple-element.122), channel_id=1, source_target_pairs={{0,2},{2,0},{1,3},{3,1},{4,6},{6,4},{5,7},{7,5}} | collective-permute-start | bytes 294920 | tf_op jit(solution)/shard_map/ppermute | solution.py:255
  16.2 60.4 %collective-permute-start.25 = (bf16[240,1024]{1,0:T(8,128)(2,1)}, bf16[240,1024]{1,0:T(8,128)(2,1)S(1)}, u32[]{:S(2)}, u32[]{:S(2)}) collective-permute-start(bf16[240,1024]{1,0:T(8,128)(2,1)} %get-tuple-element.106), channel_id=1, source_target_pairs={{0,2},{2,0},{1,3},{3,1},{4,6},{6,4},{5,7},{7,5}} | collective-permute-start | bytes 1474568 | tf_op jit(solution)/shard_map/ppermute | solution.py:255
  21.4 96.0 %collective-permute-start.1 = (bf16[128,3072]{1,0:T(8,128)(2,1)}, bf16[128,3072]{1,0:T(8,128)(2,1)S(1)}, u32[]{:S(2)}, u32[]{:S(2)}) collective-permute-start(bf16[128,3072]{1,0:T(8,128)(2,1)} %get-tuple-element.76), channel_id=1, source_target_pairs={{0,2},{2,0},{1,3},{3,1},{4,6},{6,4},{5,7},{7,5}} | collective-permute-start | bytes 2359304 | tf_op jit(solution)/shard_map/ppermute | solution.py:255
  27.3 3.5 copy-start.18
  27.3 92.3 %collective-permute-start.26 = (bf16[384,1024]{1,0:T(8,128)(2,1)}, bf16[384,1024]{1,0:T(8,128)(2,1)}, u32[]{:S(2)}, u32[]{:S(2)}) collective-permute-start(bf16[384,1024]{1,0:T(8,128)(2,1)} %get-tuple-element.108), channel_id=1, source_target_pairs={{0,2},{2,0},{1,3},{3,1},{4,6},{6,4},{5,7},{7,5}} | collective-permute-start | bytes 2359304 | tf_op jit(solution)/shard_map/ppermute | solution.py:255
  30.9 7.3 %copy-start.15 = (bf16[48,3072]{1,0:T(8,128)(2,1)}, bf16[48,3072]{1,0:T(8,128)(2,1)S(1)}, u32[]{:S(2)}) copy-start(bf16[48,3072]{1,0:T(8,128)(2,1)S(1)} %collective-permute-done.3.far) | copy-start | bytes 884740
  30.9 43.3 %collective-permute-start.24 = (bf16[96,1024]{1,0:T(8,128)(2,1)}, bf16[96,1024]{1,0:T(8,128)(2,1)S(1)}, u32[]{:S(2)}, u32[]{:S(2)}) collective-permute-start(bf16[96,1024]{1,0:T(8,128)(2,1)} %get-tuple-element.104), channel_id=1, source_target_pairs={{0,2},{2,0},{1,3},{3,1},{4,6},{6,4},{5,7},{7,5}} | collective-permute-start | bytes 589832 | tf_op jit(solution)/shard_map/ppermute | solution.py:255
  74.9 97.8 %collective-permute-start.27 = (bf16[768,1024]{1,0:T(8,128)(2,1)}, bf16[768,1024]{1,0:T(8,128)(2,1)S(1)}, u32[]{:S(2)}, u32[]{:S(2)}) collective-permute-start(bf16[768,1024]{1,0:T(8,128)(2,1)} %get-tuple-element.110), channel_id=1, source_target_pairs={{0,2},{2,0},{1,3},{3,1},{4,6},{6,4},{5,7},{7,5}} | collective-permute-start | bytes 4718600 | tf_op jit(solution)/shard_map/ppermute | solution.py:255
  76.6 6.4 %collective-permute-start.13 = (bf16[48,3072]{1,0:T(8,128)(2,1)}, bf16[48,3072]{1,0:T(8,128)(2,1)}, u32[]{:S(2)}, u32[]{:S(2)}) collective-permute-start(bf16[48,3072]{1,0:T(8,128)(2,1)} %get-tuple-element.91), channel_id=1, source_target_pairs={{0,1},{1,0},{2,3},{3,2},{4,5},{5,4},{6,7},{7,6}} | collective-permute-start | bytes 884744 | tf_op jit(solution)/shard_map/ppermute | solution.py:255
  76.6 6.4 %copy-start.13 = (bf16[240,1024]{1,0:T(8,128)(2,1)}, bf16[240,1024]{1,0:T(8,128)(2,1)S(1)}, u32[]{:S(2)}) copy-start(bf16[240,1024]{1,0:T(8,128)(2,1)S(1)} %collective-permute-done.25.far) | copy-start | bytes 1474564
  76.7 40.7 %collective-permute-start.14 = (bf16[48,3072]{1,0:T(8,128)(2,1)}, bf16[48,3072]{1,0:T(8,128)(2,1)}, u32[]{:S(2)}, u32[]{:S(2)}) collective-permute-start(bf16[48,3072]{1,0:T(8,128)(2,1)} %get-tuple-element.91), channel_id=1, source_target_pairs={{0,2},{2,0},{1,3},{3,1},{4,6},{6,4},{5,7},{7,5}} | collective-permute-start | bytes 884744 | tf_op jit(solution)/shard_map/ppermute | solution.py:255
  83.1 51.3 %collective-permute-start.10 = (bf16[80,3072]{1,0:T(8,128)(2,1)}, bf16[80,3072]{1,0:T(8,128)(2,1)}, u32[]{:S(2)}, u32[]{:S(2)}) collective-permute-start(bf16[80,3072]{1,0:T(8,128)(2,1)} %get-tuple-element.90), channel_id=1, source_target_pairs={{0,1},{1,0},{2,3},{3,2},{4,5},{5,4},{6,7},{7,6}} | collective-permute-start | bytes 1474568 | tf_op jit(solution)/shard_map/ppermute | solution.py:255
  117.3 15.6 %collective-permute-start.15 = (bf16[48,3072]{1,0:T(8,128)(2,1)}, bf16[48,3072]{1,0:T(8,128)(2,1)S(1)}, u32[]{:S(2)}, u32[]{:S(2)}) collective-permute-start(bf16[48,3072]{1,0:T(8,128)(2,1)} %collective-permute-done.14.across), channel_id=1, source_target_pairs={{0,1},{1,0},{2,3},{3,2},{4,5},{5,4},{6,7},{7,6}} | collective-permute-start | bytes 884744 | tf_op jit(solution)/shard_map/ppermute | solution.py:255
  117.3 0.9 copy-start.10
  118.2 78.6 %collective-permute-start = (bf16[256,3072]{1,0:T(8,128)(2,1)}, bf16[256,3072]{1,0:T(8,128)(2,1)S(1)}, u32[]{:S(2)}, u32[]{:S(2)}) collective-permute-start(bf16[256,3072]{1,0:T(8,128)(2,1)} %get-tuple-element.74), channel_id=1, source_target_pairs={{0,2},{2,0},{1,3},{3,1},{4,6},{6,4},{5,7},{7,5}} | collective-permute-start | bytes 4718600 | tf_op jit(solution)/shard_map/ppermute | solution.py:255
  119.7 46.7 %collective-permute-start.11 = (bf16[80,3072]{1,0:T(8,128)(2,1)}, bf16[80,3072]{1,0:T(8,128)(2,1)}, u32[]{:S(2)}, u32[]{:S(2)}) collective-permute-start(bf16[80,3072]{1,0:T(8,128)(2,1)} %get-tuple-element.90), channel_id=1, source_target_pairs={{0,2},{2,0},{1,3},{3,1},{4,6},{6,4},{5,7},{7,5}} | collective-permute-start | bytes 1474568 | tf_op jit(solution)/shard_map/ppermute | solution.py:255
  132.9 39.3 %copy-start.16 = (bf16[48,3072]{1,0:T(8,128)(2,1)}, bf16[48,3072]{1,0:T(8,128)(2,1)S(1)}, u32[]{:S(2)}) copy-start(bf16[48,3072]{1,0:T(8,128)(2,1)S(1)} %collective-permute-done.15.corner) | copy-start | bytes 884740
  132.9 119.2 %collective-permute-start.16 = (bf16[256,3072]{1,0:T(8,128)(2,1)}, bf16[256,3072]{1,0:T(8,128)(2,1)}, u32[]{:S(2)}, u32[]{:S(2)}) collective-permute-start(bf16[256,3072]{1,0:T(8,128)(2,1)} %get-tuple-element.94), channel_id=1, source_target_pairs={{0,2},{2,0},{1,3},{3,1},{4,6},{6,4},{5,7},{7,5}} | collective-permute-start | bytes 4718600 | tf_op jit(solution)/shard_map/ppermute | solution.py:255
  134.4 117.7 %collective-permute-start.17 = (bf16[256,3072]{1,0:T(8,128)(2,1)}, bf16[256,3072]{1,0:T(8,128)(2,1)}, u32[]{:S(2)}, u32[]{:S(2)}) collective-permute-start(bf16[256,3072]{1,0:T(8,128)(2,1)} %get-tuple-element.96), channel_id=1, source_target_pairs={{0,2},{2,0},{1,3},{3,1},{4,6},{6,4},{5,7},{7,5}} | collective-permute-start | bytes 4718600 | tf_op jit(solution)/shard_map/ppermute | solution.py:255
  166.3 5.9 %collective-permute-start.12 = (bf16[80,3072]{1,0:T(8,128)(2,1)}, bf16[80,3072]{1,0:T(8,128)(2,1)}, u32[]{:S(2)}, u32[]{:S(2)}) collective-permute-start(bf16[80,3072]{1,0:T(8,128)(2,1)} %collective-permute-done.11.across), channel_id=1, source_target_pairs={{0,1},{1,0},{2,3},{3,2},{4,5},{5,4},{6,7},{7,6}} | collective-permute-start | bytes 1474568 | tf_op jit(solution)/shard_map/ppermute | solution.py:255
  172.2 29.8 %collective-permute-start.7 = (bf16[128,3072]{1,0:T(8,128)(2,1)}, bf16[128,3072]{1,0:T(8,128)(2,1)}, u32[]{:S(2)}, u32[]{:S(2)}) collective-permute-start(bf16[128,3072]{1,0:T(8,128)(2,1)} %get-tuple-element.89), channel_id=1, source_target_pairs={{0,1},{1,0},{2,3},{3,2},{4,5},{5,4},{6,7},{7,6}} | collective-permute-start | bytes 2359304 | tf_op jit(solution)/shard_map/ppermute | solution.py:255
  172.7 1.5 copy-start.2
  172.7 77.8 %collective-permute-start.8 = (bf16[128,3072]{1,0:T(8,128)(2,1)}, bf16[128,3072]{1,0:T(8,128)(2,1)}, u32[]{:S(2)}, u32[]{:S(2)}) collective-permute-start(bf16[128,3072]{1,0:T(8,128)(2,1)} %get-tuple-element.89), channel_id=1, source_target_pairs={{0,2},{2,0},{1,3},{3,1},{4,6},{6,4},{5,7},{7,5}} | collective-permute-start | bytes 2359304 | tf_op jit(solution)/shard_map/ppermute | solution.py:255
  196.8 3.0 copy-start.9
  196.8 63.0 %collective-permute-start.35 = (bf16[240,1024]{1,0:T(8,128)(2,1)}, bf16[240,1024]{1,0:T(8,128)(2,1)S(1)}, u32[]{:S(2)}, u32[]{:S(2)}) collective-permute-start(bf16[240,1024]{1,0:T(8,128)(2,1)} %get-tuple-element.127), channel_id=1, source_target_pairs={{0,1},{1,0},{2,3},{3,2},{4,5},{5,4},{6,7},{7,6}} | collective-permute-start | bytes 1474568 | tf_op jit(solution)/shard_map/ppermute | solution.py:255
  202.0 50.7 %collective-permute-start.33 = (bf16[48,1024]{1,0:T(8,128)(2,1)}, bf16[48,1024]{1,0:T(8,128)(2,1)S(1)}, u32[]{:S(2)}, u32[]{:S(2)}) collective-permute-start(bf16[48,1024]{1,0:T(8,128)(2,1)} %get-tuple-element.126), channel_id=1, source_target_pairs={{0,2},{2,0},{1,3},{3,1},{4,6},{6,4},{5,7},{7,5}} | collective-permute-start | bytes 294920 | tf_op jit(solution)/shard_map/ppermute | solution.py:255
  203.1 47.5 %copy-start.20 = (bf16[96,1024]{1,0:T(8,128)(2,1)S(1)}, bf16[96,1024]{1,0:T(8,128)(2,1)}, u32[]{:S(2)}) copy-start(bf16[96,1024]{1,0:T(8,128)(2,1)} %get-tuple-element.120) | copy-start | bytes 589828
  203.1 54.7 %copy-start.19 = (bf16[240,1024]{1,0:T(8,128)(2,1)S(1)}, bf16[240,1024]{1,0:T(8,128)(2,1)}, u32[]{:S(2)}) copy-start(bf16[240,1024]{1,0:T(8,128)(2,1)} %get-tuple-element.127) | copy-start | bytes 1474564
  250.6 7.2 %collective-permute-start.29 = (bf16[96,1024]{1,0:T(8,128)(2,1)S(1)}, bf16[96,1024]{1,0:T(8,128)(2,1)S(1)}, u32[]{:S(2)}, u32[]{:S(2)}) collective-permute-start(bf16[96,1024]{1,0:T(8,128)(2,1)S(1)} %copy-done.20), channel_id=1, source_target_pairs={{0,2},{2,0},{1,3},{3,1},{4,6},{6,4},{5,7},{7,5}} | collective-permute-start | bytes 589832 | tf_op jit(solution)/shard_map/ppermute | solution.py:255
  252.0 76.8 %collective-permute-start.4 = (bf16[256,3072]{1,0:T(8,128)(2,1)}, bf16[256,3072]{1,0:T(8,128)(2,1)}, u32[]{:S(2)}, u32[]{:S(2)}) collective-permute-start(bf16[256,3072]{1,0:T(8,128)(2,1)} %get-tuple-element.88), channel_id=1, source_target_pairs={{0,1},{1,0},{2,3},{3,2},{4,5},{5,4},{6,7},{7,6}} | collective-permute-start | bytes 4718600 | tf_op jit(solution)/shard_map/ppermute | solution.py:255
  252.1 77.3 %collective-permute-start.5 = (bf16[256,3072]{1,0:T(8,128)(2,1)}, bf16[256,3072]{1,0:T(8,128)(2,1)}, u32[]{:S(2)}, u32[]{:S(2)}) collective-permute-start(bf16[256,3072]{1,0:T(8,128)(2,1)} %get-tuple-element.88), channel_id=1, source_target_pairs={{0,2},{2,0},{1,3},{3,1},{4,6},{6,4},{5,7},{7,5}} | collective-permute-start | bytes 4718600 | tf_op jit(solution)/shard_map/ppermute | solution.py:255
  252.6 71.7 %collective-permute-start.9 = (bf16[128,3072]{1,0:T(8,128)(2,1)}, bf16[128,3072]{1,0:T(8,128)(2,1)S(1)}, u32[]{:S(2)}, u32[]{:S(2)}) collective-permute-start(bf16[128,3072]{1,0:T(8,128)(2,1)} %collective-permute-done.8.across), channel_id=1, source_target_pairs={{0,1},{1,0},{2,3},{3,2},{4,5},{5,4},{6,7},{7,6}} | collective-permute-start | bytes 2359304 | tf_op jit(solution)/shard_map/ppermute | solution.py:255
  257.8 43.0 %collective-permute-start.36 = (bf16[240,1024]{1,0:T(8,128)(2,1)S(1)}, bf16[240,1024]{1,0:T(8,128)(2,1)S(1)}, u32[]{:S(2)}, u32[]{:S(2)}) collective-permute-start(bf16[240,1024]{1,0:T(8,128)(2,1)S(1)} %copy-done.19), channel_id=1, source_target_pairs={{0,2},{2,0},{1,3},{3,1},{4,6},{6,4},{5,7},{7,5}} | collective-permute-start | bytes 1474568 | tf_op jit(solution)/shard_map/ppermute | solution.py:255
  259.8 64.5 %collective-permute-start.38 = (bf16[384,1024]{1,0:T(8,128)(2,1)}, bf16[384,1024]{1,0:T(8,128)(2,1)}, u32[]{:S(2)}, u32[]{:S(2)}) collective-permute-start(bf16[384,1024]{1,0:T(8,128)(2,1)} %get-tuple-element.128), channel_id=1, source_target_pairs={{0,1},{1,0},{2,3},{3,2},{4,5},{5,4},{6,7},{7,6}} | collective-permute-start | bytes 2359304 | tf_op jit(solution)/shard_map/ppermute | solution.py:255
  300.8 24.0 %collective-permute-start.39 = (bf16[384,1024]{1,0:T(8,128)(2,1)}, bf16[384,1024]{1,0:T(8,128)(2,1)}, u32[]{:S(2)}, u32[]{:S(2)}) collective-permute-start(bf16[384,1024]{1,0:T(8,128)(2,1)} %get-tuple-element.128), channel_id=1, source_target_pairs={{0,2},{2,0},{1,3},{3,1},{4,6},{6,4},{5,7},{7,5}} | collective-permute-start | bytes 2359304 | tf_op jit(solution)/shard_map/ppermute | solution.py:255
  313.3 116.6 %copy-start.21 = (bf16[48,1024]{1,0:T(8,128)(2,1)S(1)}, bf16[48,1024]{1,0:T(8,128)(2,1)}, u32[]{:S(2)}) copy-start(bf16[48,1024]{1,0:T(8,128)(2,1)} %get-tuple-element.126) | copy-start | bytes 294916
  324.3 113.2 %copy-start.11 = (bf16[128,3072]{1,0:T(8,128)(2,1)}, bf16[128,3072]{1,0:T(8,128)(2,1)S(1)}, u32[]{:S(2)}) copy-start(bf16[128,3072]{1,0:T(8,128)(2,1)S(1)} %collective-permute-done.9.corner) | copy-start | bytes 2359300
  324.3 6.5 %collective-permute-start.18 = (bf16[256,3072]{1,0:T(8,128)(2,1)}, bf16[256,3072]{1,0:T(8,128)(2,1)S(1)}, u32[]{:S(2)}, u32[]{:S(2)}) collective-permute-start(bf16[256,3072]{1,0:T(8,128)(2,1)} %get-tuple-element.100), channel_id=1, source_target_pairs={{0,1},{1,0},{2,3},{3,2},{4,5},{5,4},{6,7},{7,6}} | collective-permute-start | bytes 4718600 | tf_op jit(solution)/shard_map/ppermute | solution.py:255
  324.4 4.3 collective-permute-start.37
  324.9 37.6 %collective-permute-start.19 = (bf16[256,3072]{1,0:T(8,128)(2,1)}, bf16[256,3072]{1,0:T(8,128)(2,1)}, u32[]{:S(2)}, u32[]{:S(2)}) collective-permute-start(bf16[256,3072]{1,0:T(8,128)(2,1)} %get-tuple-element.100), channel_id=1, source_target_pairs={{0,2},{2,0},{1,3},{3,1},{4,6},{6,4},{5,7},{7,5}} | collective-permute-start | bytes 4718600 | tf_op jit(solution)/shard_map/ppermute | solution.py:255
  328.7 33.8 %collective-permute-start.21 = (bf16[256,3072]{1,0:T(8,128)(2,1)}, bf16[256,3072]{1,0:T(8,128)(2,1)S(1)}, u32[]{:S(2)}, u32[]{:S(2)}) collective-permute-start(bf16[256,3072]{1,0:T(8,128)(2,1)} %get-tuple-element.101), channel_id=1, source_target_pairs={{0,1},{1,0},{2,3},{3,2},{4,5},{5,4},{6,7},{7,6}} | collective-permute-start | bytes 4718600 | tf_op jit(solution)/shard_map/ppermute | solution.py:255
  328.8 67.2 %collective-permute-start.22 = (bf16[256,3072]{1,0:T(8,128)(2,1)}, bf16[256,3072]{1,0:T(8,128)(2,1)S(1)}, u32[]{:S(2)}, u32[]{:S(2)}) collective-permute-start(bf16[256,3072]{1,0:T(8,128)(2,1)} %get-tuple-element.101), channel_id=1, source_target_pairs={{0,2},{2,0},{1,3},{3,1},{4,6},{6,4},{5,7},{7,5}} | collective-permute-start | bytes 4718600 | tf_op jit(solution)/shard_map/ppermute | solution.py:255
  329.4 99.4 %collective-permute-start.42 = (bf16[768,1024]{1,0:T(8,128)(2,1)}, bf16[768,1024]{1,0:T(8,128)(2,1)S(1)}, u32[]{:S(2)}, u32[]{:S(2)}) collective-permute-start(bf16[768,1024]{1,0:T(8,128)(2,1)} %get-tuple-element.129), channel_id=1, source_target_pairs={{0,2},{2,0},{1,3},{3,1},{4,6},{6,4},{5,7},{7,5}} | collective-permute-start | bytes 4718600 | tf_op jit(solution)/shard_map/ppermute | solution.py:255
  330.8 99.1 %copy-start = (bf16[256,3072]{1,0:T(8,128)(2,1)}, bf16[256,3072]{1,0:T(8,128)(2,1)S(1)}, u32[]{:S(2)}) copy-start(bf16[256,3072]{1,0:T(8,128)(2,1)S(1)} %collective-permute-done.18.beside) | copy-start | bytes 4718596
  330.8 98.0 %collective-permute-start.40 = (bf16[384,1024]{1,0:T(8,128)(2,1)}, bf16[384,1024]{1,0:T(8,128)(2,1)S(1)}, u32[]{:S(2)}, u32[]{:S(2)}) collective-permute-start(bf16[384,1024]{1,0:T(8,128)(2,1)} %collective-permute-done.39.across), channel_id=1, source_target_pairs={{0,1},{1,0},{2,3},{3,2},{4,5},{5,4},{6,7},{7,6}} | collective-permute-start | bytes 2359304 | tf_op jit(solution)/shard_map/ppermute | solution.py:255
  362.4 66.9 %collective-permute-start.41 = (bf16[768,1024]{1,0:T(8,128)(2,1)}, bf16[768,1024]{1,0:T(8,128)(2,1)S(1)}, u32[]{:S(2)}, u32[]{:S(2)}) collective-permute-start(bf16[768,1024]{1,0:T(8,128)(2,1)} %get-tuple-element.129), channel_id=1, source_target_pairs={{0,1},{1,0},{2,3},{3,2},{4,5},{5,4},{6,7},{7,6}} | collective-permute-start | bytes 4718600 | tf_op jit(solution)/shard_map/ppermute | solution.py:255
  362.4 69.8 %copy-start.1 = (bf16[256,3072]{1,0:T(8,128)(2,1)}, bf16[256,3072]{1,0:T(8,128)(2,1)S(1)}, u32[]{:S(2)}) copy-start(bf16[256,3072]{1,0:T(8,128)(2,1)S(1)} %collective-permute-done.21.beside) | copy-start | bytes 4718596
  362.5 66.9 %collective-permute-start.6 = (bf16[256,3072]{1,0:T(8,128)(2,1)}, bf16[256,3072]{1,0:T(8,128)(2,1)S(1)}, u32[]{:S(2)}, u32[]{:S(2)}) collective-permute-start(bf16[256,3072]{1,0:T(8,128)(2,1)} %collective-permute-done.5.across), channel_id=1, source_target_pairs={{0,1},{1,0},{2,3},{3,2},{4,5},{5,4},{6,7},{7,6}} | collective-permute-start | bytes 4718600 | tf_op jit(solution)/shard_map/ppermute | solution.py:255
  396.0 36.3 %copy-start.3 = (bf16[256,3072]{1,0:T(8,128)(2,1)}, bf16[256,3072]{1,0:T(8,128)(2,1)S(1)}, u32[]{:S(2)}) copy-start(bf16[256,3072]{1,0:T(8,128)(2,1)S(1)} %collective-permute-done.22.across) | copy-start | bytes 4718596
  396.0 33.8 %collective-permute-start.23 = (bf16[256,3072]{1,0:T(8,128)(2,1)S(1)}, bf16[256,3072]{1,0:T(8,128)(2,1)S(1)}, u32[]{:S(2)}, u32[]{:S(2)}) collective-permute-start(bf16[256,3072]{1,0:T(8,128)(2,1)S(1)} %collective-permute-done.22.across), channel_id=1, source_target_pairs={{0,1},{1,0},{2,3},{3,2},{4,5},{5,4},{6,7},{7,6}} | collective-permute-start | bytes 4718600 | tf_op jit(solution)/shard_map/ppermute | solution.py:255
  428.8 3.6 copy-start.4
  428.8 3.4 collective-permute-start.43
  428.8 3.6 copy-start.12
  428.8 26.0 %collective-permute-start.20 = (bf16[256,3072]{1,0:T(8,128)(2,1)}, bf16[256,3072]{1,0:T(8,128)(2,1)}, u32[]{:S(2)}, u32[]{:S(2)}) collective-permute-start(bf16[256,3072]{1,0:T(8,128)(2,1)} %collective-permute-done.19.across), channel_id=1, source_target_pairs={{0,1},{1,0},{2,3},{3,2},{4,5},{5,4},{6,7},{7,6}} | collective-permute-start | bytes 4718600 | tf_op jit(solution)/shard_map/ppermute | solution.py:255
  429.3 3.0 copy-start.7
  429.3 29.1 %collective-permute-start.28 = (bf16[96,1024]{1,0:T(8,128)(2,1)S(1)}, bf16[96,1024]{1,0:T(8,128)(2,1)S(1)}, u32[]{:S(2)}, u32[]{:S(2)}) collective-permute-start(bf16[96,1024]{1,0:T(8,128)(2,1)S(1)} %copy-done.20), channel_id=1, source_target_pairs={{0,1},{1,0},{2,3},{3,2},{4,5},{5,4},{6,7},{7,6}} | collective-permute-start | bytes 589832 | tf_op jit(solution)/shard_map/ppermute | solution.py:255
  429.4 3.0 copy-start.5
  429.4 29.1 %collective-permute-start.30 = (bf16[96,1024]{1,0:T(8,128)(2,1)S(1)}, bf16[96,1024]{1,0:T(8,128)(2,1)S(1)}, u32[]{:S(2)}, u32[]{:S(2)}) collective-permute-start(bf16[96,1024]{1,0:T(8,128)(2,1)S(1)} %collective-permute-done.29.refs_1_), channel_id=1, source_target_pairs={{0,1},{1,0},{2,3},{3,2},{4,5},{5,4},{6,7},{7,6}} | collective-permute-start | bytes 589832 | tf_op jit(solution)/shard_map/ppermute | solution.py:255
  429.9 2.5 copy-start.6
  429.9 28.6 %collective-permute-start.32 = (bf16[48,1024]{1,0:T(8,128)(2,1)S(1)}, bf16[48,1024]{1,0:T(8,128)(2,1)S(1)}, u32[]{:S(2)}, u32[]{:S(2)}) collective-permute-start(bf16[48,1024]{1,0:T(8,128)(2,1)S(1)} %copy-done.21), channel_id=1, source_target_pairs={{0,1},{1,0},{2,3},{3,2},{4,5},{5,4},{6,7},{7,6}} | collective-permute-start | bytes 294920 | tf_op jit(solution)/shard_map/ppermute | solution.py:255
  432.2 1.1 copy-start.8
  432.2 26.2 %collective-permute-start.34 = (bf16[48,1024]{1,0:T(8,128)(2,1)S(1)}, bf16[48,1024]{1,0:T(8,128)(2,1)S(1)}, u32[]{:S(2)}, u32[]{:S(2)}) collective-permute-start(bf16[48,1024]{1,0:T(8,128)(2,1)S(1)} %collective-permute-done.33.refs_4_), channel_id=1, source_target_pairs={{0,1},{1,0},{2,3},{3,2},{4,5},{5,4},{6,7},{7,6}} | collective-permute-start | bytes 294920 | tf_op jit(solution)/shard_map/ppermute | solution.py:255
  (2 other events, 1.4 us)

commit v6 on v5

--- a/solution.py
+++ b/solution.py
@@ -110,7 +110,7 @@
 
 
 def pair_tile(rows, cols):
-    return math.gcd(rows, 32 * 3072 // cols)
+    return rows if rows * cols <= 96 * 3072 else math.gcd(rows, 64 * 3072 // cols)
 
 
 def pair(terms, index, nears):
@@ -150,7 +150,7 @@
 
 def adamw(me, terms, near, far, w, m, v, layer, first, rows, before):
     block, cols = m.shape[1], m.shape[2]
-    tile = math.gcd(rows, first, block, 32 * 3072 // cols)
+    tile = math.gcd(rows, first, block, 64 * 3072 // cols)
     at, per = first // tile, block // tile
     mine = pl.BlockSpec((1, tile, cols), lambda i, me: (layer, at + i, 0))
     whole = pl.BlockSpec((1, tile, cols), lambda i, me: (layer, me[0] * per + at + i, 0))
@@ -179,33 +179,32 @@
     )(me, terms, near, far, w, m, v, *before)
 
 
-def place_body(chunks, block, me, *refs):
-    pieces, (_, out, sem) = refs[: 3 * len(chunks)], refs[3 * len(chunks) :]
+def place_body(what, block, me, *refs):
+    pieces, (_, out, sem) = refs[:-3], refs[-3:]
     copies = []
-    for i, src in enumerate(pieces):
-        _, layer, first, rows = chunks[i // 3]
-        owner = me[0] ^ (1 + i % 3)
-        copies.append(pltpu.make_async_copy(src, out.at[layer, pl.ds(pl.multiple_of(owner * block + first, 16), rows)], sem.at[i]))
+    for i, ((c, other), src) in enumerate(zip(what, pieces, strict=True)):
+        _, layer, first, rows = CHUNKS[c]
+        to = out.at[layer, pl.ds(pl.multiple_of((me[0] ^ other) * block + first, 16), rows)]
+        copies.append(pltpu.make_async_copy(src, to, sem.at[i]))
     for copy in copies:
         copy.start()
     for copy in copies:
         copy.wait()
 
 
-def place(me, chunks, pieces, out, block):
-    cols = out.shape[2]
-    size = sum(chunk[3] for chunk in chunks) * cols
-    anywhere = pl.BlockSpec(memory_space=pl.ANY)
-    n = 3 * len(chunks)
-    return pl.pallas_call(
-        functools.partial(place_body, chunks, block),
+def place(me, what, pieces, out, block):
+    size = sum(piece.size for piece in pieces)
+    anywhere = pl.BlockSpec(memory_space=pl.ANY)
+    n = len(pieces)
+    return pl.pallas_call(
+        functools.partial(place_body, what, block),
         in_specs=[pl.BlockSpec(memory_space=pltpu.SMEM)] + [pl.BlockSpec(memory_space=pltpu.VMEM)] * n + [anywhere],
         out_specs=anywhere,
         out_shape=jax.ShapeDtypeStruct(out.shape, out.dtype),
         input_output_aliases={1 + n: 0},
         scratch_shapes=[pltpu.SemaphoreType.DMA((n,))],
         compiler_params=pltpu.CompilerParams(vmem_limit_bytes=16 * 2**20),
-        cost_estimate=pl.CostEstimate(flops=3 * size, bytes_accessed=12 * size, transcendentals=0),
+        cost_estimate=pl.CostEstimate(flops=size, bytes_accessed=4 * size, transcendentals=0),
         name="place",
     )(me, *pieces, out)
 
@@ -269,14 +268,22 @@
             beside.append(send(one, BESIDE))
         for c in range(len(CHUNKS)):
             corner.append(send(across[c], BESIDE))
+        came = {1: beside, 2: across, 3: corner}
         for c in range(LAST):
             which = CHUNKS[c][0]
-            together = (c,) if c < LAST - 1 else (c, LAST)
-            pieces = [got[i] for i in together for got in (beside, across, corner)]
+            what = ((c, 1), (c, 2), (c, 3))
+            if c == LAST - 2:
+                what += ((LAST - 1, 1), (LAST, 1))
+            if c == LAST - 1:
+                what = ((c, 2), (c, 3), (LAST, 2))
+            pieces = [came[other][i] for i, other in what]
             if c < LAST - 2:
                 state[which][0] = carry(me, CHUNKS[c], pieces, state[which][0], m[which].shape[1])
             else:
-                state[which][0] = place(me, [CHUNKS[i] for i in together], pieces, state[which][0], m[which].shape[1])
+                state[which][0] = place(me, what, pieces, state[which][0], m[which].shape[1])
+        which, layer, first, _ = CHUNKS[LAST]
+        row = (lax.axis_index("dp") ^ 3) * m[which].shape[1] + first
+        state[which][0] = lax.dynamic_update_slice(state[which][0], corner[LAST][None], (layer, row, 0))
         return tuple(state[which][i] for i in range(3) for which in range(3))
 
     all_of, cut_rows = P(None, None, None), P(None, "dp", None)

time: 461 us -> 467 us (1.013)
  waiting for transfers between devices: 276 us -> 290 us
  Pallas kernels: 150 us -> 139 us
    ppermute x44, waiting for transfers between devices: 276 us -> 290 us  [send(): return lax.ppermute(x, 'dp', to)]
    pallas_call x11, Pallas kernels: 76.3 us -> 66.5 us  [adamw(): pl.pallas_call(functools.partial(adamw_body, n_alias), grid_spec=pltpu.Pr...]
  transfers between devices with their start and end apart: 44 -> 44, of which waited for: 11 -> 10; matrix products, arithmetic and copies ran while one was open for 0% -> 0% of each run, Pallas kernels for 32% -> 29%
where the time goes in v6:
time: 467 us; the launch traced here: 466 us
  waiting for transfers between devices  290 us (62%)
  Pallas kernels  139 us (30%)
  starting transfers between devices  31.8 us (7%)
    ppermute x44, waiting for transfers between devices, send(): return lax.ppermute(x, 'dp', to)  290 us
    pallas_call x11, Pallas kernels, adamw(): pl.pallas_call(functools.partial(adamw_body, n_alias), grid_spec=pltpu.Pr...  66.5 us
    pallas_call x10, Pallas kernels, pair(): pl.pallas_call(functools.partial(pair_body, chunk, nears), in_specs=[anyw...  44.6 us
    ppermute x44, starting transfers between devices, send(): return lax.ppermute(x, 'dp', to)  31.8 us
    pallas_call x8, Pallas kernels, carry(): pl.pallas_call(functools.partial(carry_body, chunk, block), in_specs=[pl....  23.9 us
  transfers between devices with their start and end apart: 44, of which 10 were waited for; matrix products, arithmetic and copies ran while one was open for 0% of the time, Pallas kernels for 29%

profile of v6, /device:TPU:0, one launch (start us, length us, event | category | flops | bytes accessed | tf_op | source)
XLA Modules:
  0.0 465.8 jit_solution(9910148219339719483)
XLA Ops:
  0.6 3.4 pair.12
  4.0 3.0 collective-permute-start.2
  7.0 2.2 pair.19
  9.3 1.9 first_pair.1
  11.2 2.0 collective-permute-start.3
  13.2 3.0 pair.16
  16.3 2.4 pair.15
  18.8 2.0 collective-permute-start.24
  20.8 5.0 %pair.11 = (bf16[128,3072]{1,0:T(8,128)(2,1)}, bf16[48,3072]{1,0:T(8,128)(2,1)}, bf16[80,3072]{1,0:T(8,128)(2,1)}, bf16[128,3072]{1,0:T(8,128)(2,1)}) custom-call(bf16[1,2,1024,3072]{3,2,1,0:T(8,128)(2,1)} %refs_0_.19, bf16[1,2,1024,3072]{3,2,1,0:T(8,128)(2,1)} %refs_1_.19, bf16[1,2,3072,1024]{3,2,1,0:T(8,128)(2,1)} %own.21), custom_call_target="tpu_custom_call" | custom-call | flops 393216 | bytes 3932160 | tf_op jit(solution)/shard_map/pair/pallas_call | solution.py:123
  25.9 3.8 pair.17
  29.7 12.8 %collective-permute-done.24.far = bf16[96,1024]{1,0:T(8,128)(2,1)S(1)} collective-permute-done((bf16[96,1024]{1,0:T(8,128)(2,1)}, bf16[96,1024]{1,0:T(8,128)(2,1)S(1)}, u32[]{:S(2)}, u32[]{:S(2)}) %collective-permute-start.24) | collective-permute-done | bytes 196640 | tf_op jit(solution)/shard_map/ppermute | solution.py:254
  42.5 2.0 collective-permute-start.26
  44.5 6.2 %pair.18 = (bf16[768,1024]{1,0:T(8,128)(2,1)}, bf16[768,1024]{1,0:T(8,128)(2,1)}) custom-call(bf16[1,2,1024,3072]{3,2,1,0:T(8,128)(2,1)} %refs_0_.19, bf16[1,2,1024,3072]{3,2,1,0:T(8,128)(2,1)} %refs_1_.19, bf16[1,2,3072,1024]{3,2,1,0:T(8,128)(2,1)} %own.21), custom_call_target="tpu_custom_call" | custom-call | flops 786432 | bytes 7864320 | tf_op jit(solution)/shard_map/pair/pallas_call | solution.py:123
  50.8 0.7 copy-done.10
  51.4 3.9 adamw.11
  55.5 1.3 collective-permute-start.14
  56.8 5.7 %adamw.12 = (bf16[80,3072]{1,0:T(8,128)(2,1)}, bf16[2,1024,3072]{2,1,0:T(8,128)(2,1)}, f32[2,256,3072]{2,1,0:T(8,128)}, f32[2,256,3072]{2,1,0:T(8,128)}) custom-call(s32[1]{0:T(128)} %bitcast.me, bf16[1,2,1024,3072]{3,2,1,0:T(8,128)(2,1)} %refs_0_.19, ...), custom_call_target="tpu_custom_call", output_to_operand_aliasing={{1}: (7, {}), {2}: (8, {}), {3}: (9, {})} | custom-call | flops 3440640 | bytes 6881280 | tf_op jit(solution)/shard_map/adamw/pallas_call | solution.py:162
  62.7 53.0 %collective-permute-done.14.across = bf16[48,3072]{1,0:T(8,128)(2,1)} collective-permute-done((bf16[48,3072]{1,0:T(8,128)(2,1)}, bf16[48,3072]{1,0:T(8,128)(2,1)}, u32[]{:S(2)}, u32[]{:S(2)}) %collective-permute-start.14) | collective-permute-done | bytes 294944 | tf_op jit(solution)/shard_map/ppermute | solution.py:254
  115.7 1.8 collective-permute-start.11
  117.4 6.2 %pair.10 = (bf16[256,3072]{1,0:T(8,128)(2,1)}, bf16[256,3072]{1,0:T(8,128)(2,1)}) custom-call(bf16[1,2,1024,3072]{3,2,1,0:T(8,128)(2,1)} %refs_0_.19, bf16[1,2,1024,3072]{3,2,1,0:T(8,128)(2,1)} %refs_1_.19, bf16[1,2,3072,1024]{3,2,1,0:T(8,128)(2,1)} %own.21), custom_call_target="tpu_custom_call" | custom-call | flops 786432 | bytes 7864320 | tf_op jit(solution)/shard_map/pair/pallas_call | solution.py:123
  124.1 6.2 %pair.13 = (bf16[256,3072]{1,0:T(8,128)(2,1)}, bf16[256,3072]{1,0:T(8,128)(2,1)}) custom-call(bf16[1,2,1024,3072]{3,2,1,0:T(8,128)(2,1)} %refs_0_.19, bf16[1,2,1024,3072]{3,2,1,0:T(8,128)(2,1)} %refs_1_.19, bf16[1,2,3072,1024]{3,2,1,0:T(8,128)(2,1)} %own.21), custom_call_target="tpu_custom_call" | custom-call | flops 786432 | bytes 7864320 | tf_op jit(solution)/shard_map/pair/pallas_call | solution.py:123
  130.2 1.7 collective-permute-start.16
  131.9 6.2 %pair.14 = (bf16[256,3072]{1,0:T(8,128)(2,1)}, bf16[256,3072]{1,0:T(8,128)(2,1)}) custom-call(bf16[1,2,1024,3072]{3,2,1,0:T(8,128)(2,1)} %refs_0_.19, bf16[1,2,1024,3072]{3,2,1,0:T(8,128)(2,1)} %refs_1_.19, bf16[1,2,3072,1024]{3,2,1,0:T(8,128)(2,1)} %own.21), custom_call_target="tpu_custom_call" | custom-call | flops 786432 | bytes 7864320 | tf_op jit(solution)/shard_map/pair/pallas_call | solution.py:123
  138.5 4.9 %adamw.13 = (bf16[128,3072]{1,0:T(8,128)(2,1)}, bf16[2,1024,3072]{2,1,0:T(8,128)(2,1)}, f32[2,256,3072]{2,1,0:T(8,128)}, f32[2,256,3072]{2,1,0:T(8,128)}) custom-call(s32[1]{0:T(128)} %bitcast.me, bf16[1,2,1024,3072]{3,2,1,0:T(8,128)(2,1)} %refs_0_.19, ...), custom_call_target="tpu_custom_call", output_to_operand_aliasing={{1}: (7, {}), {2}: (8, {}), {3}: (9, {})} | custom-call | flops 5505024 | bytes 11010048 | tf_op jit(solution)/shard_map/adamw/pallas_call | solution.py:162
  143.4 0.5 collective-permute-start.7
  143.9 1.6 collective-permute-start.8
  145.6 9.2 %adamw.17 = (bf16[768,1024]{1,0:T(8,128)(2,1)}, bf16[2,3072,1024]{2,1,0:T(8,128)(2,1)}, f32[2,768,1024]{2,1,0:T(8,128)}, f32[2,768,1024]{2,1,0:T(8,128)}) custom-call(s32[1]{0:T(128)} %bitcast.me, bf16[1,2,3072,1024]{3,2,1,0:T(8,128)(2,1)} %own.21, bf16[768,1024]{1,0:T(8,128)(2,1)} %get-tuple-element.109.near, bf16[768,1024]{1,0:T(8,128)(2,1)} %copy-done.1, ...), custom_call_target="tpu_custom_call" | custom-call | flops 11010048 | bytes 22020096 | tf_op jit(solution)/shard_map/adamw/pallas_call | solution.py:162
  154.8 4.9 %adamw.18 = (bf16[384,1024]{1,0:T(8,128)(2,1)}, bf16[2,3072,1024]{2,1,0:T(8,128)(2,1)}, f32[2,768,1024]{2,1,0:T(8,128)}, f32[2,768,1024]{2,1,0:T(8,128)}) custom-call(s32[1]{0:T(128)} %bitcast.me, bf16[1,2,3072,1024]{3,2,1,0:T(8,128)(2,1)} %own.21, ...), custom_call_target="tpu_custom_call", output_to_operand_aliasing={{1}: (7, {}), {2}: (8, {}), {3}: (9, {})} | custom-call | flops 5505024 | bytes 11010048 | tf_op jit(solution)/shard_map/adamw/pallas_call | solution.py:162
  159.7 5.7 %adamw.19 = (bf16[240,1024]{1,0:T(8,128)(2,1)}, bf16[2,3072,1024]{2,1,0:T(8,128)(2,1)}, f32[2,768,1024]{2,1,0:T(8,128)}, f32[2,768,1024]{2,1,0:T(8,128)}) custom-call(s32[1]{0:T(128)} %bitcast.me, bf16[1,2,3072,1024]{3,2,1,0:T(8,128)(2,1)} %own.21, ...), custom_call_target="tpu_custom_call", output_to_operand_aliasing={{1}: (7, {}), {2}: (8, {}), {3}: (9, {})} | custom-call | flops 3440640 | bytes 6881280 | tf_op jit(solution)/shard_map/adamw/pallas_call | solution.py:162
  165.4 2.5 adamw.20
  167.9 1.1 collective-permute-start.28
  169.1 79.0 %collective-permute-done.8.across = bf16[128,3072]{1,0:T(8,128)(2,1)} collective-permute-done((bf16[128,3072]{1,0:T(8,128)(2,1)}, bf16[128,3072]{1,0:T(8,128)(2,1)}, u32[]{:S(2)}, u32[]{:S(2)}) %collective-permute-start.8) | collective-permute-done | bytes 786464 | tf_op jit(solution)/shard_map/ppermute | solution.py:254
  248.1 2.2 adamw.21
  250.2 1.7 collective-permute-start.31
  252.2 3.4 collective-permute-done.31.refs_2_
  255.7 9.2 %adamw.14 = (bf16[256,3072]{1,0:T(8,128)(2,1)}, bf16[2,1024,3072]{2,1,0:T(8,128)(2,1)}, f32[2,256,3072]{2,1,0:T(8,128)}, f32[2,256,3072]{2,1,0:T(8,128)}) custom-call(s32[1]{0:T(128)} %bitcast.me, bf16[1,2,1024,3072]{3,2,1,0:T(8,128)(2,1)} %refs_0_.19, ...), custom_call_target="tpu_custom_call", output_to_operand_aliasing={{1}: (7, {}), {2}: (8, {}), {3}: (9, {})} | custom-call | flops 11010048 | bytes 22020096 | tf_op jit(solution)/shard_map/adamw/pallas_call | solution.py:162
  264.9 0.5 collective-permute-start.4
  265.4 1.7 collective-permute-start.5
  267.1 1.8 collective-permute-done.29.refs_1_
  268.9 1.7 collective-permute-start.33
  270.7 41.7 %collective-permute-done.33.refs_1_ = bf16[240,1024]{1,0:T(8,128)(2,1)S(1)} collective-permute-done((bf16[240,1024]{1,0:T(8,128)(2,1)}, bf16[240,1024]{1,0:T(8,128)(2,1)S(1)}, u32[]{:S(2)}, u32[]{:S(2)}) %collective-permute-start.33) | collective-permute-done | bytes 491552 | tf_op jit(solution)/shard_map/ppermute | solution.py:254
  312.5 1.7 collective-permute-start.38
  314.2 9.2 %adamw.15 = (bf16[256,3072]{1,0:T(8,128)(2,1)}, bf16[2,1024,3072]{2,1,0:T(8,128)(2,1)}, f32[2,256,3072]{2,1,0:T(8,128)}, f32[2,256,3072]{2,1,0:T(8,128)}) custom-call(s32[1]{0:T(128)} %bitcast.me, bf16[1,2,1024,3072]{3,2,1,0:T(8,128)(2,1)} %refs_1_.19, bf16[256,3072]{1,0:T(8,128)(2,1)} %get-tuple-element.95.near, bf16[256,3072]{1,0:T(8,128)(2,1)} %copy-done, ...), custom_call_target="tpu_custom_call" | custom-call | flops 11010048 | bytes 22020096 | tf_op jit(solution)/shard_map/adamw/pallas_call | solution.py:162
  323.4 9.2 %adamw.16 = (bf16[256,3072]{1,0:T(8,128)(2,1)}, bf16[2,1024,3072]{2,1,0:T(8,128)(2,1)}, f32[2,256,3072]{2,1,0:T(8,128)}, f32[2,256,3072]{2,1,0:T(8,128)}) custom-call(s32[1]{0:T(128)} %bitcast.me, bf16[1,2,1024,3072]{3,2,1,0:T(8,128)(2,1)} %refs_1_.19, ...), custom_call_target="tpu_custom_call", output_to_operand_aliasing={{1}: (7, {}), {2}: (8, {}), {3}: (9, {})} | custom-call | flops 11010048 | bytes 22020096 | tf_op jit(solution)/shard_map/adamw/pallas_call | solution.py:162
  332.9 1.8 collective-permute-start.41
  334.7 1.8 collective-permute-start.22
  336.5 0.5 collective-permute-start.6
  337.0 33.2 %collective-permute-done.19.across = bf16[256,3072]{1,0:T(8,128)(2,1)} collective-permute-done((bf16[256,3072]{1,0:T(8,128)(2,1)}, bf16[256,3072]{1,0:T(8,128)(2,1)}, u32[]{:S(2)}, u32[]{:S(2)}) %collective-permute-start.19) | collective-permute-done | bytes 1572896 | tf_op jit(solution)/shard_map/ppermute | solution.py:254
  370.2 33.6 %collective-permute-done.41.across = bf16[768,1024]{1,0:T(8,128)(2,1)S(1)} collective-permute-done((bf16[768,1024]{1,0:T(8,128)(2,1)}, bf16[768,1024]{1,0:T(8,128)(2,1)S(1)}, u32[]{:S(2)}, u32[]{:S(2)}) %collective-permute-start.41) | collective-permute-done | bytes 1572896 | tf_op jit(solution)/shard_map/ppermute | solution.py:254
  403.8 31.7 %collective-permute-done.22.across = bf16[256,3072]{1,0:T(8,128)(2,1)} collective-permute-done((bf16[256,3072]{1,0:T(8,128)(2,1)}, bf16[256,3072]{1,0:T(8,128)(2,1)}, u32[]{:S(2)}, u32[]{:S(2)}) %collective-permute-start.22) | collective-permute-done | bytes 1572896 | tf_op jit(solution)/shard_map/ppermute | solution.py:254
  435.5 0.5 collective-permute-start.23
  436.5 0.7 copy-done.2
  437.7 1.2 copy-done.5
  439.1 1.9 carry.8.before
  441.0 2.2 carry.9.before
  443.3 3.6 carry.14.before
  446.9 2.6 carry.15.refs_5_
  449.5 1.2 place.2.refs_3_
  450.7 2.6 carry.10.before
  453.3 0.8 place.3
  454.2 3.6 carry.11
  457.8 3.6 carry.12.before
  461.5 3.6 carry.13
  465.2 0.7 bitcast_dynamic-update-slice_fusion
  (85 shorter events, 3.4 us)
Async XLA Ops:
  4.0 51.3 %collective-permute-start.2 = (bf16[80,3072]{1,0:T(8,128)(2,1)}, bf16[80,3072]{1,0:T(8,128)(2,1)}, u32[]{:S(2)}, u32[]{:S(2)}) collective-permute-start(bf16[80,3072]{1,0:T(8,128)(2,1)} %pair.12), channel_id=1, source_target_pairs={{0,2},{2,0},{1,3},{3,1},{4,6},{6,4},{5,7},{7,5}} | collective-permute-start | bytes 1474568 | tf_op jit(solution)/shard_map/ppermute | solution.py:254
  9.3 16.5 %collective-permute-start.30 = (bf16[48,1024]{1,0:T(8,128)(2,1)}, bf16[48,1024]{1,0:T(8,128)(2,1)S(1)}, u32[]{:S(2)}, u32[]{:S(2)}) collective-permute-start(bf16[48,1024]{1,0:T(8,128)(2,1)} %get-tuple-element.122), channel_id=1, source_target_pairs={{0,2},{2,0},{1,3},{3,1},{4,6},{6,4},{5,7},{7,5}} | collective-permute-start | bytes 294920 | tf_op jit(solution)/shard_map/ppermute | solution.py:254
  11.2 39.5 %collective-permute-start.3 = (bf16[48,3072]{1,0:T(8,128)(2,1)S(1)}, bf16[48,3072]{1,0:T(8,128)(2,1)S(1)}, u32[]{:S(2)}, u32[]{:S(2)}) collective-permute-start(bf16[48,3072]{1,0:T(8,128)(2,1)S(1)} %first_pair.1), channel_id=1, source_target_pairs={{0,2},{2,0},{1,3},{3,1},{4,6},{6,4},{5,7},{7,5}} | collective-permute-start | bytes 884744 | tf_op jit(solution)/shard_map/ppermute | solution.py:254
  16.3 39.3 %collective-permute-start.25 = (bf16[240,1024]{1,0:T(8,128)(2,1)}, bf16[240,1024]{1,0:T(8,128)(2,1)}, u32[]{:S(2)}, u32[]{:S(2)}) collective-permute-start(bf16[240,1024]{1,0:T(8,128)(2,1)} %get-tuple-element.106), channel_id=1, source_target_pairs={{0,2},{2,0},{1,3},{3,1},{4,6},{6,4},{5,7},{7,5}} | collective-permute-start | bytes 1474568 | tf_op jit(solution)/shard_map/ppermute | solution.py:254
  18.8 23.7 %collective-permute-start.24 = (bf16[96,1024]{1,0:T(8,128)(2,1)}, bf16[96,1024]{1,0:T(8,128)(2,1)S(1)}, u32[]{:S(2)}, u32[]{:S(2)}) collective-permute-start(bf16[96,1024]{1,0:T(8,128)(2,1)} %get-tuple-element.104), channel_id=1, source_target_pairs={{0,2},{2,0},{1,3},{3,1},{4,6},{6,4},{5,7},{7,5}} | collective-permute-start | bytes 589832 | tf_op jit(solution)/shard_map/ppermute | solution.py:254
  25.8 3.9 copy-start.13
  25.8 89.9 %collective-permute-start.1 = (bf16[128,3072]{1,0:T(8,128)(2,1)}, bf16[128,3072]{1,0:T(8,128)(2,1)S(1)}, u32[]{:S(2)}, u32[]{:S(2)}) collective-permute-start(bf16[128,3072]{1,0:T(8,128)(2,1)} %get-tuple-element.76), channel_id=1, source_target_pairs={{0,2},{2,0},{1,3},{3,1},{4,6},{6,4},{5,7},{7,5}} | collective-permute-start | bytes 2359304 | tf_op jit(solution)/shard_map/ppermute | solution.py:254
  42.5 8.2 %copy-start.12 = (bf16[96,1024]{1,0:T(8,128)(2,1)}, bf16[96,1024]{1,0:T(8,128)(2,1)S(1)}, u32[]{:S(2)}) copy-start(bf16[96,1024]{1,0:T(8,128)(2,1)S(1)} %collective-permute-done.24.far) | copy-start | bytes 589828
  42.5 81.1 %collective-permute-start.26 = (bf16[384,1024]{1,0:T(8,128)(2,1)}, bf16[384,1024]{1,0:T(8,128)(2,1)S(1)}, u32[]{:S(2)}, u32[]{:S(2)}) collective-permute-start(bf16[384,1024]{1,0:T(8,128)(2,1)} %get-tuple-element.108), channel_id=1, source_target_pairs={{0,2},{2,0},{1,3},{3,1},{4,6},{6,4},{5,7},{7,5}} | collective-permute-start | bytes 2359304 | tf_op jit(solution)/shard_map/ppermute | solution.py:254
  50.7 0.7 copy-start.10
  50.7 93.2 %collective-permute-start.27 = (bf16[768,1024]{1,0:T(8,128)(2,1)}, bf16[768,1024]{1,0:T(8,128)(2,1)S(1)}, u32[]{:S(2)}, u32[]{:S(2)}) collective-permute-start(bf16[768,1024]{1,0:T(8,128)(2,1)} %get-tuple-element.110), channel_id=1, source_target_pairs={{0,2},{2,0},{1,3},{3,1},{4,6},{6,4},{5,7},{7,5}} | collective-permute-start | bytes 4718600 | tf_op jit(solution)/shard_map/ppermute | solution.py:254
  55.4 7.1 %collective-permute-start.13 = (bf16[48,3072]{1,0:T(8,128)(2,1)}, bf16[48,3072]{1,0:T(8,128)(2,1)S(1)}, u32[]{:S(2)}, u32[]{:S(2)}) collective-permute-start(bf16[48,3072]{1,0:T(8,128)(2,1)} %get-tuple-element.91), channel_id=1, source_target_pairs={{0,1},{1,0},{2,3},{3,2},{4,5},{5,4},{6,7},{7,6}} | collective-permute-start | bytes 884744 | tf_op jit(solution)/shard_map/ppermute | solution.py:254
  55.5 60.1 %collective-permute-start.14 = (bf16[48,3072]{1,0:T(8,128)(2,1)}, bf16[48,3072]{1,0:T(8,128)(2,1)}, u32[]{:S(2)}, u32[]{:S(2)}) collective-permute-start(bf16[48,3072]{1,0:T(8,128)(2,1)} %get-tuple-element.91), channel_id=1, source_target_pairs={{0,2},{2,0},{1,3},{3,1},{4,6},{6,4},{5,7},{7,5}} | collective-permute-start | bytes 884744 | tf_op jit(solution)/shard_map/ppermute | solution.py:254
  62.5 61.1 %copy-start.11 = (bf16[48,3072]{1,0:T(8,128)(2,1)}, bf16[48,3072]{1,0:T(8,128)(2,1)S(1)}, u32[]{:S(2)}) copy-start(bf16[48,3072]{1,0:T(8,128)(2,1)S(1)} %collective-permute-done.13.beside) | copy-start | bytes 884740
  62.5 75.6 %collective-permute-start.10 = (bf16[80,3072]{1,0:T(8,128)(2,1)}, bf16[80,3072]{1,0:T(8,128)(2,1)}, u32[]{:S(2)}, u32[]{:S(2)}) collective-permute-start(bf16[80,3072]{1,0:T(8,128)(2,1)} %get-tuple-element.90), channel_id=1, source_target_pairs={{0,1},{1,0},{2,3},{3,2},{4,5},{5,4},{6,7},{7,6}} | collective-permute-start | bytes 1474568 | tf_op jit(solution)/shard_map/ppermute | solution.py:254
  115.7 14.6 %collective-permute-start.15 = (bf16[48,3072]{1,0:T(8,128)(2,1)}, bf16[48,3072]{1,0:T(8,128)(2,1)}, u32[]{:S(2)}, u32[]{:S(2)}) collective-permute-start(bf16[48,3072]{1,0:T(8,128)(2,1)} %collective-permute-done.14.across), channel_id=1, source_target_pairs={{0,1},{1,0},{2,3},{3,2},{4,5},{5,4},{6,7},{7,6}} | collective-permute-start | bytes 884744 | tf_op jit(solution)/shard_map/ppermute | solution.py:254
  115.7 7.9 %copy-start.7 = (bf16[128,3072]{1,0:T(8,128)(2,1)}, bf16[128,3072]{1,0:T(8,128)(2,1)S(1)}, u32[]{:S(2)}) copy-start(bf16[128,3072]{1,0:T(8,128)(2,1)S(1)} %collective-permute-done.1.far) | copy-start | bytes 2359300
  115.7 22.8 %collective-permute-start.11 = (bf16[80,3072]{1,0:T(8,128)(2,1)}, bf16[80,3072]{1,0:T(8,128)(2,1)}, u32[]{:S(2)}, u32[]{:S(2)}) collective-permute-start(bf16[80,3072]{1,0:T(8,128)(2,1)} %get-tuple-element.90), channel_id=1, source_target_pairs={{0,2},{2,0},{1,3},{3,1},{4,6},{6,4},{5,7},{7,5}} | collective-permute-start | bytes 1474568 | tf_op jit(solution)/shard_map/ppermute | solution.py:254
  123.6 6.6 %copy-start.6 = (bf16[384,1024]{1,0:T(8,128)(2,1)}, bf16[384,1024]{1,0:T(8,128)(2,1)S(1)}, u32[]{:S(2)}) copy-start(bf16[384,1024]{1,0:T(8,128)(2,1)S(1)} %collective-permute-done.26.far) | copy-start | bytes 2359300
  123.6 41.8 %collective-permute-start = (bf16[256,3072]{1,0:T(8,128)(2,1)}, bf16[256,3072]{1,0:T(8,128)(2,1)}, u32[]{:S(2)}, u32[]{:S(2)}) collective-permute-start(bf16[256,3072]{1,0:T(8,128)(2,1)} %get-tuple-element.74), channel_id=1, source_target_pairs={{0,2},{2,0},{1,3},{3,1},{4,6},{6,4},{5,7},{7,5}} | collective-permute-start | bytes 4718600 | tf_op jit(solution)/shard_map/ppermute | solution.py:254
  130.2 120.0 %collective-permute-start.16 = (bf16[256,3072]{1,0:T(8,128)(2,1)}, bf16[256,3072]{1,0:T(8,128)(2,1)}, u32[]{:S(2)}, u32[]{:S(2)}) collective-permute-start(bf16[256,3072]{1,0:T(8,128)(2,1)} %get-tuple-element.94), channel_id=1, source_target_pairs={{0,2},{2,0},{1,3},{3,1},{4,6},{6,4},{5,7},{7,5}} | collective-permute-start | bytes 4718600 | tf_op jit(solution)/shard_map/ppermute | solution.py:254
  138.1 113.9 %collective-permute-start.17 = (bf16[256,3072]{1,0:T(8,128)(2,1)}, bf16[256,3072]{1,0:T(8,128)(2,1)S(1)}, u32[]{:S(2)}, u32[]{:S(2)}) collective-permute-start(bf16[256,3072]{1,0:T(8,128)(2,1)} %get-tuple-element.96), channel_id=1, source_target_pairs={{0,2},{2,0},{1,3},{3,1},{4,6},{6,4},{5,7},{7,5}} | collective-permute-start | bytes 4718600 | tf_op jit(solution)/shard_map/ppermute | solution.py:254
  138.5 4.9 %collective-permute-start.12 = (bf16[80,3072]{1,0:T(8,128)(2,1)}, bf16[80,3072]{1,0:T(8,128)(2,1)}, u32[]{:S(2)}, u32[]{:S(2)}) collective-permute-start(bf16[80,3072]{1,0:T(8,128)(2,1)} %collective-permute-done.11.across), channel_id=1, source_target_pairs={{0,1},{1,0},{2,3},{3,2},{4,5},{5,4},{6,7},{7,6}} | collective-permute-start | bytes 1474568 | tf_op jit(solution)/shard_map/ppermute | solution.py:254
  143.4 24.5 %collective-permute-start.7 = (bf16[128,3072]{1,0:T(8,128)(2,1)}, bf16[128,3072]{1,0:T(8,128)(2,1)}, u32[]{:S(2)}, u32[]{:S(2)}) collective-permute-start(bf16[128,3072]{1,0:T(8,128)(2,1)} %get-tuple-element.89), channel_id=1, source_target_pairs={{0,1},{1,0},{2,3},{3,2},{4,5},{5,4},{6,7},{7,6}} | collective-permute-start | bytes 2359304 | tf_op jit(solution)/shard_map/ppermute | solution.py:254
  143.9 1.6 copy-start.1
  143.9 104.1 %collective-permute-start.8 = (bf16[128,3072]{1,0:T(8,128)(2,1)}, bf16[128,3072]{1,0:T(8,128)(2,1)}, u32[]{:S(2)}, u32[]{:S(2)}) collective-permute-start(bf16[128,3072]{1,0:T(8,128)(2,1)} %get-tuple-element.89), channel_id=1, source_target_pairs={{0,2},{2,0},{1,3},{3,1},{4,6},{6,4},{5,7},{7,5}} | collective-permute-start | bytes 2359304 | tf_op jit(solution)/shard_map/ppermute | solution.py:254
  165.4 105.2 %collective-permute-start.32 = (bf16[240,1024]{1,0:T(8,128)(2,1)}, bf16[240,1024]{1,0:T(8,128)(2,1)S(1)}, u32[]{:S(2)}, u32[]{:S(2)}) collective-permute-start(bf16[240,1024]{1,0:T(8,128)(2,1)} %get-tuple-element.127), channel_id=1, source_target_pairs={{0,1},{1,0},{2,3},{3,2},{4,5},{5,4},{6,7},{7,6}} | collective-permute-start | bytes 1474568 | tf_op jit(solution)/shard_map/ppermute | solution.py:254
  167.9 97.5 %collective-permute-start.28 = (bf16[96,1024]{1,0:T(8,128)(2,1)}, bf16[96,1024]{1,0:T(8,128)(2,1)S(1)}, u32[]{:S(2)}, u32[]{:S(2)}) collective-permute-start(bf16[96,1024]{1,0:T(8,128)(2,1)} %get-tuple-element.120), channel_id=1, source_target_pairs={{0,2},{2,0},{1,3},{3,1},{4,6},{6,4},{5,7},{7,5}} | collective-permute-start | bytes 589832 | tf_op jit(solution)/shard_map/ppermute | solution.py:254
  248.1 19.0 %collective-permute-start.35 = (bf16[96,1024]{1,0:T(8,128)(2,1)}, bf16[96,1024]{1,0:T(8,128)(2,1)S(1)}, u32[]{:S(2)}, u32[]{:S(2)}) collective-permute-start(bf16[96,1024]{1,0:T(8,128)(2,1)} %get-tuple-element.120), channel_id=1, source_target_pairs={{0,1},{1,0},{2,3},{3,2},{4,5},{5,4},{6,7},{7,6}} | collective-permute-start | bytes 589832 | tf_op jit(solution)/shard_map/ppermute | solution.py:254
  250.2 5.4 %collective-permute-start.31 = (bf16[48,1024]{1,0:T(8,128)(2,1)}, bf16[48,1024]{1,0:T(8,128)(2,1)S(1)}, u32[]{:S(2)}, u32[]{:S(2)}) collective-permute-start(bf16[48,1024]{1,0:T(8,128)(2,1)} %get-tuple-element.126), channel_id=1, source_target_pairs={{0,2},{2,0},{1,3},{3,1},{4,6},{6,4},{5,7},{7,5}} | collective-permute-start | bytes 294920 | tf_op jit(solution)/shard_map/ppermute | solution.py:254
  252.0 12.9 %copy-start = (bf16[256,3072]{1,0:T(8,128)(2,1)}, bf16[256,3072]{1,0:T(8,128)(2,1)S(1)}, u32[]{:S(2)}) copy-start(bf16[256,3072]{1,0:T(8,128)(2,1)S(1)} %collective-permute-done.17.far) | copy-start | bytes 4718596
  252.0 12.9 %collective-permute-start.36 = (bf16[48,1024]{1,0:T(8,128)(2,1)}, bf16[48,1024]{1,0:T(8,128)(2,1)S(1)}, u32[]{:S(2)}, u32[]{:S(2)}) collective-permute-start(bf16[48,1024]{1,0:T(8,128)(2,1)} %get-tuple-element.126), channel_id=1, source_target_pairs={{0,1},{1,0},{2,3},{3,2},{4,5},{5,4},{6,7},{7,6}} | collective-permute-start | bytes 294920 | tf_op jit(solution)/shard_map/ppermute | solution.py:254
  255.7 76.9 %collective-permute-start.9 = (bf16[128,3072]{1,0:T(8,128)(2,1)}, bf16[128,3072]{1,0:T(8,128)(2,1)}, u32[]{:S(2)}, u32[]{:S(2)}) collective-permute-start(bf16[128,3072]{1,0:T(8,128)(2,1)} %collective-permute-done.8.across), channel_id=1, source_target_pairs={{0,1},{1,0},{2,3},{3,2},{4,5},{5,4},{6,7},{7,6}} | collective-permute-start | bytes 2359304 | tf_op jit(solution)/shard_map/ppermute | solution.py:254
  264.9 71.6 %collective-permute-start.4 = (bf16[256,3072]{1,0:T(8,128)(2,1)}, bf16[256,3072]{1,0:T(8,128)(2,1)}, u32[]{:S(2)}, u32[]{:S(2)}) collective-permute-start(bf16[256,3072]{1,0:T(8,128)(2,1)} %get-tuple-element.88), channel_id=1, source_target_pairs={{0,1},{1,0},{2,3},{3,2},{4,5},{5,4},{6,7},{7,6}} | collective-permute-start | bytes 4718600 | tf_op jit(solution)/shard_map/ppermute | solution.py:254
  265.4 71.1 %collective-permute-start.5 = (bf16[256,3072]{1,0:T(8,128)(2,1)}, bf16[256,3072]{1,0:T(8,128)(2,1)}, u32[]{:S(2)}, u32[]{:S(2)}) collective-permute-start(bf16[256,3072]{1,0:T(8,128)(2,1)} %get-tuple-element.88), channel_id=1, source_target_pairs={{0,2},{2,0},{1,3},{3,1},{4,6},{6,4},{5,7},{7,5}} | collective-permute-start | bytes 4718600 | tf_op jit(solution)/shard_map/ppermute | solution.py:254
  267.1 1.8 collective-permute-start.29
  268.9 43.6 %collective-permute-start.33 = (bf16[240,1024]{1,0:T(8,128)(2,1)}, bf16[240,1024]{1,0:T(8,128)(2,1)S(1)}, u32[]{:S(2)}, u32[]{:S(2)}) collective-permute-start(bf16[240,1024]{1,0:T(8,128)(2,1)} %get-tuple-element.127), channel_id=1, source_target_pairs={{0,2},{2,0},{1,3},{3,1},{4,6},{6,4},{5,7},{7,5}} | collective-permute-start | bytes 1474568 | tf_op jit(solution)/shard_map/ppermute | solution.py:254
  270.6 62.2 %collective-permute-start.37 = (bf16[384,1024]{1,0:T(8,128)(2,1)}, bf16[384,1024]{1,0:T(8,128)(2,1)S(1)}, u32[]{:S(2)}, u32[]{:S(2)}) collective-permute-start(bf16[384,1024]{1,0:T(8,128)(2,1)} %get-tuple-element.128), channel_id=1, source_target_pairs={{0,1},{1,0},{2,3},{3,2},{4,5},{5,4},{6,7},{7,6}} | collective-permute-start | bytes 2359304 | tf_op jit(solution)/shard_map/ppermute | solution.py:254
  312.5 20.4 %collective-permute-start.38 = (bf16[384,1024]{1,0:T(8,128)(2,1)}, bf16[384,1024]{1,0:T(8,128)(2,1)}, u32[]{:S(2)}, u32[]{:S(2)}) collective-permute-start(bf16[384,1024]{1,0:T(8,128)(2,1)} %get-tuple-element.128), channel_id=1, source_target_pairs={{0,2},{2,0},{1,3},{3,1},{4,6},{6,4},{5,7},{7,5}} | collective-permute-start | bytes 2359304 | tf_op jit(solution)/shard_map/ppermute | solution.py:254
  332.6 37.6 %collective-permute-start.19 = (bf16[256,3072]{1,0:T(8,128)(2,1)}, bf16[256,3072]{1,0:T(8,128)(2,1)}, u32[]{:S(2)}, u32[]{:S(2)}) collective-permute-start(bf16[256,3072]{1,0:T(8,128)(2,1)} %get-tuple-element.100), channel_id=1, source_target_pairs={{0,2},{2,0},{1,3},{3,1},{4,6},{6,4},{5,7},{7,5}} | collective-permute-start | bytes 4718600 | tf_op jit(solution)/shard_map/ppermute | solution.py:254
  332.9 110.4 %copy-start.8 = (bf16[384,1024]{1,0:T(8,128)(2,1)}, bf16[384,1024]{1,0:T(8,128)(2,1)S(1)}, u32[]{:S(2)}) copy-start(bf16[384,1024]{1,0:T(8,128)(2,1)S(1)} %collective-permute-done.37.beside) | copy-start | bytes 2359300
  332.9 1.9 collective-permute-start.34
  332.9 70.9 %collective-permute-start.41 = (bf16[768,1024]{1,0:T(8,128)(2,1)}, bf16[768,1024]{1,0:T(8,128)(2,1)S(1)}, u32[]{:S(2)}, u32[]{:S(2)}) collective-permute-start(bf16[768,1024]{1,0:T(8,128)(2,1)} %get-tuple-element.129), channel_id=1, source_target_pairs={{0,2},{2,0},{1,3},{3,1},{4,6},{6,4},{5,7},{7,5}} | collective-permute-start | bytes 4718600 | tf_op jit(solution)/shard_map/ppermute | solution.py:254
  334.7 100.8 %collective-permute-start.22 = (bf16[256,3072]{1,0:T(8,128)(2,1)}, bf16[256,3072]{1,0:T(8,128)(2,1)}, u32[]{:S(2)}, u32[]{:S(2)}) collective-permute-start(bf16[256,3072]{1,0:T(8,128)(2,1)} %get-tuple-element.101), channel_id=1, source_target_pairs={{0,2},{2,0},{1,3},{3,1},{4,6},{6,4},{5,7},{7,5}} | collective-permute-start | bytes 4718600 | tf_op jit(solution)/shard_map/ppermute | solution.py:254
  336.5 99.5 %collective-permute-start.40 = (bf16[768,1024]{1,0:T(8,128)(2,1)}, bf16[768,1024]{1,0:T(8,128)(2,1)S(1)}, u32[]{:S(2)}, u32[]{:S(2)}) collective-permute-start(bf16[768,1024]{1,0:T(8,128)(2,1)} %get-tuple-element.129), channel_id=1, source_target_pairs={{0,1},{1,0},{2,3},{3,2},{4,5},{5,4},{6,7},{7,6}} | collective-permute-start | bytes 4718600 | tf_op jit(solution)/shard_map/ppermute | solution.py:254
  336.5 99.6 %collective-permute-start.6 = (bf16[256,3072]{1,0:T(8,128)(2,1)}, bf16[256,3072]{1,0:T(8,128)(2,1)S(1)}, u32[]{:S(2)}, u32[]{:S(2)}) collective-permute-start(bf16[256,3072]{1,0:T(8,128)(2,1)} %collective-permute-done.5.across), channel_id=1, source_target_pairs={{0,1},{1,0},{2,3},{3,2},{4,5},{5,4},{6,7},{7,6}} | collective-permute-start | bytes 4718600 | tf_op jit(solution)/shard_map/ppermute | solution.py:254
  370.2 65.3 %collective-permute-start.39 = (bf16[384,1024]{1,0:T(8,128)(2,1)}, bf16[384,1024]{1,0:T(8,128)(2,1)S(1)}, u32[]{:S(2)}, u32[]{:S(2)}) collective-permute-start(bf16[384,1024]{1,0:T(8,128)(2,1)} %collective-permute-done.38.across), channel_id=1, source_target_pairs={{0,1},{1,0},{2,3},{3,2},{4,5},{5,4},{6,7},{7,6}} | collective-permute-start | bytes 2359304 | tf_op jit(solution)/shard_map/ppermute | solution.py:254
  403.8 33.5 %copy-start.3 = (bf16[768,1024]{1,0:T(8,128)(2,1)}, bf16[768,1024]{1,0:T(8,128)(2,1)S(1)}, u32[]{:S(2)}) copy-start(bf16[768,1024]{1,0:T(8,128)(2,1)S(1)} %collective-permute-done.41.across) | copy-start | bytes 4718596
  403.8 33.5 %collective-permute-start.42 = (bf16[768,1024]{1,0:T(8,128)(2,1)S(1)}, bf16[768,1024]{1,0:T(8,128)(2,1)S(1)}, u32[]{:S(2)}, u32[]{:S(2)}) collective-permute-start(bf16[768,1024]{1,0:T(8,128)(2,1)S(1)} %collective-permute-done.41.across), channel_id=1, source_target_pairs={{0,1},{1,0},{2,3},{3,2},{4,5},{5,4},{6,7},{7,6}} | collective-permute-start | bytes 4718600 | tf_op jit(solution)/shard_map/ppermute | solution.py:254
  435.5 22.3 %collective-permute-start.21 = (bf16[256,3072]{1,0:T(8,128)(2,1)}, bf16[256,3072]{1,0:T(8,128)(2,1)}, u32[]{:S(2)}, u32[]{:S(2)}) collective-permute-start(bf16[256,3072]{1,0:T(8,128)(2,1)} %get-tuple-element.101), channel_id=1, source_target_pairs={{0,1},{1,0},{2,3},{3,2},{4,5},{5,4},{6,7},{7,6}} | collective-permute-start | bytes 4718600 | tf_op jit(solution)/shard_map/ppermute | solution.py:254
  435.5 1.8 copy-start.9
  435.5 22.3 %collective-permute-start.23 = (bf16[256,3072]{1,0:T(8,128)(2,1)}, bf16[256,3072]{1,0:T(8,128)(2,1)}, u32[]{:S(2)}, u32[]{:S(2)}) collective-permute-start(bf16[256,3072]{1,0:T(8,128)(2,1)} %collective-permute-done.22.across), channel_id=1, source_target_pairs={{0,1},{1,0},{2,3},{3,2},{4,5},{5,4},{6,7},{7,6}} | collective-permute-start | bytes 4718600 | tf_op jit(solution)/shard_map/ppermute | solution.py:254
  436.0 1.7 copy-start.4
  436.0 25.4 %collective-permute-start.18 = (bf16[256,3072]{1,0:T(8,128)(2,1)}, bf16[256,3072]{1,0:T(8,128)(2,1)}, u32[]{:S(2)}, u32[]{:S(2)}) collective-permute-start(bf16[256,3072]{1,0:T(8,128)(2,1)} %get-tuple-element.100), channel_id=1, source_target_pairs={{0,1},{1,0},{2,3},{3,2},{4,5},{5,4},{6,7},{7,6}} | collective-permute-start | bytes 4718600 | tf_op jit(solution)/shard_map/ppermute | solution.py:254
  436.1 1.2 copy-start.2
  436.1 25.4 %collective-permute-start.20 = (bf16[256,3072]{1,0:T(8,128)(2,1)}, bf16[256,3072]{1,0:T(8,128)(2,1)}, u32[]{:S(2)}, u32[]{:S(2)}) collective-permute-start(bf16[256,3072]{1,0:T(8,128)(2,1)} %collective-permute-done.19.across), channel_id=1, source_target_pairs={{0,1},{1,0},{2,3},{3,2},{4,5},{5,4},{6,7},{7,6}} | collective-permute-start | bytes 4718600 | tf_op jit(solution)/shard_map/ppermute | solution.py:254
  437.7 1.2 copy-start.5
  438.9 26.3 %collective-permute-start.43 = (bf16[48,1024]{1,0:T(8,128)(2,1)S(1)}, bf16[48,1024]{1,0:T(8,128)(2,1)S(1)}, u32[]{:S(2)}, u32[]{:S(2)}) collective-permute-start(bf16[48,1024]{1,0:T(8,128)(2,1)S(1)} %collective-permute-done.31.refs_2_), channel_id=1, source_target_pairs={{0,1},{1,0},{2,3},{3,2},{4,5},{5,4},{6,7},{7,6}} | collective-permute-start | bytes 294920 | tf_op jit(solution)/shard_map/ppermute | solution.py:254

commit v7 on v6

--- a/solution.py
+++ b/solution.py
@@ -13,9 +13,9 @@
 BESIDE = [(0, 1), (1, 0), (2, 3), (3, 2)]
 
 CHUNKS = (
-    (0, 0, 0, 48), (0, 0, 48, 80), (0, 0, 128, 128), (0, 1, 0, 256),
+    (0, 0, 0, 32), (0, 0, 32, 32), (0, 0, 64, 64), (0, 0, 128, 128), (0, 1, 0, 256),
     (1, 0, 0, 256), (1, 1, 0, 256),
-    (2, 0, 0, 768), (2, 1, 0, 384), (2, 1, 384, 240), (2, 1, 624, 96), (2, 1, 720, 48),
+    (2, 0, 0, 768), (2, 1, 0, 384), (2, 1, 384, 192), (2, 1, 576, 96), (2, 1, 672, 48), (2, 1, 720, 48),
 )
 LAST = len(CHUNKS) - 1
 MESH = pl.DeviceIdType.MESH
@@ -255,7 +255,7 @@
 
         arrived, near = [], []
         for c in range(len(CHUNKS)):
-            both, *more = pair(terms, c, () if c == 1 else (0, 1, 2) if c == 2 else (c,)) if c else (first_pair(terms),)
+            both, *more = pair(terms, c, () if c < 3 else (0, 1, 2, 3) if c == 3 else (c,)) if c else (first_pair(terms),)
             near += more
             arrived.append(send(both, ACROSS))
 

time: 467 us -> 463 us (level)
  waiting for transfers between devices: 290 us -> 276 us
  Pallas kernels: 139 us -> 147 us
    ppermute x44 -> x52, waiting for transfers between devices: 290 us -> 276 us  [send(): return lax.ppermute(x, 'dp', to)]
    pallas_call x10 -> x12, Pallas kernels: 44.6 us -> 49.1 us  [pair(): pl.pallas_call(functools.partial(pair_body, chunk, nears), in_specs=[anyw...]
    pallas_call x8 -> x10, Pallas kernels: 23.9 us -> 27.6 us  [carry(): pl.pallas_call(functools.partial(carry_body, chunk, block), in_specs=[pl....]
    pallas_call x11 -> x13, Pallas kernels: 66.5 us -> 67 us  [adamw(): pl.pallas_call(functools.partial(adamw_body, n_alias), grid_spec=pltpu.Pr...]
    ppermute x44 -> x52, starting transfers between devices: 31.8 us -> 31.3 us  [send(): return lax.ppermute(x, 'dp', to)]
  transfers between devices with their start and end apart: 44 -> 52, of which waited for: 10 -> 13; matrix products, arithmetic and copies ran while one was open for 0% -> 0% of each run, Pallas kernels for 29% -> 31%
where the time goes in v7:
time: 463 us; the launch traced here: 462 us
  waiting for transfers between devices  276 us (60%)
  Pallas kernels  147 us (32%)
  starting transfers between devices  31.3 us (7%)
  local copies, waits for them, and re-layouts  7.26 us (2%)
    ppermute x52, waiting for transfers between devices, send(): return lax.ppermute(x, 'dp', to)  276 us
    pallas_call x13, Pallas kernels, adamw(): pl.pallas_call(functools.partial(adamw_body, n_alias), grid_spec=pltpu.Pr...  67 us
    pallas_call x12, Pallas kernels, pair(): pl.pallas_call(functools.partial(pair_body, chunk, nears), in_specs=[anyw...  49.1 us
    ppermute x52, starting transfers between devices, send(): return lax.ppermute(x, 'dp', to)  31.3 us
    pallas_call x10, Pallas kernels, carry(): pl.pallas_call(functools.partial(carry_body, chunk, block), in_specs=[pl....  27.6 us
  transfers between devices with their start and end apart: 52, of which 13 were waited for; matrix products, arithmetic and copies ran while one was open for 0% of the time, Pallas kernels for 31%

profile of v7, /device:TPU:0, one launch (start us, length us, event | category | flops | bytes accessed | tf_op | source)
XLA Modules:
  0.0 462.5 jit_solution(10486309208111125712)
XLA Ops:
  0.6 3.2 pair.14
  3.8 3.0 collective-permute-start.2
  6.8 1.7 first_pair.1
  8.6 2.4 pair.15
  11.0 2.0 collective-permute-start.3
  13.1 2.2 pair.18
  15.4 2.4 pair.19
  17.8 2.0 collective-permute-start.29
  19.8 5.0 %pair.13 = (bf16[128,3072]{1,0:T(8,128)(2,1)}, bf16[32,3072]{1,0:T(8,128)(2,1)}, bf16[32,3072]{1,0:T(8,128)(2,1)}, bf16[64,3072]{1,0:T(8,128)(2,1)}, bf16[128,3072]{1,0:T(8,128)(2,1)}) custom-call(bf16[1,2,1024,3072]{3,2,1,0:T(8,128)(2,1)} %refs_0_.23, bf16[1,2,1024,3072]{3,2,1,0:T(8,128)(2,1)} %refs_1_.23, bf16[1,2,3072,1024]{3,2,1,0:T(8,128)(2,1)} %own.25), custom_call_target="tpu_custom_call" | custom-call | flops 393216 | bytes 3932160 | tf_op jit(solution)/shard_map/pair/pallas_call | solution.py:123
  25.5 2.8 adamw.13
  29.0 2.8 adamw.14
  31.9 2.3 pair.23
  34.3 1.9 collective-permute-start.35
  36.2 2.8 pair.20
  39.0 2.3 collective-permute-done.35.far
  43.0 1.7 collective-permute-start.30
  44.7 6.2 %pair.22 = (bf16[768,1024]{1,0:T(8,128)(2,1)}, bf16[768,1024]{1,0:T(8,128)(2,1)}) custom-call(bf16[1,2,1024,3072]{3,2,1,0:T(8,128)(2,1)} %refs_0_.23, bf16[1,2,1024,3072]{3,2,1,0:T(8,128)(2,1)} %refs_1_.23, bf16[1,2,3072,1024]{3,2,1,0:T(8,128)(2,1)} %own.25), custom_call_target="tpu_custom_call" | custom-call | flops 786432 | bytes 7864320 | tf_op jit(solution)/shard_map/pair/pallas_call | solution.py:123
  51.3 1.8 collective-permute-start.18
  53.2 54.3 %collective-permute-done.18.across = bf16[32,3072]{1,0:T(8,128)(2,1)S(1)} collective-permute-done((bf16[32,3072]{1,0:T(8,128)(2,1)S(1)}, bf16[32,3072]{1,0:T(8,128)(2,1)S(1)}, u32[]{:S(2)}, u32[]{:S(2)}) %collective-permute-start.18) | collective-permute-done | bytes 196640 | tf_op jit(solution)/shard_map/ppermute | solution.py:254
  107.5 4.0 pair.21
  112.1 3.8 adamw.15
  116.0 1.5 collective-permute-start.12
  117.6 6.2 %pair.12 = (bf16[256,3072]{1,0:T(8,128)(2,1)}, bf16[256,3072]{1,0:T(8,128)(2,1)}) custom-call(bf16[1,2,1024,3072]{3,2,1,0:T(8,128)(2,1)} %refs_0_.23, bf16[1,2,1024,3072]{3,2,1,0:T(8,128)(2,1)} %refs_1_.23, bf16[1,2,3072,1024]{3,2,1,0:T(8,128)(2,1)} %own.25), custom_call_target="tpu_custom_call" | custom-call | flops 786432 | bytes 7864320 | tf_op jit(solution)/shard_map/pair/pallas_call | solution.py:123
  124.3 6.2 %pair.16 = (bf16[256,3072]{1,0:T(8,128)(2,1)}, bf16[256,3072]{1,0:T(8,128)(2,1)}) custom-call(bf16[1,2,1024,3072]{3,2,1,0:T(8,128)(2,1)} %refs_0_.23, bf16[1,2,1024,3072]{3,2,1,0:T(8,128)(2,1)} %refs_1_.23, bf16[1,2,3072,1024]{3,2,1,0:T(8,128)(2,1)} %own.25), custom_call_target="tpu_custom_call" | custom-call | flops 786432 | bytes 7864320 | tf_op jit(solution)/shard_map/pair/pallas_call | solution.py:123
  130.5 6.2 %pair.17 = (bf16[256,3072]{1,0:T(8,128)(2,1)}, bf16[256,3072]{1,0:T(8,128)(2,1)}) custom-call(bf16[1,2,1024,3072]{3,2,1,0:T(8,128)(2,1)} %refs_0_.23, bf16[1,2,1024,3072]{3,2,1,0:T(8,128)(2,1)} %refs_1_.23, bf16[1,2,3072,1024]{3,2,1,0:T(8,128)(2,1)} %own.25), custom_call_target="tpu_custom_call" | custom-call | flops 786432 | bytes 7864320 | tf_op jit(solution)/shard_map/pair/pallas_call | solution.py:123
  136.7 1.6 collective-permute-start.20
  138.2 2.4 collective-permute-done.12.across
  141.9 5.2 %adamw.16 = (bf16[128,3072]{1,0:T(8,128)(2,1)}, bf16[2,1024,3072]{2,1,0:T(8,128)(2,1)}, f32[2,256,3072]{2,1,0:T(8,128)}, f32[2,256,3072]{2,1,0:T(8,128)}) custom-call(s32[1]{0:T(128)} %bitcast.me, bf16[1,2,1024,3072]{3,2,1,0:T(8,128)(2,1)} %refs_0_.23, ...), custom_call_target="tpu_custom_call", output_to_operand_aliasing={{1}: (7, {}), {2}: (8, {}), {3}: (9, {})} | custom-call | flops 5505024 | bytes 11010048 | tf_op jit(solution)/shard_map/adamw/pallas_call | solution.py:162
  147.4 1.5 collective-permute-start.9
  148.9 9.2 %adamw.20 = (bf16[768,1024]{1,0:T(8,128)(2,1)}, bf16[2,3072,1024]{2,1,0:T(8,128)(2,1)}, f32[2,768,1024]{2,1,0:T(8,128)}, f32[2,768,1024]{2,1,0:T(8,128)}) custom-call(s32[1]{0:T(128)} %bitcast.me, bf16[1,2,3072,1024]{3,2,1,0:T(8,128)(2,1)} %own.25, bf16[768,1024]{1,0:T(8,128)(2,1)} %get-tuple-element.127.near, ...), custom_call_target="tpu_custom_call" | custom-call | flops 11010048 | bytes 22020096 | tf_op jit(solution)/shard_map/adamw/pallas_call | solution.py:162
  158.1 4.9 %adamw.21 = (bf16[384,1024]{1,0:T(8,128)(2,1)}, bf16[2,3072,1024]{2,1,0:T(8,128)(2,1)}, f32[2,768,1024]{2,1,0:T(8,128)}, f32[2,768,1024]{2,1,0:T(8,128)}) custom-call(s32[1]{0:T(128)} %bitcast.me, bf16[1,2,3072,1024]{3,2,1,0:T(8,128)(2,1)} %own.25, ...), custom_call_target="tpu_custom_call", output_to_operand_aliasing={{1}: (7, {}), {2}: (8, {}), {3}: (9, {})} | custom-call | flops 5505024 | bytes 11010048 | tf_op jit(solution)/shard_map/adamw/pallas_call | solution.py:162
  163.0 3.8 adamw.22
  166.8 2.8 adamw.23
  169.6 2.2 adamw.24
  171.7 2.2 adamw.25
  174.9 1.5 collective-permute-start.36
  176.5 82.2 %collective-permute-done.9.across = bf16[128,3072]{1,0:T(8,128)(2,1)} collective-permute-done((bf16[128,3072]{1,0:T(8,128)(2,1)}, bf16[128,3072]{1,0:T(8,128)(2,1)}, u32[]{:S(2)}, u32[]{:S(2)}) %collective-permute-start.9) | collective-permute-done | bytes 786464 | tf_op jit(solution)/shard_map/ppermute | solution.py:254
  259.3 1.4 collective-permute-done.33.refs_0_
  260.7 1.5 collective-permute-done.36.refs_2_
  262.7 1.5 collective-permute-start.43
  264.3 9.2 %adamw.17 = (bf16[256,3072]{1,0:T(8,128)(2,1)}, bf16[2,1024,3072]{2,1,0:T(8,128)(2,1)}, f32[2,256,3072]{2,1,0:T(8,128)}, f32[2,256,3072]{2,1,0:T(8,128)}) custom-call(s32[1]{0:T(128)} %bitcast.me, bf16[1,2,1024,3072]{3,2,1,0:T(8,128)(2,1)} %refs_0_.23, ...), custom_call_target="tpu_custom_call", output_to_operand_aliasing={{1}: (7, {}), {2}: (8, {}), {3}: (9, {})} | custom-call | flops 11010048 | bytes 22020096 | tf_op jit(solution)/shard_map/adamw/pallas_call | solution.py:162
  274.5 3.0 collective-permute-done.39.refs_2_
  278.0 1.4 collective-permute-done.42.beside
  279.4 0.8 copy-done.17
  280.6 9.2 %adamw.18 = (bf16[256,3072]{1,0:T(8,128)(2,1)}, bf16[2,1024,3072]{2,1,0:T(8,128)(2,1)}, f32[2,256,3072]{2,1,0:T(8,128)}, f32[2,256,3072]{2,1,0:T(8,128)}) custom-call(s32[1]{0:T(128)} %bitcast.me, bf16[1,2,1024,3072]{3,2,1,0:T(8,128)(2,1)} %refs_1_.23, bf16[256,3072]{1,0:T(8,128)(2,1)} %get-tuple-element.111.near, bf16[256,3072]{1,0:T(8,128)(2,1)} %copy-done, ...), custom_call_target="tpu_custom_call" | custom-call | flops 11010048 | bytes 22020096 | tf_op jit(solution)/shard_map/adamw/pallas_call | solution.py:162
  289.7 9.2 %adamw.19 = (bf16[256,3072]{1,0:T(8,128)(2,1)}, bf16[2,1024,3072]{2,1,0:T(8,128)(2,1)}, f32[2,256,3072]{2,1,0:T(8,128)}, f32[2,256,3072]{2,1,0:T(8,128)}) custom-call(s32[1]{0:T(128)} %bitcast.me, bf16[1,2,1024,3072]{3,2,1,0:T(8,128)(2,1)} %refs_1_.23, ...), custom_call_target="tpu_custom_call", output_to_operand_aliasing={{1}: (7, {}), {2}: (8, {}), {3}: (9, {})} | custom-call | flops 11010048 | bytes 22020096 | tf_op jit(solution)/shard_map/adamw/pallas_call | solution.py:162
  299.4 1.5 collective-permute-start.23
  301.5 26.8 %collective-permute-done.46.across = bf16[384,1024]{1,0:T(8,128)(2,1)S(1)} collective-permute-done((bf16[384,1024]{1,0:T(8,128)(2,1)}, bf16[384,1024]{1,0:T(8,128)(2,1)S(1)}, u32[]{:S(2)}, u32[]{:S(2)}) %collective-permute-start.46) | collective-permute-done | bytes 786464 | tf_op jit(solution)/shard_map/ppermute | solution.py:254
  329.3 32.8 %collective-permute-done.23.across = bf16[256,3072]{1,0:T(8,128)(2,1)} collective-permute-done((bf16[256,3072]{1,0:T(8,128)(2,1)}, bf16[256,3072]{1,0:T(8,128)(2,1)}, u32[]{:S(2)}, u32[]{:S(2)}) %collective-permute-start.23) | collective-permute-done | bytes 1572896 | tf_op jit(solution)/shard_map/ppermute | solution.py:254
  362.1 33.6 %collective-permute-done.49.across = bf16[768,1024]{1,0:T(8,128)(2,1)S(1)} collective-permute-done((bf16[768,1024]{1,0:T(8,128)(2,1)}, bf16[768,1024]{1,0:T(8,128)(2,1)S(1)}, u32[]{:S(2)}, u32[]{:S(2)}) %collective-permute-start.49) | collective-permute-done | bytes 1572896 | tf_op jit(solution)/shard_map/ppermute | solution.py:254
  395.7 33.0 %collective-permute-done.26.across = bf16[256,3072]{1,0:T(8,128)(2,1)} collective-permute-done((bf16[256,3072]{1,0:T(8,128)(2,1)}, bf16[256,3072]{1,0:T(8,128)(2,1)}, u32[]{:S(2)}, u32[]{:S(2)}) %collective-permute-start.26) | collective-permute-done | bytes 1572896 | tf_op jit(solution)/shard_map/ppermute | solution.py:254
  429.8 1.2 copy-done.2
  431.0 1.2 copy-done.5
  432.4 1.8 carry.10.before
  434.3 1.8 carry.11.before
  436.2 3.6 carry.17.before
  439.8 2.6 carry.18.before
  442.4 2.1 carry.19.refs_5_
  444.5 2.1 carry.12.before
  446.5 0.9 place.2.refs_3_
  447.5 2.6 carry.13.before
  450.8 3.6 carry.14
  454.5 3.6 carry.15.before
  458.2 3.6 carry.16
  (141 shorter events, 15.1 us)
Async XLA Ops:
  3.8 47.1 %collective-permute-start.2 = (bf16[64,3072]{1,0:T(8,128)(2,1)}, bf16[64,3072]{1,0:T(8,128)(2,1)S(1)}, u32[]{:S(2)}, u32[]{:S(2)}) collective-permute-start(bf16[64,3072]{1,0:T(8,128)(2,1)} %pair.14), channel_id=1, source_target_pairs={{0,2},{2,0},{1,3},{3,1},{4,6},{6,4},{5,7},{7,5}} | collective-permute-start | bytes 1179656 | tf_op jit(solution)/shard_map/ppermute | solution.py:254
  8.6 16.3 %collective-permute-start.4 = (bf16[32,3072]{1,0:T(8,128)(2,1)S(1)}, bf16[32,3072]{1,0:T(8,128)(2,1)S(1)}, u32[]{:S(2)}, u32[]{:S(2)}) collective-permute-start(bf16[32,3072]{1,0:T(8,128)(2,1)S(1)} %first_pair.1), channel_id=1, source_target_pairs={{0,2},{2,0},{1,3},{3,1},{4,6},{6,4},{5,7},{7,5}} | collective-permute-start | bytes 589832 | tf_op jit(solution)/shard_map/ppermute | solution.py:254
  11.0 17.3 %collective-permute-start.3 = (bf16[32,3072]{1,0:T(8,128)(2,1)}, bf16[32,3072]{1,0:T(8,128)(2,1)S(1)}, u32[]{:S(2)}, u32[]{:S(2)}) collective-permute-start(bf16[32,3072]{1,0:T(8,128)(2,1)} %pair.15), channel_id=1, source_target_pairs={{0,2},{2,0},{1,3},{3,1},{4,6},{6,4},{5,7},{7,5}} | collective-permute-start | bytes 589832 | tf_op jit(solution)/shard_map/ppermute | solution.py:254
  15.3 18.9 %collective-permute-start.28 = (bf16[48,1024]{1,0:T(8,128)(2,1)}, bf16[48,1024]{1,0:T(8,128)(2,1)S(1)}, u32[]{:S(2)}, u32[]{:S(2)}) collective-permute-start(bf16[48,1024]{1,0:T(8,128)(2,1)} %get-tuple-element.120), channel_id=1, source_target_pairs={{0,2},{2,0},{1,3},{3,1},{4,6},{6,4},{5,7},{7,5}} | collective-permute-start | bytes 294920 | tf_op jit(solution)/shard_map/ppermute | solution.py:254
  17.8 24.5 %collective-permute-start.29 = (bf16[96,1024]{1,0:T(8,128)(2,1)}, bf16[96,1024]{1,0:T(8,128)(2,1)S(1)}, u32[]{:S(2)}, u32[]{:S(2)}) collective-permute-start(bf16[96,1024]{1,0:T(8,128)(2,1)} %get-tuple-element.122), channel_id=1, source_target_pairs={{0,2},{2,0},{1,3},{3,1},{4,6},{6,4},{5,7},{7,5}} | collective-permute-start | bytes 589832 | tf_op jit(solution)/shard_map/ppermute | solution.py:254
  31.7 19.5 %collective-permute-start.14 = (bf16[32,3072]{1,0:T(8,128)(2,1)}, bf16[32,3072]{1,0:T(8,128)(2,1)S(1)}, u32[]{:S(2)}, u32[]{:S(2)}) collective-permute-start(bf16[32,3072]{1,0:T(8,128)(2,1)} %get-tuple-element.106), channel_id=1, source_target_pairs={{0,1},{1,0},{2,3},{3,2},{4,5},{5,4},{6,7},{7,6}} | collective-permute-start | bytes 589832 | tf_op jit(solution)/shard_map/ppermute | solution.py:254
  31.9 19.4 %collective-permute-start.15 = (bf16[32,3072]{1,0:T(8,128)(2,1)}, bf16[32,3072]{1,0:T(8,128)(2,1)S(1)}, u32[]{:S(2)}, u32[]{:S(2)}) collective-permute-start(bf16[32,3072]{1,0:T(8,128)(2,1)} %get-tuple-element.106), channel_id=1, source_target_pairs={{0,2},{2,0},{1,3},{3,1},{4,6},{6,4},{5,7},{7,5}} | collective-permute-start | bytes 589832 | tf_op jit(solution)/shard_map/ppermute | solution.py:254
  34.3 7.1 %collective-permute-start.35 = (bf16[48,1024]{1,0:T(8,128)(2,1)}, bf16[48,1024]{1,0:T(8,128)(2,1)S(1)}, u32[]{:S(2)}, u32[]{:S(2)}) collective-permute-start(bf16[48,1024]{1,0:T(8,128)(2,1)} %get-tuple-element.143), channel_id=1, source_target_pairs={{0,2},{2,0},{1,3},{3,1},{4,6},{6,4},{5,7},{7,5}} | collective-permute-start | bytes 294920 | tf_op jit(solution)/shard_map/ppermute | solution.py:254
  42.0 81.7 %collective-permute-start.1 = (bf16[128,3072]{1,0:T(8,128)(2,1)}, bf16[128,3072]{1,0:T(8,128)(2,1)S(1)}, u32[]{:S(2)}, u32[]{:S(2)}) collective-permute-start(bf16[128,3072]{1,0:T(8,128)(2,1)} %get-tuple-element.87), channel_id=1, source_target_pairs={{0,2},{2,0},{1,3},{3,1},{4,6},{6,4},{5,7},{7,5}} | collective-permute-start | bytes 2359304 | tf_op jit(solution)/shard_map/ppermute | solution.py:254
  43.0 68.6 %collective-permute-start.30 = (bf16[192,1024]{1,0:T(8,128)(2,1)}, bf16[192,1024]{1,0:T(8,128)(2,1)S(1)}, u32[]{:S(2)}, u32[]{:S(2)}) collective-permute-start(bf16[192,1024]{1,0:T(8,128)(2,1)} %get-tuple-element.124), channel_id=1, source_target_pairs={{0,2},{2,0},{1,3},{3,1},{4,6},{6,4},{5,7},{7,5}} | collective-permute-start | bytes 1179656 | tf_op jit(solution)/shard_map/ppermute | solution.py:254
  50.9 60.6 %copy-start.13 = (bf16[64,3072]{1,0:T(8,128)(2,1)}, bf16[64,3072]{1,0:T(8,128)(2,1)S(1)}, u32[]{:S(2)}) copy-start(bf16[64,3072]{1,0:T(8,128)(2,1)S(1)} %collective-permute-done.2.far) | copy-start | bytes 1179652
  50.9 96.4 %collective-permute-start.32 = (bf16[768,1024]{1,0:T(8,128)(2,1)}, bf16[768,1024]{1,0:T(8,128)(2,1)}, u32[]{:S(2)}, u32[]{:S(2)}) collective-permute-start(bf16[768,1024]{1,0:T(8,128)(2,1)} %get-tuple-element.128), channel_id=1, source_target_pairs={{0,2},{2,0},{1,3},{3,1},{4,6},{6,4},{5,7},{7,5}} | collective-permute-start | bytes 4718600 | tf_op jit(solution)/shard_map/ppermute | solution.py:254
  51.2 60.3 %copy-start.18 = (bf16[32,3072]{1,0:T(8,128)(2,1)}, bf16[32,3072]{1,0:T(8,128)(2,1)S(1)}, u32[]{:S(2)}) copy-start(bf16[32,3072]{1,0:T(8,128)(2,1)S(1)} %collective-permute-done.14.beside) | copy-start | bytes 589828
  51.2 1.8 collective-permute-start.17
  51.3 60.3 %copy-start.19 = (bf16[32,3072]{1,0:T(8,128)(2,1)}, bf16[32,3072]{1,0:T(8,128)(2,1)S(1)}, u32[]{:S(2)}) copy-start(bf16[32,3072]{1,0:T(8,128)(2,1)S(1)} %collective-permute-done.15.across) | copy-start | bytes 589828
  51.3 56.2 %collective-permute-start.18 = (bf16[32,3072]{1,0:T(8,128)(2,1)S(1)}, bf16[32,3072]{1,0:T(8,128)(2,1)S(1)}, u32[]{:S(2)}, u32[]{:S(2)}) collective-permute-start(bf16[32,3072]{1,0:T(8,128)(2,1)S(1)} %copy-done.29), channel_id=1, source_target_pairs={{0,2},{2,0},{1,3},{3,1},{4,6},{6,4},{5,7},{7,5}} | collective-permute-start | bytes 589832 | tf_op jit(solution)/shard_map/ppermute | solution.py:254
  53.0 62.8 %collective-permute-start.16 = (bf16[32,3072]{1,0:T(8,128)(2,1)S(1)}, bf16[32,3072]{1,0:T(8,128)(2,1)S(1)}, u32[]{:S(2)}, u32[]{:S(2)}) collective-permute-start(bf16[32,3072]{1,0:T(8,128)(2,1)S(1)} %collective-permute-done.15.across), channel_id=1, source_target_pairs={{0,1},{1,0},{2,3},{3,2},{4,5},{5,4},{6,7},{7,6}} | collective-permute-start | bytes 589832 | tf_op jit(solution)/shard_map/ppermute | solution.py:254
  107.5 8.5 %collective-permute-start.19 = (bf16[32,3072]{1,0:T(8,128)(2,1)S(1)}, bf16[32,3072]{1,0:T(8,128)(2,1)S(1)}, u32[]{:S(2)}, u32[]{:S(2)}) collective-permute-start(bf16[32,3072]{1,0:T(8,128)(2,1)S(1)} %collective-permute-done.18.across), channel_id=1, source_target_pairs={{0,1},{1,0},{2,3},{3,2},{4,5},{5,4},{6,7},{7,6}} | collective-permute-start | bytes 589832 | tf_op jit(solution)/shard_map/ppermute | solution.py:254
  111.6 30.3 %collective-permute-start.31 = (bf16[384,1024]{1,0:T(8,128)(2,1)}, bf16[384,1024]{1,0:T(8,128)(2,1)S(1)}, u32[]{:S(2)}, u32[]{:S(2)}) collective-permute-start(bf16[384,1024]{1,0:T(8,128)(2,1)} %get-tuple-element.126), channel_id=1, source_target_pairs={{0,2},{2,0},{1,3},{3,1},{4,6},{6,4},{5,7},{7,5}} | collective-permute-start | bytes 2359304 | tf_op jit(solution)/shard_map/ppermute | solution.py:254
  115.9 20.7 %collective-permute-start.11 = (bf16[64,3072]{1,0:T(8,128)(2,1)}, bf16[64,3072]{1,0:T(8,128)(2,1)S(1)}, u32[]{:S(2)}, u32[]{:S(2)}) collective-permute-start(bf16[64,3072]{1,0:T(8,128)(2,1)} %get-tuple-element.105), channel_id=1, source_target_pairs={{0,1},{1,0},{2,3},{3,2},{4,5},{5,4},{6,7},{7,6}} | collective-permute-start | bytes 1179656 | tf_op jit(solution)/shard_map/ppermute | solution.py:254
  116.0 24.6 %collective-permute-start.12 = (bf16[64,3072]{1,0:T(8,128)(2,1)}, bf16[64,3072]{1,0:T(8,128)(2,1)S(1)}, u32[]{:S(2)}, u32[]{:S(2)}) collective-permute-start(bf16[64,3072]{1,0:T(8,128)(2,1)} %get-tuple-element.105), channel_id=1, source_target_pairs={{0,2},{2,0},{1,3},{3,1},{4,6},{6,4},{5,7},{7,5}} | collective-permute-start | bytes 1179656 | tf_op jit(solution)/shard_map/ppermute | solution.py:254
  123.8 50.7 %collective-permute-start = (bf16[256,3072]{1,0:T(8,128)(2,1)}, bf16[256,3072]{1,0:T(8,128)(2,1)}, u32[]{:S(2)}, u32[]{:S(2)}) collective-permute-start(bf16[256,3072]{1,0:T(8,128)(2,1)} %get-tuple-element.85), channel_id=1, source_target_pairs={{0,2},{2,0},{1,3},{3,1},{4,6},{6,4},{5,7},{7,5}} | collective-permute-start | bytes 4718600 | tf_op jit(solution)/shard_map/ppermute | solution.py:254
  136.6 10.4 %copy-start.14 = (bf16[64,3072]{1,0:T(8,128)(2,1)}, bf16[64,3072]{1,0:T(8,128)(2,1)S(1)}, u32[]{:S(2)}) copy-start(bf16[64,3072]{1,0:T(8,128)(2,1)S(1)} %collective-permute-done.11.beside) | copy-start | bytes 1179652
  136.7 122.1 %collective-permute-start.20 = (bf16[256,3072]{1,0:T(8,128)(2,1)}, bf16[256,3072]{1,0:T(8,128)(2,1)}, u32[]{:S(2)}, u32[]{:S(2)}) collective-permute-start(bf16[256,3072]{1,0:T(8,128)(2,1)} %get-tuple-element.110), channel_id=1, source_target_pairs={{0,2},{2,0},{1,3},{3,1},{4,6},{6,4},{5,7},{7,5}} | collective-permute-start | bytes 4718600 | tf_op jit(solution)/shard_map/ppermute | solution.py:254
  141.4 117.9 %collective-permute-start.21 = (bf16[256,3072]{1,0:T(8,128)(2,1)}, bf16[256,3072]{1,0:T(8,128)(2,1)S(1)}, u32[]{:S(2)}, u32[]{:S(2)}) collective-permute-start(bf16[256,3072]{1,0:T(8,128)(2,1)} %get-tuple-element.112), channel_id=1, source_target_pairs={{0,2},{2,0},{1,3},{3,1},{4,6},{6,4},{5,7},{7,5}} | collective-permute-start | bytes 4718600 | tf_op jit(solution)/shard_map/ppermute | solution.py:254
  141.9 5.2 %collective-permute-start.13 = (bf16[64,3072]{1,0:T(8,128)(2,1)}, bf16[64,3072]{1,0:T(8,128)(2,1)S(1)}, u32[]{:S(2)}, u32[]{:S(2)}) collective-permute-start(bf16[64,3072]{1,0:T(8,128)(2,1)} %copy-done.15), channel_id=1, source_target_pairs={{0,1},{1,0},{2,3},{3,2},{4,5},{5,4},{6,7},{7,6}} | collective-permute-start | bytes 1179656 | tf_op jit(solution)/shard_map/ppermute | solution.py:254
  147.1 11.0 %copy-start.16 = (bf16[64,3072]{1,0:T(8,128)(2,1)}, bf16[64,3072]{1,0:T(8,128)(2,1)S(1)}, u32[]{:S(2)}) copy-start(bf16[64,3072]{1,0:T(8,128)(2,1)S(1)} %collective-permute-done.13.corner) | copy-start | bytes 1179652
  147.1 27.9 %collective-permute-start.8 = (bf16[128,3072]{1,0:T(8,128)(2,1)}, bf16[128,3072]{1,0:T(8,128)(2,1)S(1)}, u32[]{:S(2)}, u32[]{:S(2)}) collective-permute-start(bf16[128,3072]{1,0:T(8,128)(2,1)} %get-tuple-element.104), channel_id=1, source_target_pairs={{0,1},{1,0},{2,3},{3,2},{4,5},{5,4},{6,7},{7,6}} | collective-permute-start | bytes 2359304 | tf_op jit(solution)/shard_map/ppermute | solution.py:254
  147.4 111.4 %collective-permute-start.9 = (bf16[128,3072]{1,0:T(8,128)(2,1)}, bf16[128,3072]{1,0:T(8,128)(2,1)}, u32[]{:S(2)}, u32[]{:S(2)}) collective-permute-start(bf16[128,3072]{1,0:T(8,128)(2,1)} %get-tuple-element.104), channel_id=1, source_target_pairs={{0,2},{2,0},{1,3},{3,1},{4,6},{6,4},{5,7},{7,5}} | collective-permute-start | bytes 2359304 | tf_op jit(solution)/shard_map/ppermute | solution.py:254
  171.7 87.0 %copy-start.28 = (bf16[96,1024]{1,0:T(8,128)(2,1)S(1)}, bf16[96,1024]{1,0:T(8,128)(2,1)}, u32[]{:S(2)}) copy-start(bf16[96,1024]{1,0:T(8,128)(2,1)} %get-tuple-element.148) | copy-start | bytes 589828
  174.5 86.3 %collective-permute-start.33 = (bf16[48,1024]{1,0:T(8,128)(2,1)S(1)}, bf16[48,1024]{1,0:T(8,128)(2,1)S(1)}, u32[]{:S(2)}, u32[]{:S(2)}) collective-permute-start(bf16[48,1024]{1,0:T(8,128)(2,1)S(1)} %copy-done.30), channel_id=1, source_target_pairs={{0,2},{2,0},{1,3},{3,1},{4,6},{6,4},{5,7},{7,5}} | collective-permute-start | bytes 294920 | tf_op jit(solution)/shard_map/ppermute | solution.py:254
  174.9 98.5 %copy-start.8 = (bf16[128,3072]{1,0:T(8,128)(2,1)}, bf16[128,3072]{1,0:T(8,128)(2,1)S(1)}, u32[]{:S(2)}) copy-start(bf16[128,3072]{1,0:T(8,128)(2,1)S(1)} %collective-permute-done.8.beside) | copy-start | bytes 2359300
  174.9 87.3 %collective-permute-start.36 = (bf16[48,1024]{1,0:T(8,128)(2,1)}, bf16[48,1024]{1,0:T(8,128)(2,1)S(1)}, u32[]{:S(2)}, u32[]{:S(2)}) collective-permute-start(bf16[48,1024]{1,0:T(8,128)(2,1)} %get-tuple-element.147), channel_id=1, source_target_pairs={{0,2},{2,0},{1,3},{3,1},{4,6},{6,4},{5,7},{7,5}} | collective-permute-start | bytes 294920 | tf_op jit(solution)/shard_map/ppermute | solution.py:254
  258.7 15.3 %collective-permute-start.37 = (bf16[96,1024]{1,0:T(8,128)(2,1)S(1)}, bf16[96,1024]{1,0:T(8,128)(2,1)S(1)}, u32[]{:S(2)}, u32[]{:S(2)}) collective-permute-start(bf16[96,1024]{1,0:T(8,128)(2,1)S(1)} %copy-done.28), channel_id=1, source_target_pairs={{0,1},{1,0},{2,3},{3,2},{4,5},{5,4},{6,7},{7,6}} | collective-permute-start | bytes 589832 | tf_op jit(solution)/shard_map/ppermute | solution.py:254
  258.7 4.0 collective-permute-start.40
  259.2 14.2 %copy-start = (bf16[256,3072]{1,0:T(8,128)(2,1)}, bf16[256,3072]{1,0:T(8,128)(2,1)S(1)}, u32[]{:S(2)}) copy-start(bf16[256,3072]{1,0:T(8,128)(2,1)S(1)} %collective-permute-done.21.far) | copy-start | bytes 4718596
  259.2 5.0 %collective-permute-start.41 = (bf16[48,1024]{1,0:T(8,128)(2,1)}, bf16[48,1024]{1,0:T(8,128)(2,1)S(1)}, u32[]{:S(2)}, u32[]{:S(2)}) collective-permute-start(bf16[48,1024]{1,0:T(8,128)(2,1)} %get-tuple-element.147), channel_id=1, source_target_pairs={{0,1},{1,0},{2,3},{3,2},{4,5},{5,4},{6,7},{7,6}} | collective-permute-start | bytes 294920 | tf_op jit(solution)/shard_map/ppermute | solution.py:254
  260.7 12.7 %collective-permute-start.34 = (bf16[48,1024]{1,0:T(8,128)(2,1)S(1)}, bf16[48,1024]{1,0:T(8,128)(2,1)S(1)}, u32[]{:S(2)}, u32[]{:S(2)}) collective-permute-start(bf16[48,1024]{1,0:T(8,128)(2,1)S(1)} %collective-permute-done.33.refs_0_), channel_id=1, source_target_pairs={{0,1},{1,0},{2,3},{3,2},{4,5},{5,4},{6,7},{7,6}} | collective-permute-start | bytes 294920 | tf_op jit(solution)/shard_map/ppermute | solution.py:254
  262.2 12.2 %collective-permute-start.38 = (bf16[96,1024]{1,0:T(8,128)(2,1)S(1)}, bf16[96,1024]{1,0:T(8,128)(2,1)S(1)}, u32[]{:S(2)}, u32[]{:S(2)}) collective-permute-start(bf16[96,1024]{1,0:T(8,128)(2,1)S(1)} %copy-done.28), channel_id=1, source_target_pairs={{0,2},{2,0},{1,3},{3,1},{4,6},{6,4},{5,7},{7,5}} | collective-permute-start | bytes 589832 | tf_op jit(solution)/shard_map/ppermute | solution.py:254
  262.7 15.2 %collective-permute-start.43 = (bf16[192,1024]{1,0:T(8,128)(2,1)}, bf16[192,1024]{1,0:T(8,128)(2,1)}, u32[]{:S(2)}, u32[]{:S(2)}) collective-permute-start(bf16[192,1024]{1,0:T(8,128)(2,1)} %get-tuple-element.149), channel_id=1, source_target_pairs={{0,2},{2,0},{1,3},{3,1},{4,6},{6,4},{5,7},{7,5}} | collective-permute-start | bytes 1179656 | tf_op jit(solution)/shard_map/ppermute | solution.py:254
  264.3 34.7 %collective-permute-start.10 = (bf16[128,3072]{1,0:T(8,128)(2,1)}, bf16[128,3072]{1,0:T(8,128)(2,1)}, u32[]{:S(2)}, u32[]{:S(2)}) collective-permute-start(bf16[128,3072]{1,0:T(8,128)(2,1)} %collective-permute-done.9.across), channel_id=1, source_target_pairs={{0,1},{1,0},{2,3},{3,2},{4,5},{5,4},{6,7},{7,6}} | collective-permute-start | bytes 2359304 | tf_op jit(solution)/shard_map/ppermute | solution.py:254
  273.5 55.3 %collective-permute-start.5 = (bf16[256,3072]{1,0:T(8,128)(2,1)}, bf16[256,3072]{1,0:T(8,128)(2,1)S(1)}, u32[]{:S(2)}, u32[]{:S(2)}) collective-permute-start(bf16[256,3072]{1,0:T(8,128)(2,1)} %get-tuple-element.103), channel_id=1, source_target_pairs={{0,1},{1,0},{2,3},{3,2},{4,5},{5,4},{6,7},{7,6}} | collective-permute-start | bytes 4718600 | tf_op jit(solution)/shard_map/ppermute | solution.py:254
  274.0 54.8 %collective-permute-start.6 = (bf16[256,3072]{1,0:T(8,128)(2,1)}, bf16[256,3072]{1,0:T(8,128)(2,1)}, u32[]{:S(2)}, u32[]{:S(2)}) collective-permute-start(bf16[256,3072]{1,0:T(8,128)(2,1)} %get-tuple-element.103), channel_id=1, source_target_pairs={{0,2},{2,0},{1,3},{3,1},{4,6},{6,4},{5,7},{7,5}} | collective-permute-start | bytes 4718600 | tf_op jit(solution)/shard_map/ppermute | solution.py:254
  274.5 3.0 collective-permute-start.39
  277.5 1.9 collective-permute-start.42
  277.9 21.6 %collective-permute-start.44 = (bf16[192,1024]{1,0:T(8,128)(2,1)}, bf16[192,1024]{1,0:T(8,128)(2,1)}, u32[]{:S(2)}, u32[]{:S(2)}) collective-permute-start(bf16[192,1024]{1,0:T(8,128)(2,1)} %collective-permute-done.43.across), channel_id=1, source_target_pairs={{0,1},{1,0},{2,3},{3,2},{4,5},{5,4},{6,7},{7,6}} | collective-permute-start | bytes 1179656 | tf_op jit(solution)/shard_map/ppermute | solution.py:254
  280.2 20.8 %collective-permute-start.45 = (bf16[384,1024]{1,0:T(8,128)(2,1)}, bf16[384,1024]{1,0:T(8,128)(2,1)S(1)}, u32[]{:S(2)}, u32[]{:S(2)}) collective-permute-start(bf16[384,1024]{1,0:T(8,128)(2,1)} %get-tuple-element.150), channel_id=1, source_target_pairs={{0,1},{1,0},{2,3},{3,2},{4,5},{5,4},{6,7},{7,6}} | collective-permute-start | bytes 2359304 | tf_op jit(solution)/shard_map/ppermute | solution.py:254
  298.9 29.4 %collective-permute-start.46 = (bf16[384,1024]{1,0:T(8,128)(2,1)}, bf16[384,1024]{1,0:T(8,128)(2,1)S(1)}, u32[]{:S(2)}, u32[]{:S(2)}) collective-permute-start(bf16[384,1024]{1,0:T(8,128)(2,1)} %get-tuple-element.150), channel_id=1, source_target_pairs={{0,2},{2,0},{1,3},{3,1},{4,6},{6,4},{5,7},{7,5}} | collective-permute-start | bytes 2359304 | tf_op jit(solution)/shard_map/ppermute | solution.py:254
  299.4 62.7 %collective-permute-start.23 = (bf16[256,3072]{1,0:T(8,128)(2,1)}, bf16[256,3072]{1,0:T(8,128)(2,1)}, u32[]{:S(2)}, u32[]{:S(2)}) collective-permute-start(bf16[256,3072]{1,0:T(8,128)(2,1)} %get-tuple-element.116), channel_id=1, source_target_pairs={{0,2},{2,0},{1,3},{3,1},{4,6},{6,4},{5,7},{7,5}} | collective-permute-start | bytes 4718600 | tf_op jit(solution)/shard_map/ppermute | solution.py:254
  301.0 135.2 %copy-start.9 = (bf16[384,1024]{1,0:T(8,128)(2,1)}, bf16[384,1024]{1,0:T(8,128)(2,1)S(1)}, u32[]{:S(2)}) copy-start(bf16[384,1024]{1,0:T(8,128)(2,1)S(1)} %collective-permute-done.45.beside) | copy-start | bytes 2359300
  301.0 94.7 %collective-permute-start.49 = (bf16[768,1024]{1,0:T(8,128)(2,1)}, bf16[768,1024]{1,0:T(8,128)(2,1)S(1)}, u32[]{:S(2)}, u32[]{:S(2)}) collective-permute-start(bf16[768,1024]{1,0:T(8,128)(2,1)} %get-tuple-element.151), channel_id=1, source_target_pairs={{0,2},{2,0},{1,3},{3,1},{4,6},{6,4},{5,7},{7,5}} | collective-permute-start | bytes 4718600 | tf_op jit(solution)/shard_map/ppermute | solution.py:254
  328.3 102.6 %copy-start.10 = (bf16[384,1024]{1,0:T(8,128)(2,1)}, bf16[384,1024]{1,0:T(8,128)(2,1)S(1)}, u32[]{:S(2)}) copy-start(bf16[384,1024]{1,0:T(8,128)(2,1)S(1)} %collective-permute-done.46.across) | copy-start | bytes 2359300
  328.3 100.4 %collective-permute-start.26 = (bf16[256,3072]{1,0:T(8,128)(2,1)}, bf16[256,3072]{1,0:T(8,128)(2,1)}, u32[]{:S(2)}, u32[]{:S(2)}) collective-permute-start(bf16[256,3072]{1,0:T(8,128)(2,1)} %get-tuple-element.117), channel_id=1, source_target_pairs={{0,2},{2,0},{1,3},{3,1},{4,6},{6,4},{5,7},{7,5}} | collective-permute-start | bytes 4718600 | tf_op jit(solution)/shard_map/ppermute | solution.py:254
  328.8 105.5 %copy-start.1 = (bf16[256,3072]{1,0:T(8,128)(2,1)}, bf16[256,3072]{1,0:T(8,128)(2,1)S(1)}, u32[]{:S(2)}) copy-start(bf16[256,3072]{1,0:T(8,128)(2,1)S(1)} %collective-permute-done.5.beside) | copy-start | bytes 4718596
  328.8 100.5 %collective-permute-start.48 = (bf16[768,1024]{1,0:T(8,128)(2,1)}, bf16[768,1024]{1,0:T(8,128)(2,1)S(1)}, u32[]{:S(2)}, u32[]{:S(2)}) collective-permute-start(bf16[768,1024]{1,0:T(8,128)(2,1)} %get-tuple-element.151), channel_id=1, source_target_pairs={{0,1},{1,0},{2,3},{3,2},{4,5},{5,4},{6,7},{7,6}} | collective-permute-start | bytes 4718600 | tf_op jit(solution)/shard_map/ppermute | solution.py:254
  328.8 100.5 %collective-permute-start.7 = (bf16[256,3072]{1,0:T(8,128)(2,1)}, bf16[256,3072]{1,0:T(8,128)(2,1)S(1)}, u32[]{:S(2)}, u32[]{:S(2)}) collective-permute-start(bf16[256,3072]{1,0:T(8,128)(2,1)} %collective-permute-done.6.across), channel_id=1, source_target_pairs={{0,1},{1,0},{2,3},{3,2},{4,5},{5,4},{6,7},{7,6}} | collective-permute-start | bytes 4718600 | tf_op jit(solution)/shard_map/ppermute | solution.py:254
  362.1 66.6 %collective-permute-start.47 = (bf16[384,1024]{1,0:T(8,128)(2,1)S(1)}, bf16[384,1024]{1,0:T(8,128)(2,1)S(1)}, u32[]{:S(2)}, u32[]{:S(2)}) collective-permute-start(bf16[384,1024]{1,0:T(8,128)(2,1)S(1)} %collective-permute-done.46.across), channel_id=1, source_target_pairs={{0,1},{1,0},{2,3},{3,2},{4,5},{5,4},{6,7},{7,6}} | collective-permute-start | bytes 2359304 | tf_op jit(solution)/shard_map/ppermute | solution.py:254
  395.7 35.2 %copy-start.3 = (bf16[768,1024]{1,0:T(8,128)(2,1)}, bf16[768,1024]{1,0:T(8,128)(2,1)S(1)}, u32[]{:S(2)}) copy-start(bf16[768,1024]{1,0:T(8,128)(2,1)S(1)} %collective-permute-done.49.across) | copy-start | bytes 4718596
  395.7 35.2 %collective-permute-start.50 = (bf16[768,1024]{1,0:T(8,128)(2,1)S(1)}, bf16[768,1024]{1,0:T(8,128)(2,1)S(1)}, u32[]{:S(2)}, u32[]{:S(2)}) collective-permute-start(bf16[768,1024]{1,0:T(8,128)(2,1)S(1)} %collective-permute-done.49.across), channel_id=1, source_target_pairs={{0,1},{1,0},{2,3},{3,2},{4,5},{5,4},{6,7},{7,6}} | collective-permute-start | bytes 4718600 | tf_op jit(solution)/shard_map/ppermute | solution.py:254
  428.8 25.7 %collective-permute-start.25 = (bf16[256,3072]{1,0:T(8,128)(2,1)}, bf16[256,3072]{1,0:T(8,128)(2,1)}, u32[]{:S(2)}, u32[]{:S(2)}) collective-permute-start(bf16[256,3072]{1,0:T(8,128)(2,1)} %get-tuple-element.117), channel_id=1, source_target_pairs={{0,1},{1,0},{2,3},{3,2},{4,5},{5,4},{6,7},{7,6}} | collective-permute-start | bytes 4718600 | tf_op jit(solution)/shard_map/ppermute | solution.py:254
  428.8 25.7 %collective-permute-start.27 = (bf16[256,3072]{1,0:T(8,128)(2,1)}, bf16[256,3072]{1,0:T(8,128)(2,1)}, u32[]{:S(2)}, u32[]{:S(2)}) collective-permute-start(bf16[256,3072]{1,0:T(8,128)(2,1)} %collective-permute-done.26.across), channel_id=1, source_target_pairs={{0,1},{1,0},{2,3},{3,2},{4,5},{5,4},{6,7},{7,6}} | collective-permute-start | bytes 4718600 | tf_op jit(solution)/shard_map/ppermute | solution.py:254
  429.3 28.9 %collective-permute-start.22 = (bf16[256,3072]{1,0:T(8,128)(2,1)}, bf16[256,3072]{1,0:T(8,128)(2,1)}, u32[]{:S(2)}, u32[]{:S(2)}) collective-permute-start(bf16[256,3072]{1,0:T(8,128)(2,1)} %get-tuple-element.116), channel_id=1, source_target_pairs={{0,1},{1,0},{2,3},{3,2},{4,5},{5,4},{6,7},{7,6}} | collective-permute-start | bytes 4718600 | tf_op jit(solution)/shard_map/ppermute | solution.py:254
  429.3 28.8 %collective-permute-start.24 = (bf16[256,3072]{1,0:T(8,128)(2,1)}, bf16[256,3072]{1,0:T(8,128)(2,1)}, u32[]{:S(2)}, u32[]{:S(2)}) collective-permute-start(bf16[256,3072]{1,0:T(8,128)(2,1)} %collective-permute-done.23.across), channel_id=1, source_target_pairs={{0,1},{1,0},{2,3},{3,2},{4,5},{5,4},{6,7},{7,6}} | collective-permute-start | bytes 4718600 | tf_op jit(solution)/shard_map/ppermute | solution.py:254
  432.2 29.6 %collective-permute-start.51 = (bf16[48,1024]{1,0:T(8,128)(2,1)S(1)}, bf16[48,1024]{1,0:T(8,128)(2,1)S(1)}, u32[]{:S(2)}, u32[]{:S(2)}) collective-permute-start(bf16[48,1024]{1,0:T(8,128)(2,1)S(1)} %collective-permute-done.36.refs_2_), channel_id=1, source_target_pairs={{0,1},{1,0},{2,3},{3,2},{4,5},{5,4},{6,7},{7,6}} | collective-permute-start | bytes 294920 | tf_op jit(solution)/shard_map/ppermute | solution.py:254
  (19 other events, 62.4 us)
